TPU v7x, 128 devices: a whole 4x4x4 slice. The times are simulated.
128 devices in a mesh: grp: 2 (over core), shard: 64 (over y, z, x).
Axes of the slice: x: 4, y: 4, z: 4, core: 2. Of those that a mesh axis runs over, the one named last changes fastest.
Arguments:
- blocks: float32 [8192, 128, 128], P(('grp', 'shard')), may hold values from -0.1875 to 0.1875
- block_row: int32 [8192], P(('grp', 'shard')), may hold values from 0 to 2047, as said below
- block_owner: int32 [8192, 1], P(('grp', 'shard')), may hold values from 0 to 63; in each aligned block of 64 rows (0 to 63, 64 to 127, ...) at most 2 rows name the same one
- block_col: int32 [8192], P(('grp', 'shard')), may hold values from 0 to 15
- right_side: float32 [262144, 8], P(('grp', 'shard')), may hold values from -6 to 6
Outputs:
- solution: float32 [131072, 8], P('shard')
- left_vector: float32 [262144, 8], P(('grp', 'shard'))
- rel_residual: float32 [8], replicated
Inputs may be any that keep to these rules, and one draw needn't show every extreme that they name: `block_row`: block k lies in a row block of the device that holds it: between (k // 64) * 16 and (k // 64) * 16 + 15. `block_owner`: among the 64 blocks of one device, each owner is named at most 2 times, and in every draw some device names some owner exactly 2 times. `block_col`: a column block index among the 16 of the owner.
All inputs are finite; a program needn't handle non-finite values.
Results may differ from a plain program's by a relative error of at most 0.00024.
Values sent between devices are 32-bit elements; how exact they have to be, the bound alone decides.
No kernel may reach another device: no remote copies, remote signals or barrier semaphores. Data moves between devices by JAX's collectives and lax.ppermute only.
A program may use at most 64 MiB of HBM per device.

v0:
```python
import jax
import jax.numpy as jnp
from jax import lax
from jax.sharding import Mesh
from jax.sharding import PartitionSpec as P

ITERS = 4
COLS_OWN = 16
SHARD = ("shard_0", "shard_1", "shard_2")
GRP_SHARD = ("grp", "shard_0", "shard_1", "shard_2")


PRECISE = lax.Precision.HIGHEST


def sent_to_all(shard, axis):
    length = lax.axis_size(axis)
    return lax.all_to_all(
        jnp.broadcast_to(shard[None], (length, *shard.shape)), axis, 0, 0, tiled=True
    )


def taken_together(shard, axis):
    everything = sent_to_all(shard, axis)
    return jnp.sum(everything, axis=0)


def by_axis(shard, axes):
    for axis in axes:
        shard = lax.psum(shard, axis)
    return shard


def squares_by_column(values):
    return jnp.sum(values * values, axis=0)


def rotate(state, norm_left, norm_right, right_vec):
    solution, search, diag_bar, residual_norm = state
    radius = jnp.sqrt(diag_bar * diag_bar + norm_left * norm_left)
    cosine = diag_bar / radius
    sine_term = norm_left / radius
    coupling = sine_term * norm_right
    step_size = cosine * residual_norm
    solution = solution + step_size / radius * search
    search = right_vec - coupling / radius * search
    return (solution, search, -cosine * norm_right, sine_term * residual_norm)


def on_device(blocks, block_row, block_owner, block_col, right_side):
    count = blocks.shape[0]
    block_width = blocks.shape[1]
    columns = right_side.shape[1]
    flat_width = block_width * columns
    owners = lax.axis_size(SHARD)
    capacity = 2 * count // owners
    row_blocks = right_side.shape[0] // block_width
    first_row = lax.axis_index(GRP_SHARD) * row_blocks
    local_row = block_row - first_row
    row_onehot = (local_row[:, None] == jnp.arange(row_blocks, dtype=jnp.int32)[None, :]).astype(
        jnp.float32
    )
    owner = block_owner[:, 0]
    owner_onehot = (owner[:, None] == jnp.arange(owners, dtype=jnp.int32)[None, :]).astype(
        jnp.int32
    )
    earlier = jnp.cumsum(owner_onehot, axis=0) - owner_onehot
    slot_rank = jnp.sum(earlier * owner_onehot, axis=1)
    position = owner * capacity + slot_rank
    source = (
        jnp.full((owners * capacity,), count, jnp.int32)
        .at[position]
        .set(jnp.arange(count, dtype=jnp.int32))
    )
    sent_cols = jnp.concatenate([block_col, jnp.full((1,), -1, jnp.int32)])[source]
    got_cols = lax.all_to_all(sent_cols, SHARD, split_axis=0, concat_axis=0, tiled=True)
    col_onehot = (got_cols[:, None] == jnp.arange(COLS_OWN, dtype=jnp.int32)[None, :]).astype(
        jnp.float32
    )

    def adjoint(vector):
        pieces = vector.reshape(row_blocks, block_width, columns)[local_row]
        product = jnp.einsum("kij,kir->kjr", blocks, pieces, precision=PRECISE).reshape(
            count, flat_width
        )
        padded = jnp.concatenate([product, jnp.zeros((1, flat_width), jnp.float32)])
        incoming = lax.all_to_all(padded[source], SHARD, split_axis=0, concat_axis=0, tiled=True)
        owned = jnp.dot(col_onehot.T, incoming, precision=PRECISE)
        owned = taken_together(owned, "grp")
        return owned.reshape(COLS_OWN * block_width, columns)

    def norm_rows(values):
        return jnp.sqrt(by_axis(squares_by_column(values), GRP_SHARD))

    def norm_columns(values):
        return jnp.sqrt(taken_together(squares_by_column(values), SHARD))

    norm_start = norm_rows(right_side)
    left_vec = right_side / norm_start
    right_raw = adjoint(left_vec)
    norm_left = norm_start
    for repeat in range(ITERS):
        flat = right_raw.reshape(COLS_OWN, flat_width)
        outgoing = jnp.dot(col_onehot, flat, precision=PRECISE)
        forward_incoming = lax.all_to_all(outgoing, SHARD, split_axis=0, concat_axis=0, tiled=True)
        forward_pieces = forward_incoming[position]
        forward_pieces = forward_pieces.reshape(count, block_width, columns)
        forward_product = jnp.einsum("kij,kjr->kir", blocks, forward_pieces, precision=PRECISE)
        summed = jnp.dot(
            row_onehot.T, forward_product.reshape(count, flat_width), precision=PRECISE
        )
        image = summed.reshape(row_blocks * block_width, columns)
        norm_right = norm_columns(right_raw)
        right_vec = right_raw / norm_right
        if repeat == 0:
            state = (jnp.zeros_like(right_vec), right_vec, norm_right, norm_start)
        else:
            state = rotate(state, norm_left, norm_right, right_vec)
        left_raw = image / norm_right - norm_right * left_vec
        terms = adjoint(left_raw)
        norm_left = norm_rows(left_raw)
        left_vec = left_raw / norm_left
        right_raw = terms / norm_left - norm_left * right_vec
    norm_right = norm_columns(right_raw)
    right_vec = right_raw / norm_right
    state = rotate(state, norm_left, norm_right, right_vec)
    return (state[0], left_vec, state[3] / norm_start)


def solution(mesh):
    torus = Mesh(
        mesh.devices.reshape(mesh.shape["grp"], 4, 4, 4), ("grp", "shard_0", "shard_1", "shard_2")
    )
    return jax.shard_map(
        on_device,
        mesh=torus,
        in_specs=(
            P(GRP_SHARD, None, None),
            P(GRP_SHARD),
            P(GRP_SHARD, None),
            P(GRP_SHARD),
            P(GRP_SHARD, None),
        ),
        out_specs=(P(SHARD, None), P(GRP_SHARD, None), P()),
        check_vma=False,
    )
```

profile of v0, /device:TPU:0, one launch (start us, length us, event | category | flops | bytes accessed | tf_op | source)
XLA Modules:
  0.0 452.3 jit_solution(524212540637487059)
XLA Ops:
  4.5 1.2 gather_fusion
  6.5 11.5 %all-to-all-start = ((s32[64,2,1]{1,2,0:T(1,128)}), s32[64,2,1]{1,2,0:T(1,128)S(1)}, u32[]{:S(2)}, u32[]{:S(2)}) async-start(s32[64,2,1]{1,2,0:T(1,128)} %bitcast.3), calls=%async_computation | async-start | bytes 65536 | tf_op jit(solution)/shard_map/all_to_all | solution.py:76
  18.0 1.0 multiply_reduce_fusion.8
  19.0 2.5 psum.140
  21.5 10.7 %psum.141 = f32[8]{0:T(128)S(1)} all-reduce(f32[8]{0:T(128)S(1)} %psum.140), channel_id=1, replica_groups=mesh['grp'=2,'shard_0'=4,'shard_1'=4,'shard_2'=4] {'shard_0'}, use_global_device_ids=true, to_apply=%region_5.6 | all-reduce | flops 8 | bytes 64 | tf_op jit(solution)/shard_map/psum | solution.py:30
  32.2 10.5 %psum.142 = f32[8]{0:T(128)S(1)} all-reduce(f32[8]{0:T(128)S(1)} %psum.141), channel_id=1, replica_groups=mesh['grp'=2,'shard_0'=4,'shard_1'=4,'shard_2'=4] {'shard_1'}, use_global_device_ids=true, to_apply=%region_6.7 | all-reduce | flops 8 | bytes 64 | tf_op jit(solution)/shard_map/psum | solution.py:30
  42.6 10.4 %psum.143 = f32[8]{0:T(128)S(1)} all-reduce(f32[8]{0:T(128)S(1)} %psum.142), channel_id=1, replica_groups=mesh['grp'=2,'shard_0'=4,'shard_1'=4,'shard_2'=4] {'shard_2'}, use_global_device_ids=true, to_apply=%region_7.8 | all-reduce | flops 8 | bytes 64 | tf_op jit(solution)/shard_map/psum | solution.py:30
  55.3 5.3 %convolution_bitcast_fusion.7 = f32[64,128,8]{1,2,0:T(8,128)S(1)} fusion(f32[64,128,8]{1,2,0:T(8,128)S(1)} %gather_fusion.1, f32[64,128,128]{2,1,0:T(8,128)} %param.5), kind=kOutput, calls=%fused_computation.21 | convolution fusion | flops 100663296 | bytes 4718592 | tf_op jit(solution)/shard_map/kij,kir->kjr/dot_general | solution.py:83
  61.8 1.1 all_to_all.92
  62.9 4.6 %all-to-all-start.1 = ((f32[64,2,1024]{2,1,0:T(2,128)}), f32[64,2,1024]{2,1,0:T(2,128)S(1)}, u32[]{:S(2)}, u32[]{:S(2)}) async-start(f32[64,2,1024]{2,1,0:T(2,128)} %all_to_all.92), calls=%async_computation.1 | async-start | bytes 1048576 | tf_op jit(solution)/shard_map/all_to_all | solution.py:87
  69.0 10.6 %all-to-all-done.1 = f32[64,2,1024]{2,1,0:T(2,128)S(1)} async-done(((f32[64,2,1024]{2,1,0:T(2,128)}), f32[64,2,1024]{2,1,0:T(2,128)S(1)}, u32[]{:S(2)}, u32[]{:S(2)}) %all-to-all-start.1) | async-done | bytes 524320 | tf_op jit(solution)/shard_map/all_to_all | solution.py:87
  80.4 3.8 all_to_all.137
  85.7 4.6 %all-to-all-start.3 = ((f32[64,1,8]{2,1,0:T(1,128)}), f32[64,1,8]{2,1,0:T(1,128)S(1)}, u32[]{:S(2)}, u32[]{:S(2)}) async-start(f32[64,1,8]{2,1,0:T(1,128)} %broadcast_in_dim.26), calls=%async_computation.3 | async-start | bytes 65536 | tf_op jit(solution)/shard_map/all_to_all | solution.py:18
  90.8 1.2 copy.179
  92.0 7.9 %all-to-all-done.3 = f32[64,1,8]{2,1,0:T(1,128)S(1)} async-done(((f32[64,1,8]{2,1,0:T(1,128)}), f32[64,1,8]{2,1,0:T(1,128)S(1)}, u32[]{:S(2)}, u32[]{:S(2)}) %all-to-all-start.3) | async-done | bytes 2080 | tf_op jit(solution)/shard_map/all_to_all | solution.py:18
  99.9 5.4 %all-to-all-start.4 = ((f32[64,2,1024]{2,1,0:T(2,128)}), f32[64,2,1024]{2,1,0:T(2,128)S(1)}, u32[]{:S(2)}, u32[]{:S(2)}) async-start(f32[64,2,1024]{2,1,0:T(2,128)} %copy.179), calls=%async_computation.4 | async-start | bytes 1048576 | tf_op jit(solution)/shard_map/all_to_all | solution.py:105
  105.4 12.5 %all-to-all-done.4 = f32[64,2,1024]{2,1,0:T(2,128)S(1)} async-done(((f32[64,2,1024]{2,1,0:T(2,128)}), f32[64,2,1024]{2,1,0:T(2,128)S(1)}, u32[]{:S(2)}, u32[]{:S(2)}) %all-to-all-start.4) | async-done | bytes 524320 | tf_op jit(solution)/shard_map/all_to_all | solution.py:105
  119.4 8.3 %convolution_bitcast_fusion.6 = f32[64,128,8]{1,2,0:T(8,128)S(1)} fusion(f32[64,128,8]{1,2,0:T(8,128)S(1)} %copy.181, f32[64,128,128]{2,1,0:T(8,128)} %param.5), kind=kOutput, calls=%fused_computation.20 | convolution fusion | flops 100663296 | bytes 4718592 | tf_op jit(solution)/shard_map/kij,kjr->kir/dot_general | solution.py:108
  130.2 5.3 %convolution_bitcast_fusion.5 = f32[64,128,8]{1,2,0:T(8,128)S(1)} fusion(f32[64,128,8]{1,2,0:T(8,128)S(1)} %gather_fusion.4, f32[64,128,128]{2,1,0:T(8,128)} %param.5), kind=kOutput, calls=%fused_computation.19 | convolution fusion | flops 100663296 | bytes 4718592 | tf_op jit(solution)/shard_map/kij,kir->kjr/dot_general | solution.py:83
  136.8 1.1 all_to_all.99
  137.8 4.6 %all-to-all-start.5 = ((f32[64,2,1024]{2,1,0:T(2,128)}), f32[64,2,1024]{2,1,0:T(2,128)S(1)}, u32[]{:S(2)}, u32[]{:S(2)}) async-start(f32[64,2,1024]{2,1,0:T(2,128)} %all_to_all.99), calls=%async_computation.5 | async-start | bytes 1048576 | tf_op jit(solution)/shard_map/all_to_all | solution.py:87
  142.5 2.5 psum.144
  145.0 10.7 %psum.145 = f32[8]{0:T(128)S(1)} all-reduce(f32[8]{0:T(128)S(1)} %psum.144), channel_id=1, replica_groups=mesh['grp'=2,'shard_0'=4,'shard_1'=4,'shard_2'=4] {'shard_0'}, use_global_device_ids=true, to_apply=%region_13.14 | all-reduce | flops 8 | bytes 64 | tf_op jit(solution)/shard_map/psum | solution.py:30
  155.9 10.5 %psum.146 = f32[8]{0:T(128)S(1)} all-reduce(f32[8]{0:T(128)S(1)} %psum.145), channel_id=1, replica_groups=mesh['grp'=2,'shard_0'=4,'shard_1'=4,'shard_2'=4] {'shard_1'}, use_global_device_ids=true, to_apply=%region_14.15 | all-reduce | flops 8 | bytes 64 | tf_op jit(solution)/shard_map/psum | solution.py:30
  166.5 10.4 %psum.147 = f32[8]{0:T(128)S(1)} all-reduce(f32[8]{0:T(128)S(1)} %psum.146), channel_id=1, replica_groups=mesh['grp'=2,'shard_0'=4,'shard_1'=4,'shard_2'=4] {'shard_2'}, use_global_device_ids=true, to_apply=%region_15.16 | all-reduce | flops 8 | bytes 64 | tf_op jit(solution)/shard_map/psum | solution.py:30
  177.8 3.8 all_to_all.138
  183.4 4.6 %all-to-all-start.7 = ((f32[64,1,8]{2,1,0:T(1,128)}), f32[64,1,8]{2,1,0:T(1,128)S(1)}, u32[]{:S(2)}, u32[]{:S(2)}) async-start(f32[64,1,8]{2,1,0:T(1,128)} %broadcast_in_dim.28), calls=%async_computation.7 | async-start | bytes 65536 | tf_op jit(solution)/shard_map/all_to_all | solution.py:18
  188.4 1.2 copy.189
  189.6 7.9 %all-to-all-done.7 = f32[64,1,8]{2,1,0:T(1,128)S(1)} async-done(((f32[64,1,8]{2,1,0:T(1,128)}), f32[64,1,8]{2,1,0:T(1,128)S(1)}, u32[]{:S(2)}, u32[]{:S(2)}) %all-to-all-start.7) | async-done | bytes 2080 | tf_op jit(solution)/shard_map/all_to_all | solution.py:18
  197.5 5.1 %all-to-all-start.8 = ((f32[64,2,1024]{2,1,0:T(2,128)}), f32[64,2,1024]{2,1,0:T(2,128)S(1)}, u32[]{:S(2)}, u32[]{:S(2)}) async-start(f32[64,2,1024]{2,1,0:T(2,128)} %copy.189), calls=%async_computation.8 | async-start | bytes 1048576 | tf_op jit(solution)/shard_map/all_to_all | solution.py:105
  202.7 12.5 %all-to-all-done.8 = f32[64,2,1024]{2,1,0:T(2,128)S(1)} async-done(((f32[64,2,1024]{2,1,0:T(2,128)}), f32[64,2,1024]{2,1,0:T(2,128)S(1)}, u32[]{:S(2)}, u32[]{:S(2)}) %all-to-all-start.8) | async-done | bytes 524320 | tf_op jit(solution)/shard_map/all_to_all | solution.py:105
  216.8 8.3 %convolution_bitcast_fusion.4 = f32[64,128,8]{1,2,0:T(8,128)S(1)} fusion(f32[64,128,8]{1,2,0:T(8,128)S(1)} %copy.191, f32[64,128,128]{2,1,0:T(8,128)} %param.5), kind=kOutput, calls=%fused_computation.18 | convolution fusion | flops 100663296 | bytes 4718592 | tf_op jit(solution)/shard_map/kij,kjr->kir/dot_general | solution.py:108
  227.5 5.3 %convolution_bitcast_fusion.3 = f32[64,128,8]{1,2,0:T(8,128)S(1)} fusion(f32[64,128,8]{1,2,0:T(8,128)S(1)} %gather_fusion.7, f32[64,128,128]{2,1,0:T(8,128)} %param.5), kind=kOutput, calls=%fused_computation.17 | convolution fusion | flops 100663296 | bytes 4718592 | tf_op jit(solution)/shard_map/kij,kir->kjr/dot_general | solution.py:83
  234.1 1.1 all_to_all.106
  235.2 4.6 %all-to-all-start.9 = ((f32[64,2,1024]{2,1,0:T(2,128)}), f32[64,2,1024]{2,1,0:T(2,128)S(1)}, u32[]{:S(2)}, u32[]{:S(2)}) async-start(f32[64,2,1024]{2,1,0:T(2,128)} %all_to_all.106), calls=%async_computation.9 | async-start | bytes 1048576 | tf_op jit(solution)/shard_map/all_to_all | solution.py:87
  239.8 2.5 psum.148
  242.3 10.7 %psum.149 = f32[8]{0:T(128)S(1)} all-reduce(f32[8]{0:T(128)S(1)} %psum.148), channel_id=1, replica_groups=mesh['grp'=2,'shard_0'=4,'shard_1'=4,'shard_2'=4] {'shard_0'}, use_global_device_ids=true, to_apply=%region_21.22 | all-reduce | flops 8 | bytes 64 | tf_op jit(solution)/shard_map/psum | solution.py:30
  253.0 10.5 %psum.150 = f32[8]{0:T(128)S(1)} all-reduce(f32[8]{0:T(128)S(1)} %psum.149), channel_id=1, replica_groups=mesh['grp'=2,'shard_0'=4,'shard_1'=4,'shard_2'=4] {'shard_1'}, use_global_device_ids=true, to_apply=%region_22.23 | all-reduce | flops 8 | bytes 64 | tf_op jit(solution)/shard_map/psum | solution.py:30
  263.6 10.4 %psum.151 = f32[8]{0:T(128)S(1)} all-reduce(f32[8]{0:T(128)S(1)} %psum.150), channel_id=1, replica_groups=mesh['grp'=2,'shard_0'=4,'shard_1'=4,'shard_2'=4] {'shard_2'}, use_global_device_ids=true, to_apply=%region_23.24 | all-reduce | flops 8 | bytes 64 | tf_op jit(solution)/shard_map/psum | solution.py:30
  274.9 3.8 all_to_all.139
  280.5 4.8 %all-to-all-start.11 = ((f32[64,1,8]{2,1,0:T(1,128)}), f32[64,1,8]{2,1,0:T(1,128)S(1)}, u32[]{:S(2)}, u32[]{:S(2)}) async-start(f32[64,1,8]{2,1,0:T(1,128)} %broadcast_in_dim.30), calls=%async_computation.11 | async-start | bytes 65536 | tf_op jit(solution)/shard_map/all_to_all | solution.py:18
  285.7 1.2 copy.198
  286.9 8.0 %all-to-all-done.11 = f32[64,1,8]{2,1,0:T(1,128)S(1)} async-done(((f32[64,1,8]{2,1,0:T(1,128)}), f32[64,1,8]{2,1,0:T(1,128)S(1)}, u32[]{:S(2)}, u32[]{:S(2)}) %all-to-all-start.11) | async-done | bytes 2080 | tf_op jit(solution)/shard_map/all_to_all | solution.py:18
  294.9 5.0 %all-to-all-start.12 = ((f32[64,2,1024]{2,1,0:T(2,128)}), f32[64,2,1024]{2,1,0:T(2,128)S(1)}, u32[]{:S(2)}, u32[]{:S(2)}) async-start(f32[64,2,1024]{2,1,0:T(2,128)} %copy.198), calls=%async_computation.12 | async-start | bytes 1048576 | tf_op jit(solution)/shard_map/all_to_all | solution.py:105
  299.9 12.5 %all-to-all-done.12 = f32[64,2,1024]{2,1,0:T(2,128)S(1)} async-done(((f32[64,2,1024]{2,1,0:T(2,128)}), f32[64,2,1024]{2,1,0:T(2,128)S(1)}, u32[]{:S(2)}, u32[]{:S(2)}) %all-to-all-start.12) | async-done | bytes 524320 | tf_op jit(solution)/shard_map/all_to_all | solution.py:105
  314.0 8.3 %convolution_bitcast_fusion.2 = f32[64,128,8]{1,2,0:T(8,128)S(1)} fusion(f32[64,128,8]{1,2,0:T(8,128)S(1)} %copy.200, f32[64,128,128]{2,1,0:T(8,128)} %param.5), kind=kOutput, calls=%fused_computation.16 | convolution fusion | flops 100663296 | bytes 4718592 | tf_op jit(solution)/shard_map/kij,kjr->kir/dot_general | solution.py:108
  324.7 5.3 %convolution_bitcast_fusion.1 = f32[64,128,8]{1,2,0:T(8,128)S(1)} fusion(f32[64,128,8]{1,2,0:T(8,128)S(1)} %gather_fusion.10, f32[64,128,128]{2,1,0:T(8,128)} %param.5), kind=kOutput, calls=%fused_computation.15 | convolution fusion | flops 100663296 | bytes 4718592 | tf_op jit(solution)/shard_map/kij,kir->kjr/dot_general | solution.py:83
  331.3 1.1 all_to_all.113
  332.4 4.6 %all-to-all-start.13 = ((f32[64,2,1024]{2,1,0:T(2,128)}), f32[64,2,1024]{2,1,0:T(2,128)S(1)}, u32[]{:S(2)}, u32[]{:S(2)}) async-start(f32[64,2,1024]{2,1,0:T(2,128)} %all_to_all.113), calls=%async_computation.13 | async-start | bytes 1048576 | tf_op jit(solution)/shard_map/all_to_all | solution.py:87
  337.0 2.5 psum.152
  339.5 10.7 %psum.153 = f32[8]{0:T(128)S(1)} all-reduce(f32[8]{0:T(128)S(1)} %psum.152), channel_id=1, replica_groups=mesh['grp'=2,'shard_0'=4,'shard_1'=4,'shard_2'=4] {'shard_0'}, use_global_device_ids=true, to_apply=%region_29.30 | all-reduce | flops 8 | bytes 64 | tf_op jit(solution)/shard_map/psum | solution.py:30
  350.2 10.5 %psum.154 = f32[8]{0:T(128)S(1)} all-reduce(f32[8]{0:T(128)S(1)} %psum.153), channel_id=1, replica_groups=mesh['grp'=2,'shard_0'=4,'shard_1'=4,'shard_2'=4] {'shard_1'}, use_global_device_ids=true, to_apply=%region_30.31 | all-reduce | flops 8 | bytes 64 | tf_op jit(solution)/shard_map/psum | solution.py:30
  360.8 10.4 %psum.155 = f32[8]{0:T(128)S(1)} all-reduce(f32[8]{0:T(128)S(1)} %psum.154), channel_id=1, replica_groups=mesh['grp'=2,'shard_0'=4,'shard_1'=4,'shard_2'=4] {'shard_2'}, use_global_device_ids=true, to_apply=%region_31.32 | all-reduce | flops 8 | bytes 64 | tf_op jit(solution)/shard_map/psum | solution.py:30
  372.1 3.8 all_to_all.140
  377.7 4.8 %all-to-all-start.15 = ((f32[64,1,8]{2,1,0:T(1,128)}), f32[64,1,8]{2,1,0:T(1,128)S(1)}, u32[]{:S(2)}, u32[]{:S(2)}) async-start(f32[64,1,8]{2,1,0:T(1,128)} %broadcast_in_dim.32), calls=%async_computation.15 | async-start | bytes 65536 | tf_op jit(solution)/shard_map/all_to_all | solution.py:18
  382.9 1.2 copy.207
  384.1 7.9 %all-to-all-done.15 = f32[64,1,8]{2,1,0:T(1,128)S(1)} async-done(((f32[64,1,8]{2,1,0:T(1,128)}), f32[64,1,8]{2,1,0:T(1,128)S(1)}, u32[]{:S(2)}, u32[]{:S(2)}) %all-to-all-start.15) | async-done | bytes 2080 | tf_op jit(solution)/shard_map/all_to_all | solution.py:18
  392.0 5.0 %all-to-all-start.16 = ((f32[64,2,1024]{2,1,0:T(2,128)}), f32[64,2,1024]{2,1,0:T(2,128)S(1)}, u32[]{:S(2)}, u32[]{:S(2)}) async-start(f32[64,2,1024]{2,1,0:T(2,128)} %copy.207), calls=%async_computation.16 | async-start | bytes 1048576 | tf_op jit(solution)/shard_map/all_to_all | solution.py:105
  397.1 12.5 %all-to-all-done.16 = f32[64,2,1024]{2,1,0:T(2,128)S(1)} async-done(((f32[64,2,1024]{2,1,0:T(2,128)}), f32[64,2,1024]{2,1,0:T(2,128)S(1)}, u32[]{:S(2)}, u32[]{:S(2)}) %all-to-all-start.16) | async-done | bytes 524320 | tf_op jit(solution)/shard_map/all_to_all | solution.py:105
  411.1 8.3 %convolution_bitcast_fusion = f32[64,128,8]{1,2,0:T(8,128)S(1)} fusion(f32[64,128,8]{1,2,0:T(8,128)S(1)} %copy.209, f32[64,128,128]{2,1,0:T(8,128)} %param.5), kind=kOutput, calls=%fused_computation.14 | convolution fusion | flops 100663296 | bytes 4718592 | tf_op jit(solution)/shard_map/kij,kjr->kir/dot_general | solution.py:108
  421.2 2.5 psum.156
  423.7 8.5 %psum.157 = f32[8]{0:T(128)S(1)} all-reduce(f32[8]{0:T(128)S(1)} %psum.156), channel_id=1, replica_groups=mesh['grp'=2,'shard_0'=4,'shard_1'=4,'shard_2'=4] {'shard_0'}, use_global_device_ids=true, to_apply=%region_37.38 | all-reduce | flops 8 | bytes 64 | tf_op jit(solution)/shard_map/psum | solution.py:30
  432.2 8.5 %psum.158 = f32[8]{0:T(128)S(1)} all-reduce(f32[8]{0:T(128)S(1)} %psum.157), channel_id=1, replica_groups=mesh['grp'=2,'shard_0'=4,'shard_1'=4,'shard_2'=4] {'shard_1'}, use_global_device_ids=true, to_apply=%region_38.39 | all-reduce | flops 8 | bytes 64 | tf_op jit(solution)/shard_map/psum | solution.py:30
  440.7 9.1 %psum.159 = f32[8]{0:T(128)S(1)} all-reduce(f32[8]{0:T(128)S(1)} %psum.158), channel_id=1, replica_groups=mesh['grp'=2,'shard_0'=4,'shard_1'=4,'shard_2'=4] {'shard_2'}, use_global_device_ids=true, to_apply=%region_39.40 | all-reduce | flops 8 | bytes 64 | tf_op jit(solution)/shard_map/psum | solution.py:30
  (144 shorter events, 42.9 us)
Async XLA Ops:
  6.5 56.4 %all-to-all-start = ((s32[64,2,1]{1,2,0:T(1,128)}), s32[64,2,1]{1,2,0:T(1,128)S(1)}, u32[]{:S(2)}, u32[]{:S(2)}) async-start(s32[64,2,1]{1,2,0:T(1,128)} %bitcast.3), calls=%async_computation | async-start | bytes 65536 | tf_op jit(solution)/shard_map/all_to_all | solution.py:76
  62.9 16.7 %all-to-all-start.1 = ((f32[64,2,1024]{2,1,0:T(2,128)}), f32[64,2,1024]{2,1,0:T(2,128)S(1)}, u32[]{:S(2)}, u32[]{:S(2)}) async-start(f32[64,2,1024]{2,1,0:T(2,128)} %all_to_all.92), calls=%async_computation.1 | async-start | bytes 1048576 | tf_op jit(solution)/shard_map/all_to_all | solution.py:87
  85.7 14.2 %all-to-all-start.3 = ((f32[64,1,8]{2,1,0:T(1,128)}), f32[64,1,8]{2,1,0:T(1,128)S(1)}, u32[]{:S(2)}, u32[]{:S(2)}) async-start(f32[64,1,8]{2,1,0:T(1,128)} %broadcast_in_dim.26), calls=%async_computation.3 | async-start | bytes 65536 | tf_op jit(solution)/shard_map/all_to_all | solution.py:18
  99.9 18.0 %all-to-all-start.4 = ((f32[64,2,1024]{2,1,0:T(2,128)}), f32[64,2,1024]{2,1,0:T(2,128)S(1)}, u32[]{:S(2)}, u32[]{:S(2)}) async-start(f32[64,2,1024]{2,1,0:T(2,128)} %copy.179), calls=%async_computation.4 | async-start | bytes 1048576 | tf_op jit(solution)/shard_map/all_to_all | solution.py:105
  119.4 9.9 %copy-start = (f32[2048,8]{0,1:T(8,128)S(1)}, f32[2048,8]{0,1:T(8,128)}, u32[]{:S(2)}) copy-start(f32[2048,8]{0,1:T(8,128)} %param.9) | copy-start | bytes 196612
  137.8 39.2 %all-to-all-start.5 = ((f32[64,2,1024]{2,1,0:T(2,128)}), f32[64,2,1024]{2,1,0:T(2,128)S(1)}, u32[]{:S(2)}, u32[]{:S(2)}) async-start(f32[64,2,1024]{2,1,0:T(2,128)} %all_to_all.99), calls=%async_computation.5 | async-start | bytes 1048576 | tf_op jit(solution)/shard_map/all_to_all | solution.py:87
  183.4 14.1 %all-to-all-start.7 = ((f32[64,1,8]{2,1,0:T(1,128)}), f32[64,1,8]{2,1,0:T(1,128)S(1)}, u32[]{:S(2)}, u32[]{:S(2)}) async-start(f32[64,1,8]{2,1,0:T(1,128)} %broadcast_in_dim.28), calls=%async_computation.7 | async-start | bytes 65536 | tf_op jit(solution)/shard_map/all_to_all | solution.py:18
  197.5 17.8 %all-to-all-start.8 = ((f32[64,2,1024]{2,1,0:T(2,128)}), f32[64,2,1024]{2,1,0:T(2,128)S(1)}, u32[]{:S(2)}, u32[]{:S(2)}) async-start(f32[64,2,1024]{2,1,0:T(2,128)} %copy.189), calls=%async_computation.8 | async-start | bytes 1048576 | tf_op jit(solution)/shard_map/all_to_all | solution.py:105
  235.2 38.9 %all-to-all-start.9 = ((f32[64,2,1024]{2,1,0:T(2,128)}), f32[64,2,1024]{2,1,0:T(2,128)S(1)}, u32[]{:S(2)}, u32[]{:S(2)}) async-start(f32[64,2,1024]{2,1,0:T(2,128)} %all_to_all.106), calls=%async_computation.9 | async-start | bytes 1048576 | tf_op jit(solution)/shard_map/all_to_all | solution.py:87
  280.5 14.4 %all-to-all-start.11 = ((f32[64,1,8]{2,1,0:T(1,128)}), f32[64,1,8]{2,1,0:T(1,128)S(1)}, u32[]{:S(2)}, u32[]{:S(2)}) async-start(f32[64,1,8]{2,1,0:T(1,128)} %broadcast_in_dim.30), calls=%async_computation.11 | async-start | bytes 65536 | tf_op jit(solution)/shard_map/all_to_all | solution.py:18
  294.9 17.6 %all-to-all-start.12 = ((f32[64,2,1024]{2,1,0:T(2,128)}), f32[64,2,1024]{2,1,0:T(2,128)S(1)}, u32[]{:S(2)}, u32[]{:S(2)}) async-start(f32[64,2,1024]{2,1,0:T(2,128)} %copy.198), calls=%async_computation.12 | async-start | bytes 1048576 | tf_op jit(solution)/shard_map/all_to_all | solution.py:105
  332.4 38.9 %all-to-all-start.13 = ((f32[64,2,1024]{2,1,0:T(2,128)}), f32[64,2,1024]{2,1,0:T(2,128)S(1)}, u32[]{:S(2)}, u32[]{:S(2)}) async-start(f32[64,2,1024]{2,1,0:T(2,128)} %all_to_all.113), calls=%async_computation.13 | async-start | bytes 1048576 | tf_op jit(solution)/shard_map/all_to_all | solution.py:87
  377.7 14.4 %all-to-all-start.15 = ((f32[64,1,8]{2,1,0:T(1,128)}), f32[64,1,8]{2,1,0:T(1,128)S(1)}, u32[]{:S(2)}, u32[]{:S(2)}) async-start(f32[64,1,8]{2,1,0:T(1,128)} %broadcast_in_dim.32), calls=%async_computation.15 | async-start | bytes 65536 | tf_op jit(solution)/shard_map/all_to_all | solution.py:18
  392.0 17.6 %all-to-all-start.16 = ((f32[64,2,1024]{2,1,0:T(2,128)}), f32[64,2,1024]{2,1,0:T(2,128)S(1)}, u32[]{:S(2)}, u32[]{:S(2)}) async-start(f32[64,2,1024]{2,1,0:T(2,128)} %copy.207), calls=%async_computation.16 | async-start | bytes 1048576 | tf_op jit(solution)/shard_map/all_to_all | solution.py:105
where the time goes:
time: 461 us; the launch traced here: 452 us
  blocking collectives  180 us (39%)
  waiting for transfers between devices  92.3 us (20%)
  starting transfers between devices  69.5 us (15%)
  matrix products  59.1 us (13%)
  local copies, waits for them, and re-layouts  39 us (8%)
  other arithmetic  10.6 us (2%)
    psum x20, blocking collectives, by_axis(): shard = lax.psum(shard, axis)  165 us
    all_to_all x4, waiting for transfers between devices, on_device(): lax.all_to_all(outgoing, SHARD, split_axis=0, concat_axis=0, tiled=True)  50 us
    dot_general x4, matrix products, on_device(): jnp.einsum('kij,kjr->kir', blocks, forward_pieces, precision=PRECISE)  33.3 us
    all_to_all x4, waiting for transfers between devices, sent_to_all(): lax.all_to_all(jnp.broadcast_to(shard[None], (length, *shard.shape)), axi...  31.6 us
    dot_general x4, matrix products, adjoint(): jnp.einsum('kij,kir->kjr', blocks, pieces, precision=PRECISE)  21.1 us
    all_to_all x4, starting transfers between devices, on_device(): lax.all_to_all(outgoing, SHARD, split_axis=0, concat_axis=0, tiled=True)  20.5 us
    all_to_all x4, starting transfers between devices, sent_to_all(): lax.all_to_all(jnp.broadcast_to(shard[None], (length, *shard.shape)), axi...  18.9 us
    all_to_all x4, starting transfers between devices, adjoint(): lax.all_to_all(padded[source], SHARD, split_axis=0, concat_axis=0, tiled=...  18.6 us
  transfers between devices with their start and end apart: 13, of which 9 were waited for; matrix products, arithmetic and copies ran while one was open for 4% of the time, Pallas kernels for 0%

commit v1 on v0

v1 whole, which is shorter than its diff:
```python
import jax
import jax.numpy as jnp
from jax import lax
from jax.experimental import pallas as pl
from jax.experimental.pallas import tpu as pltpu
from jax.sharding import Mesh
from jax.sharding import PartitionSpec as P

ITERS = 4
COLS_OWN = 16
SHARD = ("shard_0", "shard_1", "shard_2")
GRP_SHARD = ("grp", "shard_0", "shard_1", "shard_2")

OWNERS = 64
CAP = 2
BS = 128
RHS = 8
COUNT = 64
ROWS = 16
SLOTS = OWNERS * CAP
MSG = RHS * CAP + 1
TALL = OWNERS * MSG
CHUNK = 8
CHUNKS = COUNT // CHUNK

f32 = jnp.float32
bf16 = jnp.bfloat16


def diag_mask():
    sub = lax.broadcasted_iota(jnp.int32, (RHS, BS), 0)
    lane = lax.broadcasted_iota(jnp.int32, (RHS, BS), 1)
    return sub == lane


def row_of(column):
    return jnp.sum(jnp.where(diag_mask(), column, 0.0), axis=0, keepdims=True)


def column_of(row):
    spread = jnp.broadcast_to(row, (RHS, BS))
    total = jnp.sum(jnp.where(diag_mask(), spread, 0.0), axis=1, keepdims=True)
    return jnp.broadcast_to(total, (RHS, BS))


def squares(values):
    cube = values.reshape(values.shape[0] // RHS, RHS, BS)
    total = jnp.sum(jnp.sum(cube * cube, axis=0), axis=1, keepdims=True)
    return jnp.broadcast_to(total, (RHS, BS))


def tiled(column, count):
    return jnp.concatenate([column] * count, axis=0)


def sum_rows(ref):
    rows = [ref[pl.ds(MSG * o + MSG - 1, 1), :] for o in range(OWNERS)]
    while len(rows) > 1:
        rows = [rows[i] + rows[i + 1] for i in range(0, len(rows), 2)]
    return column_of(rows[0])


def put_rows(ref, row):
    for o in range(OWNERS):
        ref[pl.ds(MSG * o + MSG - 1, 1), :] = row


def split(x):
    high = x.astype(bf16)
    low = (x - high.astype(f32)).astype(bf16)
    return high, low


def stacked(x):
    high = x.astype(bf16).astype(f32)
    both = jnp.concatenate([high, x - high], axis=0).astype(bf16)
    return jnp.concatenate([both, both], axis=1)


def fold(out):
    first = out[0:8, 0:BS] + out[8:16, 0:BS]
    second = out[16:24, BS:] + out[24:32, BS:]
    return first, second


def chunk_copy(blocks, bbuf, sem, c):
    span = pl.ds(c * CHUNK, CHUNK)
    return pltpu.make_async_copy(blocks.at[span], bbuf.at[span], sem.at[c])


def split_left(us, left):
    for r in range(ROWS):
        us[r] = stacked(left[r * RHS : (r + 1) * RHS])


def adjoint_pair(k, row, pos, us, h0, l0, h1, l1, msg):
    lhs = jnp.concatenate([us[row[k]], us[row[k + 1]]], axis=0)
    rhs = jnp.concatenate(
        [jnp.concatenate([h0, l0], axis=0), jnp.concatenate([h1, l1], axis=0)], axis=1
    )
    out = lax.dot_general(lhs, rhs, (((1,), (0,)), ((), ())), preferred_element_type=f32)
    first, second = fold(out)
    msg[pl.ds(pos[k], RHS), :] = first
    msg[pl.ds(pos[k + 1], RHS), :] = second


def first_kernel(owner, row, col, right, blocks, msg, pos, bbuf, us, taken, sem):
    def begin(c, carry):
        chunk_copy(blocks, bbuf, sem, c).start()
        return carry

    lax.fori_loop(0, CHUNKS, begin, 0)
    right_all = right[...]
    msg[...] = jnp.zeros((TALL, BS), f32)
    put_rows(msg, row_of(squares(right_all)))
    split_left(us, right_all)

    def clear(o, carry):
        taken[o] = 0
        return carry

    lax.fori_loop(0, OWNERS, clear, 0)
    lane = lax.broadcasted_iota(jnp.int32, (1, BS), 1)

    def place(k, carry):
        o = owner[k]
        rank = taken[o]
        taken[o] = rank + 1
        pos[k] = o * MSG + rank * RHS
        span = pl.ds(o * MSG + MSG - 1, 1)
        msg[span, :] = jnp.where(lane == RHS + rank, col[k].astype(f32), msg[span, :])
        return carry

    lax.fori_loop(0, COUNT, place, 0)

    def chunk(c, carry):
        chunk_copy(blocks, bbuf, sem, c).wait()
        for j in range(0, CHUNK, 2):
            k = c * CHUNK + j
            h0, l0 = split(bbuf[k])
            h1, l1 = split(bbuf[k + 1])
            adjoint_pair(k, row, pos, us, h0, l0, h1, l1, msg)
        return carry

    lax.fori_loop(0, CHUNKS, chunk, 0)


def forward_part(pos, row, inc, uraw, nleft, blocks, lraw, bbuf, sem, keep):
    def begin(c, carry):
        chunk_copy(blocks, bbuf, sem, c).start()
        return carry

    lax.fori_loop(0, CHUNKS, begin, 0)
    norm_right = jnp.sqrt(sum_rows(inc))
    lraw[...] = jnp.zeros((ROWS * RHS, BS), f32)

    def chunk(c, carry):
        chunk_copy(blocks, bbuf, sem, c).wait()
        for j in range(0, CHUNK, 2):
            k = c * CHUNK + j
            h0, l0 = split(bbuf[k])
            h1, l1 = split(bbuf[k + 1])
            if keep is not None:
                keep[0][k] = h0
                keep[1][k] = l0
                keep[0][k + 1] = h1
                keep[1][k + 1] = l1
            lhs = jnp.concatenate(
                [stacked(inc[pl.ds(pos[k], RHS), :]), stacked(inc[pl.ds(pos[k + 1], RHS), :])],
                axis=0,
            )
            rhs = jnp.concatenate(
                [jnp.concatenate([h0, l0], axis=1), jnp.concatenate([h1, l1], axis=1)], axis=0
            )
            out = lax.dot_general(lhs, rhs, (((1,), (1,)), ((), ())), preferred_element_type=f32)
            first, second = fold(out)
            span = pl.ds(pl.multiple_of(row[k] * RHS, RHS), RHS)
            lraw[span, :] = lraw[span, :] + first
            span = pl.ds(pl.multiple_of(row[k + 1] * RHS, RHS), RHS)
            lraw[span, :] = lraw[span, :] + second
        return carry

    lax.fori_loop(0, CHUNKS, chunk, 0)
    left = lraw[...] / tiled(norm_right, ROWS) - tiled(norm_right, ROWS) * (
        uraw[...] / tiled(nleft[...], ROWS)
    )
    lraw[...] = left
    return left, norm_right


def user_kernel(pos, row, inc, uraw, nleft, blocks, msg, lraw, nright, bbuf, high, low, us, sem):
    left, norm_right = forward_part(
        pos, row, inc, uraw, nleft, blocks, lraw, bbuf, sem, (high, low)
    )
    nright[...] = norm_right
    msg[...] = jnp.zeros((TALL, BS), f32)
    put_rows(msg, row_of(squares(left)))
    split_left(us, left)

    def chunk(c, carry):
        for j in range(0, CHUNK, 2):
            k = c * CHUNK + j
            adjoint_pair(k, row, pos, us, high[k], low[k], high[k + 1], low[k + 1], msg)
        return carry

    lax.fori_loop(0, CHUNKS, chunk, 0)


def last_user_kernel(pos, row, inc, uraw, nleft, blocks, msg, lraw, nright, bbuf, sem):
    left, norm_right = forward_part(pos, row, inc, uraw, nleft, blocks, lraw, bbuf, sem, None)
    nright[...] = norm_right
    msg[...] = jnp.broadcast_to(row_of(squares(left)), msg.shape)


def gather_slots(inc, cols_of, half, parts):
    for part in parts:
        part[...] = jnp.zeros((COLS_OWN * RHS, BS), f32)

    def step(g, carry):
        for j in range(4):
            o = g * 4 + j
            for s in range(CAP):
                c = cols_of(o, s)
                span = pl.ds(pl.multiple_of(c * RHS, RHS), RHS)
                part = parts[(2 * j + s) % len(parts)]
                part[span, :] = part[span, :] + inc[pl.ds(o * MSG + s * RHS, RHS), :]
        return carry

    lax.fori_loop(0, OWNERS // 4, step, 0)
    half[pl.ds(0, COLS_OWN * RHS), :] = (parts[0][...] + parts[1][...]) + (
        parts[2][...] + parts[3][...]
    )
    half[pl.ds(COLS_OWN * RHS, RHS), :] = sum_rows(inc)


def first_owner_kernel(inc, half, cols, p0, p1, p2, p3, vcols, scols, sem):
    for o in range(OWNERS):
        vcols[pl.ds(o, 1), :] = inc[pl.ds(MSG * o + MSG - 1, 1), :].astype(jnp.int32)
    copy = pltpu.make_async_copy(vcols, scols, sem)
    copy.start()
    copy.wait()

    def cols_of(o, s):
        c = scols[o, RHS + s]
        cols[o * CAP + s] = c
        return c

    gather_slots(inc, cols_of, half, (p0, p1, p2, p3))


def owner_kernel(cols, inc, half, p0, p1, p2, p3):
    gather_slots(inc, lambda o, s: cols[o * CAP + s], half, (p0, p1, p2, p3))


def send_slots(cols, raw, msg):
    put_rows(msg, row_of(squares(raw[...])))

    def step(g, carry):
        for j in range(4):
            o = g * 4 + j
            for s in range(CAP):
                c = cols[o * CAP + s]
                span = pl.ds(pl.multiple_of(c * RHS, RHS), RHS)
                msg[pl.ds(o * MSG + s * RHS, RHS), :] = raw[span, :]
        return carry

    lax.fori_loop(0, OWNERS // 4, step, 0)


def first_send_kernel(cols, mine, theirs, msg, raw, nleft):
    norm_left = jnp.sqrt(mine[pl.ds(COLS_OWN * RHS, RHS), :] + theirs[pl.ds(COLS_OWN * RHS, RHS), :])
    nleft[...] = norm_left
    body = pl.ds(0, COLS_OWN * RHS)
    raw[...] = (mine[body, :] + theirs[body, :]) / tiled(norm_left, COLS_OWN)
    send_slots(cols, raw, msg)


def advance(first, solution, search, diag_bar, residual, norm_left, norm_right, right_vec):
    radius = jnp.sqrt(diag_bar * diag_bar + norm_left * norm_left)
    cosine = diag_bar / radius
    sine_term = norm_left / radius
    return radius, cosine, sine_term


def send_kernel(first, cols, mine, theirs, qprev, nright, *refs):
    if first:
        start, msg, raw, nleft, sol, search, scal = refs
    else:
        sol_in, search_in, scal_in, msg, raw, nleft, sol, search, scal = refs
    n = COLS_OWN
    norm_left = jnp.sqrt(mine[pl.ds(n * RHS, RHS), :] + theirs[pl.ds(n * RHS, RHS), :])
    norm_right = nright[...]
    nleft[...] = norm_left
    body = pl.ds(0, n * RHS)
    vec = qprev[...] / tiled(norm_right, n)
    raw[...] = (mine[body, :] + theirs[body, :]) / tiled(norm_left, n) - tiled(norm_left, n) * vec
    send_slots(cols, raw, msg)
    if first:
        old_search = vec
        diag_bar = norm_right
        residual = start[...]
        old_sol = jnp.zeros((n * RHS, BS), f32)
    else:
        radius = scal_in[pl.ds(0, RHS), :]
        cosine = scal_in[pl.ds(RHS, RHS), :]
        sine_term = scal_in[pl.ds(2 * RHS, RHS), :]
        residual = scal_in[pl.ds(3 * RHS, RHS), :]
        coupling = sine_term * norm_right
        old_search = vec - tiled(coupling / radius, n) * search_in[...]
        diag_bar = -cosine * norm_right
        old_sol = sol_in[...]
    radius = jnp.sqrt(diag_bar * diag_bar + norm_left * norm_left)
    cosine = diag_bar / radius
    sine_term = norm_left / radius
    sol[...] = old_sol + tiled(cosine * residual / radius, n) * old_search
    search[...] = old_search
    scal[pl.ds(0, RHS), :] = radius
    scal[pl.ds(RHS, RHS), :] = cosine
    scal[pl.ds(2 * RHS, RHS), :] = sine_term
    scal[pl.ds(3 * RHS, RHS), :] = sine_term * residual


def final_kernel(rows, lraw, qprev, nright, sol_in, search_in, scal_in, start, sol, left, rel):
    n = COLS_OWN
    norm_left = jnp.sqrt(column_of(jnp.sum(rows[...], axis=0, keepdims=True)))
    norm_right = nright[...]
    left[...] = lraw[...] / tiled(norm_left, ROWS)
    radius = scal_in[pl.ds(0, RHS), :]
    cosine = scal_in[pl.ds(RHS, RHS), :]
    sine_term = scal_in[pl.ds(2 * RHS, RHS), :]
    residual = scal_in[pl.ds(3 * RHS, RHS), :]
    vec = qprev[...] / tiled(norm_right, n)
    search = vec - tiled(sine_term * norm_right / radius, n) * search_in[...]
    diag_bar = -cosine * norm_right
    radius = jnp.sqrt(diag_bar * diag_bar + norm_left * norm_left)
    cosine = diag_bar / radius
    sine_term = norm_left / radius
    sol[...] = sol_in[...] + tiled(cosine * residual / radius, n) * search
    rel[...] = row_of(sine_term * residual / start[...])


def shape(*dims, dtype=f32):
    return jax.ShapeDtypeStruct(dims, dtype)


VMEM = pl.BlockSpec(memory_space=pltpu.VMEM)
SMEM = pl.BlockSpec(memory_space=pltpu.SMEM)
HBM = pl.BlockSpec(memory_space=pl.ANY)
PARTS = [pltpu.VMEM((COLS_OWN * RHS, BS), f32)] * 4
BUFFER = pltpu.VMEM((COUNT, BS, BS), f32)
LEFTS = pltpu.VMEM((ROWS, 2 * RHS, 2 * BS), bf16)
SEMS = pltpu.SemaphoreType.DMA((CHUNKS,))


def call(body, ins, outs, specs_out=None, scratch=()):
    return pl.pallas_call(
        body,
        out_shape=outs,
        in_specs=ins,
        out_specs=specs_out or jax.tree.map(lambda _: VMEM, outs),
        scratch_shapes=scratch,
        compiler_params=pltpu.CompilerParams(vmem_limit_bytes=24 * 1024 * 1024),
    )


def exchange(msg):
    sent = msg.reshape(OWNERS, MSG * BS)
    return lax.all_to_all(sent, SHARD, 0, 0, tiled=True).reshape(TALL, BS)


def swap(half):
    return lax.ppermute(half, "grp", [(0, 1), (1, 0)])


def on_device(blocks, block_row, block_owner, block_col, right_side):
    row = lax.rem(block_row, ROWS)
    owner = block_owner[:, 0]
    right = right_side.reshape(ROWS, BS, RHS).transpose(0, 2, 1).reshape(ROWS * RHS, BS)
    vec = shape(COLS_OWN * RHS, BS)
    col8 = shape(RHS, BS)
    msg_shape = shape(TALL, BS)
    half_shape = shape(COLS_OWN * RHS + RHS, BS)

    msg, pos = call(
        first_kernel,
        [SMEM, SMEM, SMEM, VMEM, HBM],
        (msg_shape, shape(COUNT, dtype=jnp.int32)),
        (VMEM, SMEM),
        [BUFFER, LEFTS, pltpu.SMEM((OWNERS,), jnp.int32), SEMS],
    )(owner, row, block_col, right, blocks)
    inc = exchange(msg)
    half, cols = call(
        first_owner_kernel,
        [VMEM],
        (half_shape, shape(SLOTS, dtype=jnp.int32)),
        (VMEM, SMEM),
        PARTS
        + [
            pltpu.VMEM((OWNERS, BS), jnp.int32),
            pltpu.SMEM((OWNERS, BS), jnp.int32),
            pltpu.SemaphoreType.DMA(()),
        ],
    )(inc)
    msg, raw, norm_left = call(
        first_send_kernel, [SMEM, VMEM, VMEM], (msg_shape, vec, col8)
    )(cols, half, swap(half))
    start = norm_left
    left = right
    state = None
    for repeat in range(ITERS):
        inc = exchange(msg)
        if repeat == ITERS - 1:
            break
        msg, left, norm_right = call(
            user_kernel,
            [SMEM, SMEM, VMEM, VMEM, VMEM, HBM],
            (msg_shape, vec, col8),
            None,
            [
                BUFFER,
                pltpu.VMEM((COUNT, BS, BS), bf16),
                pltpu.VMEM((COUNT, BS, BS), bf16),
                LEFTS,
                SEMS,
            ],
        )(pos, row, inc, left, norm_left, blocks)
        inc = exchange(msg)
        half = call(owner_kernel, [SMEM, VMEM], half_shape, None, PARTS)(cols, inc)
        first = repeat == 0
        tail = (start,) if first else state
        outs = call(
            lambda *refs, first=first: send_kernel(first, *refs),
            [SMEM] + [VMEM] * (4 + len(tail)),
            (msg_shape, vec, col8, vec, vec, shape(4 * RHS, BS)),
        )(cols, half, swap(half), raw, norm_right, *tail)
        msg, raw, norm_left = outs[:3]
        state = outs[3:]
    rows, left, norm_right = call(
        last_user_kernel,
        [SMEM, SMEM, VMEM, VMEM, VMEM, HBM],
        (shape(2 * OWNERS, BS), vec, col8),
        None,
        [BUFFER, SEMS],
    )(pos, row, inc, left, norm_left, blocks)
    rows = lax.all_to_all(rows, GRP_SHARD, 0, 0, tiled=True)
    sol, left, rel = call(
        final_kernel, [VMEM] * 8, (vec, vec, shape(1, BS))
    )(rows, left, raw, norm_right, *state, start)

    def tall(x):
        return x.reshape(COLS_OWN, RHS, BS).transpose(0, 2, 1).reshape(COLS_OWN * BS, RHS)

    return tall(sol), tall(left), rel[0, :RHS]


def solution(mesh):
    torus = Mesh(
        mesh.devices.reshape(mesh.shape["grp"], 4, 4, 4), ("grp", "shard_0", "shard_1", "shard_2")
    )
    return jax.shard_map(
        on_device,
        mesh=torus,
        in_specs=(
            P(GRP_SHARD, None, None),
            P(GRP_SHARD),
            P(GRP_SHARD, None),
            P(GRP_SHARD),
            P(GRP_SHARD, None),
        ),
        out_specs=(P(SHARD, None), P(GRP_SHARD, None), P()),
        check_vma=False,
    )
```

time: 461 us -> 208 us (0.45); the launches traced: 452 us -> 207 us
  waiting for transfers between devices: 92.3 us -> 4.99 us
  starting transfers between devices: 69.5 us -> 0.13 us
  matrix products: 59.1 us -> 0 us
  local copies, waits for them, and re-layouts: 39 us -> 4.85 us
  Pallas kernels: 0 us -> 31.8 us
  blocking collectives: 180 us -> 164 us
  other arithmetic: 10.6 us -> 0.66 us
    psum x20 -> x0, blocking collectives: 165 us -> none  [by_axis(): shard = lax.psum(shard, axis)]
    all_to_all x4 -> x9, blocking collectives: 15.4 us -> 164 us  [the longest x8 151 us: exchange(): return lax.all_to_all(sent, SHARD, 0, 0, tiled=True).reshape(TALL, BS)]
    all_to_all x13 -> x0, waiting for transfers between devices: 92.3 us -> none  [the longest x4 50 us: on_device(): lax.all_to_all(outgoing, SHARD, split_axis=0, concat_axis=0, tiled=True)]
    all_to_all x13 -> x0, starting transfers between devices: 69.5 us -> none  [the longest x4 20.5 us: on_device(): lax.all_to_all(outgoing, SHARD, split_axis=0, concat_axis=0, tiled=True)]
    dot_general x20 -> x0, matrix products: 59.1 us -> none  [the longest x4 33.3 us: on_device(): jnp.einsum('kij,kjr->kir', blocks, forward_pieces, precision=PRECISE)]
    pallas_call x0 -> x14, Pallas kernels: none -> 31.8 us  [the longest x3 15.1 us: on_device(): call(user_kernel, [SMEM, SMEM, VMEM, VMEM, VMEM, HBM], (msg_shape, vec, c...]
    gather x17 -> x0, local copies, waits for them, and re-layouts: 10.5 us -> none  [the longest x8 3.49 us: on_device(): forward_pieces = forward_incoming[position]]
    reshape x24 -> x0, local copies, waits for them, and re-layouts: 8.75 us -> none  [the longest x8 3.58 us: on_device(): image = summed.reshape(row_blocks * block_width, columns)]
  transfers between devices with their start and end apart: 13 -> 4, of which waited for: 9 -> 4; matrix products, arithmetic and copies ran while one was open for 4% -> 0% of each run, Pallas kernels for 0% -> 0%
where the time goes in v1:
time: 208 us; the launch traced here: 207 us
  blocking collectives  164 us (79%)
  Pallas kernels  31.8 us (15%)
  waiting for transfers between devices  4.99 us (2%)
  local copies, waits for them, and re-layouts  4.85 us (2%)
    all_to_all x8, blocking collectives, exchange(): return lax.all_to_all(sent, SHARD, 0, 0, tiled=True).reshape(TALL, BS)  151 us
    pallas_call x3, Pallas kernels, on_device(): call(user_kernel, [SMEM, SMEM, VMEM, VMEM, VMEM, HBM], (msg_shape, vec, c...  15.1 us
    all_to_all x1, blocking collectives, on_device(): rows = lax.all_to_all(rows, GRP_SHARD, 0, 0, tiled=True)  13.3 us
    ppermute x4, waiting for transfers between devices, swap(): return lax.ppermute(half, 'grp', [(0, 1), (1, 0)])  4.99 us
    unnamed x12, local copies, waits for them, and re-layouts  4.34 us
    pallas_call x1, Pallas kernels, on_device(): call(first_kernel, [SMEM, SMEM, SMEM, VMEM, HBM], (msg_shape, shape(COUNT...  4.27 us
  transfers between devices with their start and end apart: 4, of which 4 were waited for; matrix products, arithmetic and copies ran while one was open for 0% of the time, Pallas kernels for 0%

profile of v1, /device:TPU:0, one launch (start us, length us, event | category | flops | bytes accessed | tf_op | source)
XLA Modules:
  0.0 207.2 jit_solution(18240318960585854337)
XLA Ops:
  0.6 0.7 compare_select_fusion.row
  1.3 0.0 copy-start
  1.3 2.2 %copy-done = f32[64,128,128]{2,1,0:T(8,128)S(1)} copy-done((f32[64,128,128]{2,1,0:T(8,128)S(1)}, f32[64,128,128]{2,1,0:T(8,128)}, u32[]{:S(2)}) %copy-start) | copy-done | bytes 4194328
  3.5 0.0 copy-start.2
  3.5 0.8 copy-done.2
  4.3 0.0 copy-start.4
  4.3 0.7 copy-done.4
  5.0 0.0 copy-start.5
  5.0 0.7 copy-done.5
  5.6 0.0 copy-start.1
  5.6 0.0 copy-start.3
  5.6 4.3 %shard_map.76 = (f32[1088,128]{1,0:T(8,128)S(1)}, s32[64]{0:T(128)S(1)}) custom-call(s32[64]{0:T(128)S(1)} %bitcast.58, s32[64]{0:T(128)S(1)} %compare_select_fusion.row, s32[64]{0:T(128)S(1)} %copy-done.5, f32[128,128]{1,0:T(8,128)S(1)} %bitcast.54, f32[64,128,128]{2,1,0:T(8,128)S(1)} %copy-done), custom_call_target="tpu_custom_call" | custom-call | tf_op jit(solution)/shard_map/pallas_call | solution.py:384
  9.9 25.1 %all_to_all.83 = f32[64,1,2176]{2,1,0:T(1,128)S(1)} all-to-all(f32[64,1,2176]{2,1,0:T(1,128)S(1)} %bitcast.53), channel_id=1, replica_groups=mesh['grp'=2,'shard_0'=4,'shard_1'=4,'shard_2'=4] {'shard_0','shard_1','..., dimensions={0} | all-to-all | bytes 1114112 | tf_op jit(solution)/shard_map/all_to_all | solution.py:368
  35.0 2.0 shard_map.77
  37.0 0.1 collective-permute-start
  37.1 1.2 collective-permute-done.theirs
  38.4 0.9 shard_map.78
  39.3 18.5 %all_to_all.84 = f32[64,1,2176]{2,1,0:T(1,128)S(1)} all-to-all(f32[64,1,2176]{2,1,0:T(1,128)S(1)} %bitcast.51), channel_id=1, replica_groups=mesh['grp'=2,'shard_0'=4,'shard_1'=4,'shard_2'=4] {'shard_0','shard_1','..., dimensions={0} | all-to-all | bytes 1114112 | tf_op jit(solution)/shard_map/all_to_all | solution.py:368
  57.8 0.0 copy-done.1
  57.8 0.0 copy-done.3
  57.8 5.0 %shard_map.79 = (f32[1088,128]{1,0:T(8,128)S(1)}, f32[128,128]{1,0:T(8,128)S(1)}, f32[8,128]{1,0:T(8,128)S(1)}) custom-call(s32[64]{0:T(128)S(1)} %get-tuple-element.43.pos, s32[64]{0:T(128)S(1)} %compare_select_fusion.row, f32[1088,128]{1,0:T(8,128)S(1)} %bitcast.41, f32[128,128]{1,0:T(8,128)S(1)} %bitcast.55, ...), custom_call_target="tpu_custom_call" | custom-call | tf_op jit(solution)/shard_map/pallas_call | solution.py:414
  62.9 17.1 %all_to_all.85 = f32[64,1,2176]{2,1,0:T(1,128)S(1)} all-to-all(f32[64,1,2176]{2,1,0:T(1,128)S(1)} %bitcast.52), channel_id=1, replica_groups=mesh['grp'=2,'shard_0'=4,'shard_1'=4,'shard_2'=4] {'shard_0','shard_1','..., dimensions={0} | all-to-all | bytes 1114112 | tf_op jit(solution)/shard_map/all_to_all | solution.py:368
  80.0 0.9 shard_map.80.refs_1_
  80.9 0.0 collective-permute-start.1
  80.9 1.2 collective-permute-done.1.refs_2_
  82.2 0.9 shard_map.81
  83.1 18.5 %all_to_all.86 = f32[64,1,2176]{2,1,0:T(1,128)S(1)} all-to-all(f32[64,1,2176]{2,1,0:T(1,128)S(1)} %bitcast.48), channel_id=1, replica_groups=mesh['grp'=2,'shard_0'=4,'shard_1'=4,'shard_2'=4] {'shard_0','shard_1','..., dimensions={0} | all-to-all | bytes 1114112 | tf_op jit(solution)/shard_map/all_to_all | solution.py:368
  101.6 5.0 %shard_map.82 = (f32[1088,128]{1,0:T(8,128)S(1)}, f32[128,128]{1,0:T(8,128)S(1)}, f32[8,128]{1,0:T(8,128)S(1)}) custom-call(s32[64]{0:T(128)S(1)} %get-tuple-element.43.pos, s32[64]{0:T(128)S(1)} %compare_select_fusion.row, f32[1088,128]{1,0:T(8,128)S(1)} %bitcast.39, f32[128,128]{1,0:T(8,128)S(1)} %get-tuple-element.53.uraw, ...), custom_call_target="tpu_custom_call" | custom-call | tf_op jit(solution)/shard_map/pallas_call | solution.py:414
  106.6 17.1 %all_to_all.87 = f32[64,1,2176]{2,1,0:T(1,128)S(1)} all-to-all(f32[64,1,2176]{2,1,0:T(1,128)S(1)} %bitcast.49), channel_id=1, replica_groups=mesh['grp'=2,'shard_0'=4,'shard_1'=4,'shard_2'=4] {'shard_0','shard_1','..., dimensions={0} | all-to-all | bytes 1114112 | tf_op jit(solution)/shard_map/all_to_all | solution.py:368
  123.8 0.9 shard_map.83.refs_1_
  124.7 0.0 collective-permute-start.2
  124.7 1.2 collective-permute-done.2.refs_2_
  126.0 0.9 shard_map.84
  126.9 18.5 %all_to_all.88 = f32[64,1,2176]{2,1,0:T(1,128)S(1)} all-to-all(f32[64,1,2176]{2,1,0:T(1,128)S(1)} %bitcast.47), channel_id=1, replica_groups=mesh['grp'=2,'shard_0'=4,'shard_1'=4,'shard_2'=4] {'shard_0','shard_1','..., dimensions={0} | all-to-all | bytes 1114112 | tf_op jit(solution)/shard_map/all_to_all | solution.py:368
  145.4 5.0 %shard_map.85 = (f32[1088,128]{1,0:T(8,128)S(1)}, f32[128,128]{1,0:T(8,128)S(1)}, f32[8,128]{1,0:T(8,128)S(1)}) custom-call(s32[64]{0:T(128)S(1)} %get-tuple-element.43.pos, s32[64]{0:T(128)S(1)} %compare_select_fusion.row, f32[1088,128]{1,0:T(8,128)S(1)} %bitcast.40, f32[128,128]{1,0:T(8,128)S(1)} %get-tuple-element.62.uraw, ...), custom_call_target="tpu_custom_call" | custom-call | tf_op jit(solution)/shard_map/pallas_call | solution.py:414
  150.4 17.1 %all_to_all.89 = f32[64,1,2176]{2,1,0:T(1,128)S(1)} all-to-all(f32[64,1,2176]{2,1,0:T(1,128)S(1)} %bitcast.50), channel_id=1, replica_groups=mesh['grp'=2,'shard_0'=4,'shard_1'=4,'shard_2'=4] {'shard_0','shard_1','..., dimensions={0} | all-to-all | bytes 1114112 | tf_op jit(solution)/shard_map/all_to_all | solution.py:368
  167.6 0.9 shard_map.86.refs_1_
  168.5 0.0 collective-permute-start.3
  168.5 1.2 collective-permute-done.3.refs_2_
  169.8 0.9 shard_map.87
  170.7 18.5 %all_to_all.90 = f32[64,1,2176]{2,1,0:T(1,128)S(1)} all-to-all(f32[64,1,2176]{2,1,0:T(1,128)S(1)} %bitcast.46), channel_id=1, replica_groups=mesh['grp'=2,'shard_0'=4,'shard_1'=4,'shard_2'=4] {'shard_0','shard_1','..., dimensions={0} | all-to-all | bytes 1114112 | tf_op jit(solution)/shard_map/all_to_all | solution.py:368
  189.2 3.4 %shard_map.88 = (f32[128,128]{1,0:T(8,128)S(1)}, f32[128,128]{1,0:T(8,128)S(1)}, f32[8,128]{1,0:T(8,128)S(1)}) custom-call(s32[64]{0:T(128)S(1)} %get-tuple-element.43.pos, s32[64]{0:T(128)S(1)} %compare_select_fusion.row, f32[1088,128]{1,0:T(8,128)S(1)} %bitcast.38, f32[128,128]{1,0:T(8,128)S(1)} %get-tuple-element.71.uraw, ...), custom_call_target="tpu_custom_call" | custom-call | tf_op jit(solution)/shard_map/pallas_call | solution.py:438
  192.6 13.3 %all_to_all.91 = f32[128,1,128]{2,1,0:T(1,128)S(1)} all-to-all(f32[128,1,128]{2,1,0:T(1,128)S(1)} %bitcast.57), channel_id=1, replica_groups=mesh['grp'=2,'shard_0'=4,'shard_1'=4,'shard_2'=4] {'grp','shard_0','shar..., dimensions={0} | all-to-all | bytes 131072 | tf_op jit(solution)/shard_map/all_to_all | solution.py:445
  205.9 0.8 shard_map.89
  206.7 0.5 slice_bitcast_fusion
Async XLA Ops:
  1.3 2.2 %copy-start = (f32[64,128,128]{2,1,0:T(8,128)S(1)}, f32[64,128,128]{2,1,0:T(8,128)}, u32[]{:S(2)}) copy-start(f32[64,128,128]{2,1,0:T(8,128)} %blocks.9) | copy-start | bytes 12582916
  3.5 0.8 copy-start.2
  4.3 0.7 copy-start.4
  5.0 0.7 copy-start.5
  5.6 52.2 %copy-start.1 = (f32[64,128,128]{2,1,0:T(8,128)S(1)}, f32[64,128,128]{2,1,0:T(8,128)}, u32[]{:S(2)}) copy-start(f32[64,128,128]{2,1,0:T(8,128)} %blocks.9) | copy-start | bytes 12582916
  5.6 52.2 %copy-start.3 = (f32[2048,8]{0,1:T(8,128)S(1)}, f32[2048,8]{0,1:T(8,128)}, u32[]{:S(2)}) copy-start(f32[2048,8]{0,1:T(8,128)} %param.9) | copy-start | bytes 196612
  37.0 1.3 collective-permute-start
  80.9 1.3 collective-permute-start.1
  124.7 1.3 collective-permute-start.2
  168.5 1.3 collective-permute-start.3

commit v2 on v1

v2 whole, which is shorter than its diff:
```python
import jax
import jax.numpy as jnp
from jax import lax
from jax.experimental import pallas as pl
from jax.experimental.pallas import tpu as pltpu
from jax.sharding import Mesh
from jax.sharding import PartitionSpec as P

ITERS = 4
COLS_OWN = 16
SHARD = ("shard_0", "shard_1", "shard_2")
GRP_SHARD = ("grp", "shard_0", "shard_1", "shard_2")

OWNERS = 64
CAP = 2
BS = 128
RHS = 8
COUNT = 64
ROWS = 16
SLOTS = OWNERS * CAP
MSG = RHS * CAP + 1
TALL = OWNERS * MSG
CHUNK = 8
UNROLL = 16
CHUNKS = COUNT // CHUNK

f32 = jnp.float32
bf16 = jnp.bfloat16


def diag_mask():
    sub = lax.broadcasted_iota(jnp.int32, (RHS, BS), 0)
    lane = lax.broadcasted_iota(jnp.int32, (RHS, BS), 1)
    return sub == lane


def row_of(column):
    return jnp.sum(jnp.where(diag_mask(), column, 0.0), axis=0, keepdims=True)


def column_of(row):
    spread = jnp.broadcast_to(row, (RHS, BS))
    total = jnp.sum(jnp.where(diag_mask(), spread, 0.0), axis=1, keepdims=True)
    return jnp.broadcast_to(total, (RHS, BS))


def squares(values):
    cube = values.reshape(values.shape[0] // RHS, RHS, BS)
    total = jnp.sum(jnp.sum(cube * cube, axis=0), axis=1, keepdims=True)
    return jnp.broadcast_to(total, (RHS, BS))


def tiled(column, count):
    return jnp.concatenate([column] * count, axis=0)


def sum_rows(ref):
    rows = [ref[pl.ds(MSG * o + MSG - 1, 1), :] for o in range(OWNERS)]
    while len(rows) > 1:
        rows = [rows[i] + rows[i + 1] for i in range(0, len(rows), 2)]
    return column_of(rows[0])


def put_rows(ref, row):
    for o in range(OWNERS):
        ref[pl.ds(MSG * o + MSG - 1, 1), :] = row


def split(x):
    high = x.astype(bf16)
    low = (x - high.astype(f32)).astype(bf16)
    return high, low


def stacked(x):
    high = x.astype(bf16).astype(f32)
    both = jnp.concatenate([high, x - high], axis=0).astype(bf16)
    return jnp.concatenate([both, both], axis=1)


def fold(out):
    first = out[0:8, 0:BS] + out[8:16, 0:BS]
    second = out[16:24, BS:] + out[24:32, BS:]
    return first, second


def chunk_copy(blocks, bbuf, sem, c):
    span = pl.ds(c * CHUNK, CHUNK)
    return pltpu.make_async_copy(blocks.at[span], bbuf.at[span], sem.at[c])


def split_left(us, left):
    for r in range(ROWS):
        us[r] = stacked(left[r * RHS : (r + 1) * RHS])


def adjoint_pair(k, tab, us, h0, l0, h1, l1, msg):
    lhs = jnp.concatenate([us[tab[COUNT + k]], us[tab[COUNT + k + 1]]], axis=0)
    rhs = jnp.concatenate(
        [jnp.concatenate([h0, l0], axis=0), jnp.concatenate([h1, l1], axis=0)], axis=1
    )
    out = lax.dot_general(lhs, rhs, (((1,), (0,)), ((), ())), preferred_element_type=f32)
    first, second = fold(out)
    msg[pl.ds(tab[k], RHS), :] = first
    msg[pl.ds(tab[k + 1], RHS), :] = second


def first_kernel(
    owner_in, row_in, col_in, right_in, blocks,
    msg, tab, high, low,
    bbuf, right, us, owner, row, col, taken, sem, small,
):
    loads = [
        pltpu.make_async_copy(owner_in, owner, small.at[0]),
        pltpu.make_async_copy(row_in, row, small.at[1]),
        pltpu.make_async_copy(col_in, col, small.at[2]),
        pltpu.make_async_copy(right_in, right, small.at[3]),
    ]
    for load in loads:
        load.start()

    def begin(c, carry):
        chunk_copy(blocks, bbuf, sem, c).start()
        return carry

    lax.fori_loop(0, CHUNKS, begin, 0)
    msg[...] = jnp.zeros((TALL, BS), f32)

    def clear(g, carry):
        for j in range(8):
            taken[g * 8 + j] = 0
        return carry

    lax.fori_loop(0, OWNERS // 8, clear, 0)
    for load in loads:
        load.wait()
    right_all = right[...]
    put_rows(msg, row_of(squares(right_all)))
    split_left(us, right_all)
    lane = lax.broadcasted_iota(jnp.int32, (1, BS), 1)

    def place(g, carry):
        for j in range(4):
            k = g * 4 + j
            o = owner[k]
            rank = taken[o]
            taken[o] = rank + 1
            tab[k] = o * MSG + rank * RHS
            tab[COUNT + k] = lax.rem(row[k], ROWS)
            span = pl.ds(o * MSG + MSG - 1, 1)
            msg[span, :] = jnp.where(lane == RHS + rank, col[k].astype(f32), msg[span, :])
        return carry

    lax.fori_loop(0, COUNT // 4, place, 0)

    def chunk(c, carry):
        chunk_copy(blocks, bbuf, sem, c).wait()
        for j in range(0, CHUNK, 2):
            k = c * CHUNK + j
            h0, l0 = split(bbuf[k])
            h1, l1 = split(bbuf[k + 1])
            high[k] = h0
            low[k] = l0
            high[k + 1] = h1
            low[k + 1] = l1
            adjoint_pair(k, tab, us, h0, l0, h1, l1, msg)
        return carry

    lax.fori_loop(0, CHUNKS, chunk, 0)


def forward_part(tab_in, inc, uraw, nleft, high, low, lraw, other, tab, sem):
    copy = pltpu.make_async_copy(tab_in, tab, sem)
    copy.start()
    norm_right = jnp.sqrt(sum_rows(inc))
    lraw[...] = jnp.zeros((ROWS * RHS, BS), f32)
    other[...] = jnp.zeros((ROWS * RHS, BS), f32)
    copy.wait()

    def chunk(c, carry):
        for j in range(0, UNROLL, 2):
            k = c * UNROLL + j
            lhs = jnp.concatenate(
                [stacked(inc[pl.ds(tab[k], RHS), :]), stacked(inc[pl.ds(tab[k + 1], RHS), :])],
                axis=0,
            )
            rhs = jnp.concatenate(
                [
                    jnp.concatenate([high[k], low[k]], axis=1),
                    jnp.concatenate([high[k + 1], low[k + 1]], axis=1),
                ],
                axis=0,
            )
            out = lax.dot_general(lhs, rhs, (((1,), (1,)), ((), ())), preferred_element_type=f32)
            first, second = fold(out)
            span = pl.ds(pl.multiple_of(tab[COUNT + k] * RHS, RHS), RHS)
            lraw[span, :] = lraw[span, :] + first
            span = pl.ds(pl.multiple_of(tab[COUNT + k + 1] * RHS, RHS), RHS)
            other[span, :] = other[span, :] + second
        return carry

    lax.fori_loop(0, COUNT // UNROLL, chunk, 0)
    image = lraw[...] + other[...]
    left = image / tiled(norm_right, ROWS) - tiled(norm_right, ROWS) * (
        uraw[...] / tiled(nleft[...], ROWS)
    )
    lraw[...] = left
    return left, norm_right


def user_kernel(tab_in, inc, uraw, nleft, high, low, msg, lraw, nright, other, us, tab, sem):
    left, norm_right = forward_part(
        tab_in, inc, uraw, nleft, high, low, lraw, other, tab, sem
    )
    nright[...] = norm_right
    msg[...] = jnp.zeros((TALL, BS), f32)
    put_rows(msg, row_of(squares(left)))
    split_left(us, left)

    def chunk(c, carry):
        for j in range(0, UNROLL, 2):
            k = c * UNROLL + j
            adjoint_pair(k, tab, us, high[k], low[k], high[k + 1], low[k + 1], msg)
        return carry

    lax.fori_loop(0, COUNT // UNROLL, chunk, 0)


def last_user_kernel(tab_in, inc, uraw, nleft, high, low, msg, lraw, nright, other, tab, sem):
    left, norm_right = forward_part(
        tab_in, inc, uraw, nleft, high, low, lraw, other, tab, sem
    )
    nright[...] = norm_right
    msg[...] = jnp.broadcast_to(row_of(squares(left)), msg.shape)


def gather_slots(inc, cols_of, half, parts, copy):
    copy.start()
    half[pl.ds(COLS_OWN * RHS, RHS), :] = sum_rows(inc)
    for part in parts:
        part[...] = jnp.zeros((COLS_OWN * RHS, BS), f32)
    copy.wait()

    def step(g, carry):
        for j in range(8):
            o = g * 8 + j
            for s in range(CAP):
                c = cols_of(o, s)
                span = pl.ds(pl.multiple_of(c * RHS, RHS), RHS)
                part = parts[(2 * j + s) % len(parts)]
                part[span, :] = part[span, :] + inc[pl.ds(o * MSG + s * RHS, RHS), :]
        return carry

    lax.fori_loop(0, OWNERS // 8, step, 0)
    half[pl.ds(0, COLS_OWN * RHS), :] = (parts[0][...] + parts[1][...]) + (
        parts[2][...] + parts[3][...]
    )


def first_owner_kernel(inc, half, cols, p0, p1, p2, p3, vcols, scols, sem):
    for o in range(OWNERS):
        vcols[pl.ds(o, 1), :] = inc[pl.ds(MSG * o + MSG - 1, 1), :].astype(jnp.int32)
    copy = pltpu.make_async_copy(vcols, scols, sem)

    def cols_of(o, s):
        c = scols[o, RHS + s]
        cols[o * CAP + s] = c
        return c

    gather_slots(inc, cols_of, half, (p0, p1, p2, p3), copy)


def owner_kernel(cols_in, inc, half, p0, p1, p2, p3, cols, sem):
    copy = pltpu.make_async_copy(cols_in, cols, sem)
    gather_slots(inc, lambda o, s: cols[o * CAP + s], half, (p0, p1, p2, p3), copy)


def send_slots(cols, raw, msg, copy):
    put_rows(msg, row_of(squares(raw[...])))
    copy.wait()

    def step(g, carry):
        for j in range(8):
            o = g * 8 + j
            for s in range(CAP):
                c = cols[o * CAP + s]
                span = pl.ds(pl.multiple_of(c * RHS, RHS), RHS)
                msg[pl.ds(o * MSG + s * RHS, RHS), :] = raw[span, :]
        return carry

    lax.fori_loop(0, OWNERS // 8, step, 0)


def first_send_kernel(cols_in, mine, theirs, msg, raw, nleft, cols, sem):
    copy = pltpu.make_async_copy(cols_in, cols, sem)
    copy.start()
    norm_left = jnp.sqrt(mine[pl.ds(COLS_OWN * RHS, RHS), :] + theirs[pl.ds(COLS_OWN * RHS, RHS), :])
    nleft[...] = norm_left
    body = pl.ds(0, COLS_OWN * RHS)
    raw[...] = (mine[body, :] + theirs[body, :]) / tiled(norm_left, COLS_OWN)
    send_slots(cols, raw, msg, copy)


def send_kernel(first, cols_in, mine, theirs, qprev, nright, *refs):
    cols, sem = refs[-2:]
    copy = pltpu.make_async_copy(cols_in, cols, sem)
    copy.start()
    if first:
        start, msg, raw, nleft, sol, search, scal = refs[:-2]
    else:
        sol_in, search_in, scal_in, msg, raw, nleft, sol, search, scal = refs[:-2]
    n = COLS_OWN
    norm_left = jnp.sqrt(mine[pl.ds(n * RHS, RHS), :] + theirs[pl.ds(n * RHS, RHS), :])
    norm_right = nright[...]
    nleft[...] = norm_left
    body = pl.ds(0, n * RHS)
    vec = qprev[...] / tiled(norm_right, n)
    raw[...] = (mine[body, :] + theirs[body, :]) / tiled(norm_left, n) - tiled(norm_left, n) * vec
    send_slots(cols, raw, msg, copy)
    if first:
        old_search = vec
        diag_bar = norm_right
        residual = start[...]
        old_sol = jnp.zeros((n * RHS, BS), f32)
    else:
        radius = scal_in[pl.ds(0, RHS), :]
        cosine = scal_in[pl.ds(RHS, RHS), :]
        sine_term = scal_in[pl.ds(2 * RHS, RHS), :]
        residual = scal_in[pl.ds(3 * RHS, RHS), :]
        coupling = sine_term * norm_right
        old_search = vec - tiled(coupling / radius, n) * search_in[...]
        diag_bar = -cosine * norm_right
        old_sol = sol_in[...]
    radius = jnp.sqrt(diag_bar * diag_bar + norm_left * norm_left)
    cosine = diag_bar / radius
    sine_term = norm_left / radius
    sol[...] = old_sol + tiled(cosine * residual / radius, n) * old_search
    search[...] = old_search
    scal[pl.ds(0, RHS), :] = radius
    scal[pl.ds(RHS, RHS), :] = cosine
    scal[pl.ds(2 * RHS, RHS), :] = sine_term
    scal[pl.ds(3 * RHS, RHS), :] = sine_term * residual


def final_kernel(rows, lraw, qprev, nright, sol_in, search_in, scal_in, start, sol, left, rel):
    n = COLS_OWN
    norm_left = jnp.sqrt(column_of(jnp.sum(rows[...], axis=0, keepdims=True)))
    norm_right = nright[...]
    left[...] = lraw[...] / tiled(norm_left, ROWS)
    radius = scal_in[pl.ds(0, RHS), :]
    cosine = scal_in[pl.ds(RHS, RHS), :]
    sine_term = scal_in[pl.ds(2 * RHS, RHS), :]
    residual = scal_in[pl.ds(3 * RHS, RHS), :]
    vec = qprev[...] / tiled(norm_right, n)
    search = vec - tiled(sine_term * norm_right / radius, n) * search_in[...]
    diag_bar = -cosine * norm_right
    radius = jnp.sqrt(diag_bar * diag_bar + norm_left * norm_left)
    cosine = diag_bar / radius
    sine_term = norm_left / radius
    sol[...] = sol_in[...] + tiled(cosine * residual / radius, n) * search
    rel[...] = row_of(sine_term * residual / start[...])[0, :RHS]


def shape(*dims, dtype=f32):
    return jax.ShapeDtypeStruct(dims, dtype)


VMEM = pl.BlockSpec(memory_space=pltpu.VMEM)
SMEM = pl.BlockSpec(memory_space=pltpu.SMEM)
HBM = pl.BlockSpec(memory_space=pltpu.HBM)
ANY = pl.BlockSpec(memory_space=pl.ANY)
PARTS = [pltpu.VMEM((COLS_OWN * RHS, BS), f32)] * 4
LEFTS = pltpu.VMEM((ROWS, 2 * RHS, 2 * BS), bf16)
LEFT = pltpu.VMEM((ROWS * RHS, BS), f32)
ONE = pltpu.SemaphoreType.DMA(())
TABLE = [pltpu.SMEM((SLOTS,), jnp.int32), ONE]


def call(body, ins, outs, specs_out=None, scratch=()):
    return pl.pallas_call(
        body,
        out_shape=outs,
        in_specs=ins,
        out_specs=specs_out or jax.tree.map(lambda _: VMEM, outs),
        scratch_shapes=scratch,
        compiler_params=pltpu.CompilerParams(vmem_limit_bytes=24 * 1024 * 1024),
    )


def exchange(msg):
    sent = msg.reshape(OWNERS, MSG * BS)
    return lax.all_to_all(sent, SHARD, 0, 0, tiled=True).reshape(TALL, BS)


def swap(half):
    return lax.ppermute(half, "grp", [(0, 1), (1, 0)])


def on_device(blocks, block_row, block_owner, block_col, right_side):
    owner = block_owner[:, 0]
    right = right_side.reshape(ROWS, BS, RHS).transpose(0, 2, 1).reshape(ROWS * RHS, BS)
    vec = shape(COLS_OWN * RHS, BS)
    col8 = shape(RHS, BS)
    msg_shape = shape(TALL, BS)
    half_shape = shape(COLS_OWN * RHS + RHS, BS)
    table = shape(SLOTS, dtype=jnp.int32)
    halves = shape(COUNT, BS, BS, dtype=bf16)

    msg, tab, high, low = call(
        first_kernel,
        [HBM] * 5,
        (msg_shape, table, halves, halves),
        (VMEM, SMEM, VMEM, VMEM),
        [pltpu.VMEM((COUNT, BS, BS), f32), LEFT, LEFTS]
        + [pltpu.SMEM((COUNT,), jnp.int32)] * 4
        + [pltpu.SemaphoreType.DMA((CHUNKS,)), pltpu.SemaphoreType.DMA((4,))],
    )(owner, block_row, block_col, right, blocks)
    inc = exchange(msg)
    half, cols = call(
        first_owner_kernel,
        [VMEM],
        (half_shape, table),
        (VMEM, SMEM),
        PARTS + [pltpu.VMEM((OWNERS, BS), jnp.int32), pltpu.SMEM((OWNERS, BS), jnp.int32), ONE],
    )(inc)
    msg, raw, norm_left = call(
        first_send_kernel, [ANY, VMEM, VMEM], (msg_shape, vec, col8), None, TABLE
    )(cols, half, swap(half))
    start = norm_left
    left = right
    state = None
    for repeat in range(ITERS):
        inc = exchange(msg)
        if repeat == ITERS - 1:
            break
        msg, left, norm_right = call(
            user_kernel,
            [ANY] + [VMEM] * 5,
            (msg_shape, vec, col8),
            None,
            [LEFT, LEFTS] + TABLE,
        )(tab, inc, left, norm_left, high, low)
        inc = exchange(msg)
        half = call(owner_kernel, [ANY, VMEM], half_shape, None, PARTS + TABLE)(cols, inc)
        first = repeat == 0
        tail = (start,) if first else state
        outs = call(
            lambda *refs, first=first: send_kernel(first, *refs),
            [ANY] + [VMEM] * (4 + len(tail)),
            (msg_shape, vec, col8, vec, vec, shape(4 * RHS, BS)),
            None,
            TABLE,
        )(cols, half, swap(half), raw, norm_right, *tail)
        msg, raw, norm_left = outs[:3]
        state = outs[3:]
    rows, left, norm_right = call(
        last_user_kernel,
        [ANY] + [VMEM] * 5,
        (shape(2 * OWNERS, BS), vec, col8),
        None,
        [LEFT] + TABLE,
    )(tab, inc, left, norm_left, high, low)
    rows = lax.all_to_all(rows, GRP_SHARD, 0, 0, tiled=True)
    sol, left, rel = call(
        final_kernel, [VMEM] * 8, (vec, vec, shape(RHS))
    )(rows, left, raw, norm_right, *state, start)

    def tall(x):
        return x.reshape(COLS_OWN, RHS, BS).transpose(0, 2, 1).reshape(COLS_OWN * BS, RHS)

    return tall(sol), tall(left), rel


def solution(mesh):
    torus = Mesh(
        mesh.devices.reshape(mesh.shape["grp"], 4, 4, 4), ("grp", "shard_0", "shard_1", "shard_2")
    )
    return jax.shard_map(
        on_device,
        mesh=torus,
        in_specs=(
            P(GRP_SHARD, None, None),
            P(GRP_SHARD),
            P(GRP_SHARD, None),
            P(GRP_SHARD),
            P(GRP_SHARD, None),
        ),
        out_specs=(P(SHARD, None), P(GRP_SHARD, None), P()),
        check_vma=False,
    )
```

time: 208 us -> 201 us (0.966)
  Pallas kernels: 31.8 us -> 24.9 us
    pallas_call x14, Pallas kernels: 31.8 us -> 24.9 us  [the longest x3 10.8 us: on_device(): call(user_kernel, [ANY] + [VMEM] * 5, (msg_shape, vec, col8), None, [LEFT...]
where the time goes in v2:
time: 201 us; the launch traced here: 200 us
  blocking collectives  164 us (82%)
  Pallas kernels  24.9 us (12%)
  local copies, waits for them, and re-layouts  4.99 us (2%)
  waiting for transfers between devices  4.99 us (2%)
    all_to_all x8, blocking collectives, exchange(): return lax.all_to_all(sent, SHARD, 0, 0, tiled=True).reshape(TALL, BS)  151 us
    all_to_all x1, blocking collectives, on_device(): rows = lax.all_to_all(rows, GRP_SHARD, 0, 0, tiled=True)  13.3 us
    pallas_call x3, Pallas kernels, on_device(): call(user_kernel, [ANY] + [VMEM] * 5, (msg_shape, vec, col8), None, [LEFT...  10.8 us
    unnamed x12, local copies, waits for them, and re-layouts  4.99 us
    ppermute x4, waiting for transfers between devices, swap(): return lax.ppermute(half, 'grp', [(0, 1), (1, 0)])  4.99 us
  transfers between devices with their start and end apart: 4, of which 4 were waited for; matrix products, arithmetic and copies ran while one was open for 0% of the time, Pallas kernels for 0%

profile of v2, /device:TPU:0, one launch (start us, length us, event | category | flops | bytes accessed | tf_op | source)
XLA Modules:
  0.0 200.2 jit_solution(3171775416940493448)
XLA Ops:
  0.6 0.0 copy-start
  0.6 2.2 %copy-done = f32[64,128,128]{2,1,0:T(8,128)S(1)} copy-done((f32[64,128,128]{2,1,0:T(8,128)S(1)}, f32[64,128,128]{2,1,0:T(8,128)}, u32[]{:S(2)}) %copy-start) | copy-done | bytes 4194328
  2.8 0.0 copy-start.1
  2.8 0.8 copy-done.1
  3.7 0.0 copy-start.3
  3.7 0.7 copy-done.3
  4.3 0.0 copy-start.4
  4.3 0.7 copy-done.4
  5.0 0.0 copy-start.5
  5.0 0.7 copy-done.5
  5.6 3.6 %shard_map.76 = (f32[1088,128]{1,0:T(8,128)S(1)}, s32[128]{0:T(128)S(1)}, bf16[64,128,128]{2,1,0:T(8,128)(2,1)S(1)}, bf16[64,128,128]{2,1,0:T(8,128)(2,1)S(1)}) custom-call(s32[64]{0:T(128)S(1)} %bitcast.56, s32[64]{0:T(128)S(1)} %copy-done.4, s32[64]{0:T(128)S(1)} %copy-done.5, f32[128,128]{1,0:T(8,128)S(1)} %bitcast.52, f32[64,128,128]{2,1,0:T(8,128)S(1)} %copy-done), custom_call_target="tpu_custom_call" | custom-call | tf_op jit(solution)/shard_map/pallas_call | solution.py:409
  9.2 0.0 copy-start.2
  9.2 25.3 %all_to_all.83 = f32[64,1,2176]{2,1,0:T(1,128)S(1)} all-to-all(f32[64,1,2176]{2,1,0:T(1,128)S(1)} %bitcast.50), channel_id=1, replica_groups=mesh['grp'=2,'shard_0'=4,'shard_1'=4,'shard_2'=4] {'shard_0','shard_1','..., dimensions={0} | all-to-all | bytes 1114112 | tf_op jit(solution)/shard_map/all_to_all | solution.py:392
  34.5 2.0 shard_map.77
  36.4 0.1 collective-permute-start
  36.5 1.2 collective-permute-done.theirs
  37.8 0.7 shard_map.78
  38.5 18.5 %all_to_all.84 = f32[64,1,2176]{2,1,0:T(1,128)S(1)} all-to-all(f32[64,1,2176]{2,1,0:T(1,128)S(1)} %bitcast.49), channel_id=1, replica_groups=mesh['grp'=2,'shard_0'=4,'shard_1'=4,'shard_2'=4] {'shard_0','shard_1','..., dimensions={0} | all-to-all | bytes 1114112 | tf_op jit(solution)/shard_map/all_to_all | solution.py:392
  57.0 0.0 copy-done.2
  57.1 3.6 %shard_map.79 = (f32[1088,128]{1,0:T(8,128)S(1)}, f32[128,128]{1,0:T(8,128)S(1)}, f32[8,128]{1,0:T(8,128)S(1)}) custom-call(s32[128]{0:T(128)S(1)} %get-tuple-element.45.tab_in, f32[1088,128]{1,0:T(8,128)S(1)} %bitcast.39, f32[128,128]{1,0:T(8,128)S(1)} %bitcast.53, f32[8,128]{1,0:T(8,128)S(1)} %get-tuple-element.50.nleft.refs_5_.start, ...), custom_call_target="tpu_custom_call" | custom-call | tf_op jit(solution)/shard_map/pallas_call | solution.py:436
  60.7 17.1 %all_to_all.85 = f32[64,1,2176]{2,1,0:T(1,128)S(1)} all-to-all(f32[64,1,2176]{2,1,0:T(1,128)S(1)} %bitcast.51), channel_id=1, replica_groups=mesh['grp'=2,'shard_0'=4,'shard_1'=4,'shard_2'=4] {'shard_0','shard_1','..., dimensions={0} | all-to-all | bytes 1114112 | tf_op jit(solution)/shard_map/all_to_all | solution.py:392
  77.8 0.8 shard_map.80.refs_1_
  78.6 0.1 collective-permute-start.1
  78.7 1.2 collective-permute-done.1.refs_2_
  80.0 0.8 shard_map.81
  80.7 18.5 %all_to_all.86 = f32[64,1,2176]{2,1,0:T(1,128)S(1)} all-to-all(f32[64,1,2176]{2,1,0:T(1,128)S(1)} %bitcast.46), channel_id=1, replica_groups=mesh['grp'=2,'shard_0'=4,'shard_1'=4,'shard_2'=4] {'shard_0','shard_1','..., dimensions={0} | all-to-all | bytes 1114112 | tf_op jit(solution)/shard_map/all_to_all | solution.py:392
  99.3 3.6 %shard_map.82 = (f32[1088,128]{1,0:T(8,128)S(1)}, f32[128,128]{1,0:T(8,128)S(1)}, f32[8,128]{1,0:T(8,128)S(1)}) custom-call(s32[128]{0:T(128)S(1)} %get-tuple-element.45.tab_in, f32[1088,128]{1,0:T(8,128)S(1)} %bitcast.37, f32[128,128]{1,0:T(8,128)S(1)} %get-tuple-element.57.uraw, f32[8,128]{1,0:T(8,128)S(1)} %get-tuple-element.58.nleft, ...), custom_call_target="tpu_custom_call" | custom-call | tf_op jit(solution)/shard_map/pallas_call | solution.py:436
  102.9 17.1 %all_to_all.87 = f32[64,1,2176]{2,1,0:T(1,128)S(1)} all-to-all(f32[64,1,2176]{2,1,0:T(1,128)S(1)} %bitcast.47), channel_id=1, replica_groups=mesh['grp'=2,'shard_0'=4,'shard_1'=4,'shard_2'=4] {'shard_0','shard_1','..., dimensions={0} | all-to-all | bytes 1114112 | tf_op jit(solution)/shard_map/all_to_all | solution.py:392
  120.0 0.8 shard_map.83.refs_1_
  120.8 0.1 collective-permute-start.2
  120.9 1.2 collective-permute-done.2.refs_2_
  122.2 0.7 shard_map.84
  122.9 18.5 %all_to_all.88 = f32[64,1,2176]{2,1,0:T(1,128)S(1)} all-to-all(f32[64,1,2176]{2,1,0:T(1,128)S(1)} %bitcast.45), channel_id=1, replica_groups=mesh['grp'=2,'shard_0'=4,'shard_1'=4,'shard_2'=4] {'shard_0','shard_1','..., dimensions={0} | all-to-all | bytes 1114112 | tf_op jit(solution)/shard_map/all_to_all | solution.py:392
  141.5 3.6 %shard_map.85 = (f32[1088,128]{1,0:T(8,128)S(1)}, f32[128,128]{1,0:T(8,128)S(1)}, f32[8,128]{1,0:T(8,128)S(1)}) custom-call(s32[128]{0:T(128)S(1)} %get-tuple-element.45.tab_in, f32[1088,128]{1,0:T(8,128)S(1)} %bitcast.38, f32[128,128]{1,0:T(8,128)S(1)} %get-tuple-element.66.uraw, f32[8,128]{1,0:T(8,128)S(1)} %get-tuple-element.67.nleft, ...), custom_call_target="tpu_custom_call" | custom-call | tf_op jit(solution)/shard_map/pallas_call | solution.py:436
  145.1 17.1 %all_to_all.89 = f32[64,1,2176]{2,1,0:T(1,128)S(1)} all-to-all(f32[64,1,2176]{2,1,0:T(1,128)S(1)} %bitcast.48), channel_id=1, replica_groups=mesh['grp'=2,'shard_0'=4,'shard_1'=4,'shard_2'=4] {'shard_0','shard_1','..., dimensions={0} | all-to-all | bytes 1114112 | tf_op jit(solution)/shard_map/all_to_all | solution.py:392
  162.2 0.8 shard_map.86.refs_1_
  163.0 0.1 collective-permute-start.3
  163.1 1.2 collective-permute-done.3.refs_2_
  164.4 0.7 shard_map.87
  165.1 18.5 %all_to_all.90 = f32[64,1,2176]{2,1,0:T(1,128)S(1)} all-to-all(f32[64,1,2176]{2,1,0:T(1,128)S(1)} %bitcast.44), channel_id=1, replica_groups=mesh['grp'=2,'shard_0'=4,'shard_1'=4,'shard_2'=4] {'shard_0','shard_1','..., dimensions={0} | all-to-all | bytes 1114112 | tf_op jit(solution)/shard_map/all_to_all | solution.py:392
  183.7 2.4 %shard_map.88 = (f32[128,128]{1,0:T(8,128)S(1)}, f32[128,128]{1,0:T(8,128)S(1)}, f32[8,128]{1,0:T(8,128)S(1)}) custom-call(s32[128]{0:T(128)S(1)} %get-tuple-element.45.tab_in, f32[1088,128]{1,0:T(8,128)S(1)} %bitcast.36, f32[128,128]{1,0:T(8,128)S(1)} %get-tuple-element.75.uraw, f32[8,128]{1,0:T(8,128)S(1)} %get-tuple-element.76.nleft, ...), custom_call_target="tpu_custom_call" | custom-call | tf_op jit(solution)/shard_map/pallas_call | solution.py:456
  186.1 13.3 %all_to_all.91 = f32[128,1,128]{2,1,0:T(1,128)S(1)} all-to-all(f32[128,1,128]{2,1,0:T(1,128)S(1)} %bitcast.55), channel_id=1, replica_groups=mesh['grp'=2,'shard_0'=4,'shard_1'=4,'shard_2'=4] {'grp','shard_0','shar..., dimensions={0} | all-to-all | bytes 131072 | tf_op jit(solution)/shard_map/all_to_all | solution.py:463
  199.4 0.8 shard_map.89
Async XLA Ops:
  0.6 2.2 %copy-start = (f32[64,128,128]{2,1,0:T(8,128)S(1)}, f32[64,128,128]{2,1,0:T(8,128)}, u32[]{:S(2)}) copy-start(f32[64,128,128]{2,1,0:T(8,128)} %blocks.1) | copy-start | bytes 12582916
  2.8 0.8 copy-start.1
  3.7 0.7 copy-start.3
  4.3 0.7 copy-start.4
  5.0 0.7 copy-start.5
  9.2 47.9 %copy-start.2 = (f32[2048,8]{0,1:T(8,128)S(1)}, f32[2048,8]{0,1:T(8,128)}, u32[]{:S(2)}) copy-start(f32[2048,8]{0,1:T(8,128)} %param.9) | copy-start | bytes 196612
  36.4 1.3 collective-permute-start
  78.6 1.3 collective-permute-start.1
  120.8 1.3 collective-permute-start.2
  163.0 1.3 collective-permute-start.3

commit v3 on v2

--- a/solution.py
+++ b/solution.py
@@ -108,13 +108,13 @@
 def first_kernel(
     owner_in, row_in, col_in, right_in, blocks,
     msg, tab, high, low,
-    bbuf, right, us, owner, row, col, taken, sem, small,
+    bbuf, right, us, owner, row, col, taken, sem, little,
 ):
     loads = [
-        pltpu.make_async_copy(owner_in, owner, small.at[0]),
-        pltpu.make_async_copy(row_in, row, small.at[1]),
-        pltpu.make_async_copy(col_in, col, small.at[2]),
-        pltpu.make_async_copy(right_in, right, small.at[3]),
+        pltpu.make_async_copy(owner_in, owner, little.at[0]),
+        pltpu.make_async_copy(row_in, row, little.at[1]),
+        pltpu.make_async_copy(col_in, col, little.at[2]),
+        pltpu.make_async_copy(right_in, right, little.at[3]),
     ]
     for load in loads:
         load.start()
@@ -169,13 +169,10 @@
     lax.fori_loop(0, CHUNKS, chunk, 0)
 
 
-def forward_part(tab_in, inc, uraw, nleft, high, low, lraw, other, tab, sem):
-    copy = pltpu.make_async_copy(tab_in, tab, sem)
-    copy.start()
+def forward_part(tab, inc, uraw, nleft, high, low, lraw, other):
     norm_right = jnp.sqrt(sum_rows(inc))
     lraw[...] = jnp.zeros((ROWS * RHS, BS), f32)
     other[...] = jnp.zeros((ROWS * RHS, BS), f32)
-    copy.wait()
 
     def chunk(c, carry):
         for j in range(0, UNROLL, 2):
@@ -208,10 +205,8 @@
     return left, norm_right
 
 
-def user_kernel(tab_in, inc, uraw, nleft, high, low, msg, lraw, nright, other, us, tab, sem):
-    left, norm_right = forward_part(
-        tab_in, inc, uraw, nleft, high, low, lraw, other, tab, sem
-    )
+def user_kernel(tab, inc, uraw, nleft, high, low, msg, lraw, nright, other, us):
+    left, norm_right = forward_part(tab, inc, uraw, nleft, high, low, lraw, other)
     nright[...] = norm_right
     msg[...] = jnp.zeros((TALL, BS), f32)
     put_rows(msg, row_of(squares(left)))
@@ -226,20 +221,20 @@
     lax.fori_loop(0, COUNT // UNROLL, chunk, 0)
 
 
-def last_user_kernel(tab_in, inc, uraw, nleft, high, low, msg, lraw, nright, other, tab, sem):
-    left, norm_right = forward_part(
-        tab_in, inc, uraw, nleft, high, low, lraw, other, tab, sem
-    )
+def last_user_kernel(tab, inc, uraw, nleft, high, low, msg, lraw, nright, other):
+    left, norm_right = forward_part(tab, inc, uraw, nleft, high, low, lraw, other)
     nright[...] = norm_right
     msg[...] = jnp.broadcast_to(row_of(squares(left)), msg.shape)
 
 
-def gather_slots(inc, cols_of, half, parts, copy):
-    copy.start()
+def gather_slots(inc, cols_of, half, parts, copy=None):
+    if copy is not None:
+        copy.start()
     half[pl.ds(COLS_OWN * RHS, RHS), :] = sum_rows(inc)
     for part in parts:
         part[...] = jnp.zeros((COLS_OWN * RHS, BS), f32)
-    copy.wait()
+    if copy is not None:
+        copy.wait()
 
     def step(g, carry):
         for j in range(8):
@@ -270,14 +265,12 @@
     gather_slots(inc, cols_of, half, (p0, p1, p2, p3), copy)
 
 
-def owner_kernel(cols_in, inc, half, p0, p1, p2, p3, cols, sem):
-    copy = pltpu.make_async_copy(cols_in, cols, sem)
-    gather_slots(inc, lambda o, s: cols[o * CAP + s], half, (p0, p1, p2, p3), copy)
-
-
-def send_slots(cols, raw, msg, copy):
+def owner_kernel(cols, inc, half, p0, p1, p2, p3):
+    gather_slots(inc, lambda o, s: cols[o * CAP + s], half, (p0, p1, p2, p3))
+
+
+def send_slots(cols, raw, msg):
     put_rows(msg, row_of(squares(raw[...])))
-    copy.wait()
 
     def step(g, carry):
         for j in range(8):
@@ -291,24 +284,19 @@
     lax.fori_loop(0, OWNERS // 8, step, 0)
 
 
-def first_send_kernel(cols_in, mine, theirs, msg, raw, nleft, cols, sem):
-    copy = pltpu.make_async_copy(cols_in, cols, sem)
-    copy.start()
+def first_send_kernel(cols, mine, theirs, msg, raw, nleft):
     norm_left = jnp.sqrt(mine[pl.ds(COLS_OWN * RHS, RHS), :] + theirs[pl.ds(COLS_OWN * RHS, RHS), :])
     nleft[...] = norm_left
     body = pl.ds(0, COLS_OWN * RHS)
     raw[...] = (mine[body, :] + theirs[body, :]) / tiled(norm_left, COLS_OWN)
-    send_slots(cols, raw, msg, copy)
-
-
-def send_kernel(first, cols_in, mine, theirs, qprev, nright, *refs):
-    cols, sem = refs[-2:]
-    copy = pltpu.make_async_copy(cols_in, cols, sem)
-    copy.start()
+    send_slots(cols, raw, msg)
+
+
+def send_kernel(first, cols, mine, theirs, qprev, nright, *refs):
     if first:
-        start, msg, raw, nleft, sol, search, scal = refs[:-2]
+        start, msg, raw, nleft, sol, search, scal = refs
     else:
-        sol_in, search_in, scal_in, msg, raw, nleft, sol, search, scal = refs[:-2]
+        sol_in, search_in, scal_in, msg, raw, nleft, sol, search, scal = refs
     n = COLS_OWN
     norm_left = jnp.sqrt(mine[pl.ds(n * RHS, RHS), :] + theirs[pl.ds(n * RHS, RHS), :])
     norm_right = nright[...]
@@ -316,7 +304,7 @@
     body = pl.ds(0, n * RHS)
     vec = qprev[...] / tiled(norm_right, n)
     raw[...] = (mine[body, :] + theirs[body, :]) / tiled(norm_left, n) - tiled(norm_left, n) * vec
-    send_slots(cols, raw, msg, copy)
+    send_slots(cols, raw, msg)
     if first:
         old_search = vec
         diag_bar = norm_right
@@ -373,7 +361,6 @@
 LEFTS = pltpu.VMEM((ROWS, 2 * RHS, 2 * BS), bf16)
 LEFT = pltpu.VMEM((ROWS * RHS, BS), f32)
 ONE = pltpu.SemaphoreType.DMA(())
-TABLE = [pltpu.SMEM((SLOTS,), jnp.int32), ONE]
 
 
 def call(body, ins, outs, specs_out=None, scratch=()):
@@ -396,6 +383,10 @@
     return lax.ppermute(half, "grp", [(0, 1), (1, 0)])
 
 
+def small(x):
+    return pltpu.with_memory_space_constraint(x, pltpu.SMEM)
+
+
 def on_device(blocks, block_row, block_owner, block_col, right_side):
     owner = block_owner[:, 0]
     right = right_side.reshape(ROWS, BS, RHS).transpose(0, 2, 1).reshape(ROWS * RHS, BS)
@@ -403,7 +394,7 @@
     col8 = shape(RHS, BS)
     msg_shape = shape(TALL, BS)
     half_shape = shape(COLS_OWN * RHS + RHS, BS)
-    table = shape(SLOTS, dtype=jnp.int32)
+    table = pltpu.MemorySpace.SMEM((SLOTS,), jnp.int32)
     halves = shape(COUNT, BS, BS, dtype=bf16)
 
     msg, tab, high, low = call(
@@ -414,7 +405,7 @@
         [pltpu.VMEM((COUNT, BS, BS), f32), LEFT, LEFTS]
         + [pltpu.SMEM((COUNT,), jnp.int32)] * 4
         + [pltpu.SemaphoreType.DMA((CHUNKS,)), pltpu.SemaphoreType.DMA((4,))],
-    )(owner, block_row, block_col, right, blocks)
+    )(*(pltpu.with_memory_space_constraint(x, pltpu.HBM) for x in (owner, block_row, block_col, right, blocks)))
     inc = exchange(msg)
     half, cols = call(
         first_owner_kernel,
@@ -424,8 +415,8 @@
         PARTS + [pltpu.VMEM((OWNERS, BS), jnp.int32), pltpu.SMEM((OWNERS, BS), jnp.int32), ONE],
     )(inc)
     msg, raw, norm_left = call(
-        first_send_kernel, [ANY, VMEM, VMEM], (msg_shape, vec, col8), None, TABLE
-    )(cols, half, swap(half))
+        first_send_kernel, [SMEM, VMEM, VMEM], (msg_shape, vec, col8)
+    )(small(cols), half, swap(half))
     start = norm_left
     left = right
     state = None
@@ -435,31 +426,29 @@
             break
         msg, left, norm_right = call(
             user_kernel,
-            [ANY] + [VMEM] * 5,
+            [SMEM] + [VMEM] * 5,
             (msg_shape, vec, col8),
             None,
-            [LEFT, LEFTS] + TABLE,
-        )(tab, inc, left, norm_left, high, low)
+            [LEFT, LEFTS],
+        )(small(tab), inc, left, norm_left, high, low)
         inc = exchange(msg)
-        half = call(owner_kernel, [ANY, VMEM], half_shape, None, PARTS + TABLE)(cols, inc)
+        half = call(owner_kernel, [SMEM, VMEM], half_shape, None, PARTS)(small(cols), inc)
         first = repeat == 0
         tail = (start,) if first else state
         outs = call(
             lambda *refs, first=first: send_kernel(first, *refs),
-            [ANY] + [VMEM] * (4 + len(tail)),
+            [SMEM] + [VMEM] * (4 + len(tail)),
             (msg_shape, vec, col8, vec, vec, shape(4 * RHS, BS)),
-            None,
-            TABLE,
-        )(cols, half, swap(half), raw, norm_right, *tail)
+        )(small(cols), half, swap(half), raw, norm_right, *tail)
         msg, raw, norm_left = outs[:3]
         state = outs[3:]
     rows, left, norm_right = call(
         last_user_kernel,
-        [ANY] + [VMEM] * 5,
+        [SMEM] + [VMEM] * 5,
         (shape(2 * OWNERS, BS), vec, col8),
         None,
-        [LEFT] + TABLE,
-    )(tab, inc, left, norm_left, high, low)
+        [LEFT],
+    )(small(tab), inc, left, norm_left, high, low)
     rows = lax.all_to_all(rows, GRP_SHARD, 0, 0, tiled=True)
     sol, left, rel = call(
         final_kernel, [VMEM] * 8, (vec, vec, shape(RHS))

time: 201 us -> 190 us (0.945)
  Pallas kernels: 24.9 us -> 18.9 us
  local copies, waits for them, and re-layouts: 4.99 us -> 0.01 us
    pallas_call x11, Pallas kernels: 18.7 us -> 13.5 us  [the longest x3 9.25 us: on_device(): call(user_kernel, [SMEM] + [VMEM] * 5, (msg_shape, vec, col8), None, [LEF...]
    unnamed x12 -> x2, local copies, waits for them, and re-layouts: 4.99 us -> 0.01 us
where the time goes in v3:
time: 190 us; the launch traced here: 189 us
  blocking collectives  164 us (86%)
  Pallas kernels  18.9 us (10%)
  waiting for transfers between devices  4.99 us (3%)
    all_to_all x8, blocking collectives, exchange(): return lax.all_to_all(sent, SHARD, 0, 0, tiled=True).reshape(TALL, BS)  151 us
    all_to_all x1, blocking collectives, on_device(): rows = lax.all_to_all(rows, GRP_SHARD, 0, 0, tiled=True)  13.3 us
    pallas_call x3, Pallas kernels, on_device(): call(user_kernel, [SMEM] + [VMEM] * 5, (msg_shape, vec, col8), None, [LEF...  9.25 us
    ppermute x4, waiting for transfers between devices, swap(): return lax.ppermute(half, 'grp', [(0, 1), (1, 0)])  4.99 us
  transfers between devices with their start and end apart: 4, of which 4 were waited for; matrix products, arithmetic and copies ran while one was open for 0% of the time, Pallas kernels for 0%

profile of v3, /device:TPU:0, one launch (start us, length us, event | category | flops | bytes accessed | tf_op | source)
XLA Modules:
  0.0 189.0 jit_solution(11412495135983280587)
XLA Ops:
  0.6 3.3 %shard_map.76 = (f32[1088,128]{1,0:T(8,128)S(1)}, s32[128]{0:T(128)S(4)}, bf16[64,128,128]{2,1,0:T(8,128)(2,1)S(1)}, bf16[64,128,128]{2,1,0:T(8,128)(2,1)S(1)}) custom-call(s32[64]{0:T(128)} %bitcast.56, s32[64]{0:T(128)} %row_in.1, s32[64]{0:T(128)} %col_in.1, f32[128,128]{1,0:T(8,128)} %bitcast.52, f32[64,128,128]{2,1,0:T(8,128)} %blocks.1), custom_call_target="tpu_custom_call" | custom-call | tf_op jit(solution)/shard_map/pallas_call | solution.py:400
  3.9 0.0 copy-start
  4.0 25.3 %all_to_all.83 = f32[64,1,2176]{2,1,0:T(1,128)S(1)} all-to-all(f32[64,1,2176]{2,1,0:T(1,128)S(1)} %bitcast.50), channel_id=1, replica_groups=mesh['grp'=2,'shard_0'=4,'shard_1'=4,'shard_2'=4] {'shard_0','shard_1','..., dimensions={0} | all-to-all | bytes 1114112 | tf_op jit(solution)/shard_map/all_to_all | solution.py:379
  29.2 1.4 shard_map.77
  30.6 0.1 collective-permute-start
  30.7 1.2 collective-permute-done.theirs
  31.9 0.3 shard_map.78
  32.3 18.5 %all_to_all.84 = f32[64,1,2176]{2,1,0:T(1,128)S(1)} all-to-all(f32[64,1,2176]{2,1,0:T(1,128)S(1)} %bitcast.49), channel_id=1, replica_groups=mesh['grp'=2,'shard_0'=4,'shard_1'=4,'shard_2'=4] {'shard_0','shard_1','..., dimensions={0} | all-to-all | bytes 1114112 | tf_op jit(solution)/shard_map/all_to_all | solution.py:379
  50.8 0.0 copy-done
  50.8 3.1 %shard_map.79 = (f32[1088,128]{1,0:T(8,128)S(1)}, f32[128,128]{1,0:T(8,128)S(1)}, f32[8,128]{1,0:T(8,128)S(1)}) custom-call(s32[128]{0:T(128)S(4)} %get-tuple-element.45.tab, f32[1088,128]{1,0:T(8,128)S(1)} %bitcast.39, f32[128,128]{1,0:T(8,128)S(1)} %bitcast.53, f32[8,128]{1,0:T(8,128)S(1)} %get-tuple-element.50.nleft.refs_5_.start, ...), custom_call_target="tpu_custom_call" | custom-call | tf_op jit(solution)/shard_map/pallas_call | solution.py:427
  53.9 17.1 %all_to_all.85 = f32[64,1,2176]{2,1,0:T(1,128)S(1)} all-to-all(f32[64,1,2176]{2,1,0:T(1,128)S(1)} %bitcast.51), channel_id=1, replica_groups=mesh['grp'=2,'shard_0'=4,'shard_1'=4,'shard_2'=4] {'shard_0','shard_1','..., dimensions={0} | all-to-all | bytes 1114112 | tf_op jit(solution)/shard_map/all_to_all | solution.py:379
  71.0 0.3 shard_map.80.refs_1_
  71.4 0.1 collective-permute-start.1
  71.5 1.2 collective-permute-done.1.refs_2_
  72.7 0.3 shard_map.81
  73.0 18.5 %all_to_all.86 = f32[64,1,2176]{2,1,0:T(1,128)S(1)} all-to-all(f32[64,1,2176]{2,1,0:T(1,128)S(1)} %bitcast.46), channel_id=1, replica_groups=mesh['grp'=2,'shard_0'=4,'shard_1'=4,'shard_2'=4] {'shard_0','shard_1','..., dimensions={0} | all-to-all | bytes 1114112 | tf_op jit(solution)/shard_map/all_to_all | solution.py:379
  91.5 3.1 %shard_map.82 = (f32[1088,128]{1,0:T(8,128)S(1)}, f32[128,128]{1,0:T(8,128)S(1)}, f32[8,128]{1,0:T(8,128)S(1)}) custom-call(s32[128]{0:T(128)S(4)} %get-tuple-element.45.tab, f32[1088,128]{1,0:T(8,128)S(1)} %bitcast.37, f32[128,128]{1,0:T(8,128)S(1)} %get-tuple-element.57.uraw, f32[8,128]{1,0:T(8,128)S(1)} %get-tuple-element.58.nleft, ...), custom_call_target="tpu_custom_call" | custom-call | tf_op jit(solution)/shard_map/pallas_call | solution.py:427
  94.6 17.1 %all_to_all.87 = f32[64,1,2176]{2,1,0:T(1,128)S(1)} all-to-all(f32[64,1,2176]{2,1,0:T(1,128)S(1)} %bitcast.47), channel_id=1, replica_groups=mesh['grp'=2,'shard_0'=4,'shard_1'=4,'shard_2'=4] {'shard_0','shard_1','..., dimensions={0} | all-to-all | bytes 1114112 | tf_op jit(solution)/shard_map/all_to_all | solution.py:379
  111.7 0.3 shard_map.83.refs_1_
  112.1 0.1 collective-permute-start.2
  112.2 1.2 collective-permute-done.2.refs_2_
  113.4 0.3 shard_map.84
  113.8 18.5 %all_to_all.88 = f32[64,1,2176]{2,1,0:T(1,128)S(1)} all-to-all(f32[64,1,2176]{2,1,0:T(1,128)S(1)} %bitcast.45), channel_id=1, replica_groups=mesh['grp'=2,'shard_0'=4,'shard_1'=4,'shard_2'=4] {'shard_0','shard_1','..., dimensions={0} | all-to-all | bytes 1114112 | tf_op jit(solution)/shard_map/all_to_all | solution.py:379
  132.3 3.1 %shard_map.85 = (f32[1088,128]{1,0:T(8,128)S(1)}, f32[128,128]{1,0:T(8,128)S(1)}, f32[8,128]{1,0:T(8,128)S(1)}) custom-call(s32[128]{0:T(128)S(4)} %get-tuple-element.45.tab, f32[1088,128]{1,0:T(8,128)S(1)} %bitcast.38, f32[128,128]{1,0:T(8,128)S(1)} %get-tuple-element.66.uraw, f32[8,128]{1,0:T(8,128)S(1)} %get-tuple-element.67.nleft, ...), custom_call_target="tpu_custom_call" | custom-call | tf_op jit(solution)/shard_map/pallas_call | solution.py:427
  135.3 17.1 %all_to_all.89 = f32[64,1,2176]{2,1,0:T(1,128)S(1)} all-to-all(f32[64,1,2176]{2,1,0:T(1,128)S(1)} %bitcast.48), channel_id=1, replica_groups=mesh['grp'=2,'shard_0'=4,'shard_1'=4,'shard_2'=4] {'shard_0','shard_1','..., dimensions={0} | all-to-all | bytes 1114112 | tf_op jit(solution)/shard_map/all_to_all | solution.py:379
  152.5 0.3 shard_map.86.refs_1_
  152.8 0.1 collective-permute-start.3
  152.9 1.2 collective-permute-done.3.refs_2_
  154.2 0.3 shard_map.87
  154.5 18.5 %all_to_all.90 = f32[64,1,2176]{2,1,0:T(1,128)S(1)} all-to-all(f32[64,1,2176]{2,1,0:T(1,128)S(1)} %bitcast.44), channel_id=1, replica_groups=mesh['grp'=2,'shard_0'=4,'shard_1'=4,'shard_2'=4] {'shard_0','shard_1','..., dimensions={0} | all-to-all | bytes 1114112 | tf_op jit(solution)/shard_map/all_to_all | solution.py:379
  173.0 1.9 %shard_map.88 = (f32[128,128]{1,0:T(8,128)S(1)}, f32[128,128]{1,0:T(8,128)S(1)}, f32[8,128]{1,0:T(8,128)S(1)}) custom-call(s32[128]{0:T(128)S(4)} %get-tuple-element.45.tab, f32[1088,128]{1,0:T(8,128)S(1)} %bitcast.36, f32[128,128]{1,0:T(8,128)S(1)} %get-tuple-element.75.uraw, f32[8,128]{1,0:T(8,128)S(1)} %get-tuple-element.76.nleft, ...), custom_call_target="tpu_custom_call" | custom-call | tf_op jit(solution)/shard_map/pallas_call | solution.py:445
  174.9 13.3 %all_to_all.91 = f32[128,1,128]{2,1,0:T(1,128)S(1)} all-to-all(f32[128,1,128]{2,1,0:T(1,128)S(1)} %bitcast.55), channel_id=1, replica_groups=mesh['grp'=2,'shard_0'=4,'shard_1'=4,'shard_2'=4] {'grp','shard_0','shar..., dimensions={0} | all-to-all | bytes 131072 | tf_op jit(solution)/shard_map/all_to_all | solution.py:452
  188.2 0.8 shard_map.89
Async XLA Ops:
  3.9 46.9 %copy-start = (f32[2048,8]{0,1:T(8,128)S(1)}, f32[2048,8]{0,1:T(8,128)}, u32[]{:S(2)}) copy-start(f32[2048,8]{0,1:T(8,128)} %param.9) | copy-start | bytes 196612
  30.6 1.3 collective-permute-start
  71.4 1.3 collective-permute-start.1
  112.1 1.3 collective-permute-start.2
  152.8 1.3 collective-permute-start.3

commit v4 on v3

--- a/solution.py
+++ b/solution.py
@@ -21,7 +21,6 @@
 MSG = RHS * CAP + 1
 TALL = OWNERS * MSG
 CHUNK = 8
-UNROLL = 16
 CHUNKS = COUNT // CHUNK
 
 f32 = jnp.float32
@@ -79,9 +78,7 @@
 
 
 def fold(out):
-    first = out[0:8, 0:BS] + out[8:16, 0:BS]
-    second = out[16:24, BS:] + out[24:32, BS:]
-    return first, second
+    return out[0:RHS] + out[RHS:]
 
 
 def chunk_copy(blocks, bbuf, sem, c):
@@ -94,15 +91,18 @@
         us[r] = stacked(left[r * RHS : (r + 1) * RHS])
 
 
-def adjoint_pair(k, tab, us, h0, l0, h1, l1, msg):
-    lhs = jnp.concatenate([us[tab[COUNT + k]], us[tab[COUNT + k + 1]]], axis=0)
-    rhs = jnp.concatenate(
-        [jnp.concatenate([h0, l0], axis=0), jnp.concatenate([h1, l1], axis=0)], axis=1
-    )
-    out = lax.dot_general(lhs, rhs, (((1,), (0,)), ((), ())), preferred_element_type=f32)
-    first, second = fold(out)
-    msg[pl.ds(tab[k], RHS), :] = first
-    msg[pl.ds(tab[k + 1], RHS), :] = second
+def adjoint_block(pos, row, us, high, low, msg):
+    rhs = jnp.concatenate([high, low], axis=0)
+    out = lax.dot_general(us[row], rhs, (((1,), (0,)), ((), ())), preferred_element_type=f32)
+    msg[pl.ds(pos, RHS), :] = fold(out)
+
+
+def forward_block(piece, high, low):
+    rhs = jnp.concatenate([high, low], axis=1)
+    out = lax.dot_general(
+        stacked(piece), rhs, (((1,), (1,)), ((), ())), preferred_element_type=f32
+    )
+    return fold(out)
 
 
 def first_kernel(
@@ -139,34 +139,22 @@
     split_left(us, right_all)
     lane = lax.broadcasted_iota(jnp.int32, (1, BS), 1)
 
-    def place(g, carry):
-        for j in range(4):
-            k = g * 4 + j
+    for c in range(CHUNKS):
+        chunk_copy(blocks, bbuf, sem, c).wait()
+        for k in range(c * CHUNK, (c + 1) * CHUNK):
             o = owner[k]
             rank = taken[o]
             taken[o] = rank + 1
-            tab[k] = o * MSG + rank * RHS
-            tab[COUNT + k] = lax.rem(row[k], ROWS)
+            pos = o * MSG + rank * RHS
+            line = lax.rem(row[k], ROWS)
+            tab[k] = pos
+            tab[COUNT + k] = line
             span = pl.ds(o * MSG + MSG - 1, 1)
             msg[span, :] = jnp.where(lane == RHS + rank, col[k].astype(f32), msg[span, :])
-        return carry
-
-    lax.fori_loop(0, COUNT // 4, place, 0)
-
-    def chunk(c, carry):
-        chunk_copy(blocks, bbuf, sem, c).wait()
-        for j in range(0, CHUNK, 2):
-            k = c * CHUNK + j
-            h0, l0 = split(bbuf[k])
-            h1, l1 = split(bbuf[k + 1])
-            high[k] = h0
-            low[k] = l0
-            high[k + 1] = h1
-            low[k + 1] = l1
-            adjoint_pair(k, tab, us, h0, l0, h1, l1, msg)
-        return carry
-
-    lax.fori_loop(0, CHUNKS, chunk, 0)
+            h, l = split(bbuf[k])
+            high[k] = h
+            low[k] = l
+            adjoint_block(pos, line, us, h, l, msg)
 
 
 def forward_part(tab, inc, uraw, nleft, high, low, lraw, other):
@@ -174,29 +162,11 @@
     lraw[...] = jnp.zeros((ROWS * RHS, BS), f32)
     other[...] = jnp.zeros((ROWS * RHS, BS), f32)
 
-    def chunk(c, carry):
-        for j in range(0, UNROLL, 2):
-            k = c * UNROLL + j
-            lhs = jnp.concatenate(
-                [stacked(inc[pl.ds(tab[k], RHS), :]), stacked(inc[pl.ds(tab[k + 1], RHS), :])],
-                axis=0,
-            )
-            rhs = jnp.concatenate(
-                [
-                    jnp.concatenate([high[k], low[k]], axis=1),
-                    jnp.concatenate([high[k + 1], low[k + 1]], axis=1),
-                ],
-                axis=0,
-            )
-            out = lax.dot_general(lhs, rhs, (((1,), (1,)), ((), ())), preferred_element_type=f32)
-            first, second = fold(out)
-            span = pl.ds(pl.multiple_of(tab[COUNT + k] * RHS, RHS), RHS)
-            lraw[span, :] = lraw[span, :] + first
-            span = pl.ds(pl.multiple_of(tab[COUNT + k + 1] * RHS, RHS), RHS)
-            other[span, :] = other[span, :] + second
-        return carry
-
-    lax.fori_loop(0, COUNT // UNROLL, chunk, 0)
+    for k in range(COUNT):
+        part = forward_block(inc[pl.ds(tab[k], RHS), :], high[k], low[k])
+        span = pl.ds(pl.multiple_of(tab[COUNT + k] * RHS, RHS), RHS)
+        into = other if k % 2 else lraw
+        into[span, :] = into[span, :] + part
     image = lraw[...] + other[...]
     left = image / tiled(norm_right, ROWS) - tiled(norm_right, ROWS) * (
         uraw[...] / tiled(nleft[...], ROWS)
@@ -212,13 +182,8 @@
     put_rows(msg, row_of(squares(left)))
     split_left(us, left)
 
-    def chunk(c, carry):
-        for j in range(0, UNROLL, 2):
-            k = c * UNROLL + j
-            adjoint_pair(k, tab, us, high[k], low[k], high[k + 1], low[k + 1], msg)
-        return carry
-
-    lax.fori_loop(0, COUNT // UNROLL, chunk, 0)
+    for k in range(COUNT):
+        adjoint_block(tab[k], tab[COUNT + k], us, high[k], low[k], msg)
 
 
 def last_user_kernel(tab, inc, uraw, nleft, high, low, msg, lraw, nright, other):

time: 190 us -> 186 us (0.979)
  Pallas kernels: 18.9 us -> 14.1 us
    pallas_call x3, Pallas kernels: 9.25 us -> 5.66 us  [on_device(): call(user_kernel, [SMEM] + [VMEM] * 5, (msg_shape, vec, col8), None, [LEF...]
where the time goes in v4:
time: 186 us; the launch traced here: 184 us
  blocking collectives  164 us (88%)
  Pallas kernels  14.1 us (8%)
  waiting for transfers between devices  4.99 us (3%)
    all_to_all x8, blocking collectives, exchange(): return lax.all_to_all(sent, SHARD, 0, 0, tiled=True).reshape(TALL, BS)  151 us
    all_to_all x1, blocking collectives, on_device(): rows = lax.all_to_all(rows, GRP_SHARD, 0, 0, tiled=True)  13.3 us
    pallas_call x3, Pallas kernels, on_device(): call(user_kernel, [SMEM] + [VMEM] * 5, (msg_shape, vec, col8), None, [LEF...  5.66 us
    ppermute x4, waiting for transfers between devices, swap(): return lax.ppermute(half, 'grp', [(0, 1), (1, 0)])  4.99 us
  transfers between devices with their start and end apart: 4, of which 4 were waited for; matrix products, arithmetic and copies ran while one was open for 0% of the time, Pallas kernels for 0%

profile of v4, /device:TPU:0, one launch (start us, length us, event | category | flops | bytes accessed | tf_op | source)
XLA Modules:
  0.0 184.4 jit_solution(12170230808149015257)
XLA Ops:
  0.6 2.8 %shard_map.76 = (f32[1088,128]{1,0:T(8,128)S(1)}, s32[128]{0:T(128)S(4)}, bf16[64,128,128]{2,1,0:T(8,128)(2,1)S(1)}, bf16[64,128,128]{2,1,0:T(8,128)(2,1)S(1)}) custom-call(s32[64]{0:T(128)} %bitcast.56, s32[64]{0:T(128)} %row_in.1, s32[64]{0:T(128)} %col_in.1, f32[128,128]{1,0:T(8,128)} %bitcast.52, f32[64,128,128]{2,1,0:T(8,128)} %blocks.1), custom_call_target="tpu_custom_call" | custom-call | tf_op jit(solution)/shard_map/pallas_call | solution.py:365
  3.4 0.0 copy-start
  3.4 25.3 %all_to_all.83 = f32[64,1,2176]{2,1,0:T(1,128)S(1)} all-to-all(f32[64,1,2176]{2,1,0:T(1,128)S(1)} %bitcast.50), channel_id=1, replica_groups=mesh['grp'=2,'shard_0'=4,'shard_1'=4,'shard_2'=4] {'shard_0','shard_1','..., dimensions={0} | all-to-all | bytes 1114112 | tf_op jit(solution)/shard_map/all_to_all | solution.py:344
  28.7 1.4 shard_map.77
  30.1 0.1 collective-permute-start
  30.2 1.2 collective-permute-done.theirs
  31.4 0.3 shard_map.78
  31.7 18.5 %all_to_all.84 = f32[64,1,2176]{2,1,0:T(1,128)S(1)} all-to-all(f32[64,1,2176]{2,1,0:T(1,128)S(1)} %bitcast.49), channel_id=1, replica_groups=mesh['grp'=2,'shard_0'=4,'shard_1'=4,'shard_2'=4] {'shard_0','shard_1','..., dimensions={0} | all-to-all | bytes 1114112 | tf_op jit(solution)/shard_map/all_to_all | solution.py:344
  50.3 0.0 copy-done
  50.3 1.9 %shard_map.79 = (f32[1088,128]{1,0:T(8,128)S(1)}, f32[128,128]{1,0:T(8,128)S(1)}, f32[8,128]{1,0:T(8,128)S(1)}) custom-call(s32[128]{0:T(128)S(4)} %get-tuple-element.45.tab, f32[1088,128]{1,0:T(8,128)S(1)} %bitcast.39, f32[128,128]{1,0:T(8,128)S(1)} %bitcast.53, f32[8,128]{1,0:T(8,128)S(1)} %get-tuple-element.50.nleft.refs_5_.start, ...), custom_call_target="tpu_custom_call" | custom-call | tf_op jit(solution)/shard_map/pallas_call | solution.py:392
  52.2 17.1 %all_to_all.85 = f32[64,1,2176]{2,1,0:T(1,128)S(1)} all-to-all(f32[64,1,2176]{2,1,0:T(1,128)S(1)} %bitcast.51), channel_id=1, replica_groups=mesh['grp'=2,'shard_0'=4,'shard_1'=4,'shard_2'=4] {'shard_0','shard_1','..., dimensions={0} | all-to-all | bytes 1114112 | tf_op jit(solution)/shard_map/all_to_all | solution.py:344
  69.3 0.3 shard_map.80.refs_1_
  69.6 0.1 collective-permute-start.1
  69.7 1.2 collective-permute-done.1.refs_2_
  70.9 0.3 shard_map.81
  71.3 18.6 %all_to_all.86 = f32[64,1,2176]{2,1,0:T(1,128)S(1)} all-to-all(f32[64,1,2176]{2,1,0:T(1,128)S(1)} %bitcast.46), channel_id=1, replica_groups=mesh['grp'=2,'shard_0'=4,'shard_1'=4,'shard_2'=4] {'shard_0','shard_1','..., dimensions={0} | all-to-all | bytes 1114112 | tf_op jit(solution)/shard_map/all_to_all | solution.py:344
  89.8 1.9 %shard_map.82 = (f32[1088,128]{1,0:T(8,128)S(1)}, f32[128,128]{1,0:T(8,128)S(1)}, f32[8,128]{1,0:T(8,128)S(1)}) custom-call(s32[128]{0:T(128)S(4)} %get-tuple-element.45.tab, f32[1088,128]{1,0:T(8,128)S(1)} %bitcast.37, f32[128,128]{1,0:T(8,128)S(1)} %get-tuple-element.57.uraw, f32[8,128]{1,0:T(8,128)S(1)} %get-tuple-element.58.nleft, ...), custom_call_target="tpu_custom_call" | custom-call | tf_op jit(solution)/shard_map/pallas_call | solution.py:392
  91.7 17.1 %all_to_all.87 = f32[64,1,2176]{2,1,0:T(1,128)S(1)} all-to-all(f32[64,1,2176]{2,1,0:T(1,128)S(1)} %bitcast.47), channel_id=1, replica_groups=mesh['grp'=2,'shard_0'=4,'shard_1'=4,'shard_2'=4] {'shard_0','shard_1','..., dimensions={0} | all-to-all | bytes 1114112 | tf_op jit(solution)/shard_map/all_to_all | solution.py:344
  108.9 0.3 shard_map.83.refs_1_
  109.2 0.1 collective-permute-start.2
  109.3 1.2 collective-permute-done.2.refs_2_
  110.5 0.3 shard_map.84
  110.8 18.6 %all_to_all.88 = f32[64,1,2176]{2,1,0:T(1,128)S(1)} all-to-all(f32[64,1,2176]{2,1,0:T(1,128)S(1)} %bitcast.45), channel_id=1, replica_groups=mesh['grp'=2,'shard_0'=4,'shard_1'=4,'shard_2'=4] {'shard_0','shard_1','..., dimensions={0} | all-to-all | bytes 1114112 | tf_op jit(solution)/shard_map/all_to_all | solution.py:344
  129.4 1.9 %shard_map.85 = (f32[1088,128]{1,0:T(8,128)S(1)}, f32[128,128]{1,0:T(8,128)S(1)}, f32[8,128]{1,0:T(8,128)S(1)}) custom-call(s32[128]{0:T(128)S(4)} %get-tuple-element.45.tab, f32[1088,128]{1,0:T(8,128)S(1)} %bitcast.38, f32[128,128]{1,0:T(8,128)S(1)} %get-tuple-element.66.uraw, f32[8,128]{1,0:T(8,128)S(1)} %get-tuple-element.67.nleft, ...), custom_call_target="tpu_custom_call" | custom-call | tf_op jit(solution)/shard_map/pallas_call | solution.py:392
  131.3 17.1 %all_to_all.89 = f32[64,1,2176]{2,1,0:T(1,128)S(1)} all-to-all(f32[64,1,2176]{2,1,0:T(1,128)S(1)} %bitcast.48), channel_id=1, replica_groups=mesh['grp'=2,'shard_0'=4,'shard_1'=4,'shard_2'=4] {'shard_0','shard_1','..., dimensions={0} | all-to-all | bytes 1114112 | tf_op jit(solution)/shard_map/all_to_all | solution.py:344
  148.5 0.3 shard_map.86.refs_1_
  148.8 0.1 collective-permute-start.3
  148.9 1.2 collective-permute-done.3.refs_2_
  150.1 0.3 shard_map.87
  150.4 18.6 %all_to_all.90 = f32[64,1,2176]{2,1,0:T(1,128)S(1)} all-to-all(f32[64,1,2176]{2,1,0:T(1,128)S(1)} %bitcast.44), channel_id=1, replica_groups=mesh['grp'=2,'shard_0'=4,'shard_1'=4,'shard_2'=4] {'shard_0','shard_1','..., dimensions={0} | all-to-all | bytes 1114112 | tf_op jit(solution)/shard_map/all_to_all | solution.py:344
  169.0 1.3 shard_map.88
  170.4 13.3 %all_to_all.91 = f32[128,1,128]{2,1,0:T(1,128)S(1)} all-to-all(f32[128,1,128]{2,1,0:T(1,128)S(1)} %bitcast.55), channel_id=1, replica_groups=mesh['grp'=2,'shard_0'=4,'shard_1'=4,'shard_2'=4] {'grp','shard_0','shar..., dimensions={0} | all-to-all | bytes 131072 | tf_op jit(solution)/shard_map/all_to_all | solution.py:417
  183.6 0.8 shard_map.89
Async XLA Ops:
  3.4 46.9 %copy-start = (f32[2048,8]{0,1:T(8,128)S(1)}, f32[2048,8]{0,1:T(8,128)}, u32[]{:S(2)}) copy-start(f32[2048,8]{0,1:T(8,128)} %param.9) | copy-start | bytes 196612
  30.1 1.3 collective-permute-start
  69.6 1.3 collective-permute-start.1
  109.2 1.3 collective-permute-start.2
  148.8 1.3 collective-permute-start.3

commit v5 on v4

v5 whole, which is shorter than its diff:
```python
import jax
import jax.numpy as jnp
from jax import lax
from jax.experimental import pallas as pl
from jax.experimental.pallas import tpu as pltpu
from jax.sharding import Mesh
from jax.sharding import PartitionSpec as P

ITERS = 4
COLS_OWN = 16
SHARD = ("shard_0", "shard_1", "shard_2")
GRP_SHARD = ("grp", "shard_0", "shard_1", "shard_2")

OWNERS = 64
CAP = 2
BS = 128
RHS = 8
COUNT = 64
ROWS = 16
SLOTS = OWNERS * CAP
MSG = RHS * CAP + 1
TALL = OWNERS * MSG
CHUNK = 8
CHUNKS = COUNT // CHUNK
PART = RHS // 2
LINES = 2 * ROWS
VEC = COLS_OWN * PART

f32 = jnp.float32
bf16 = jnp.bfloat16


def diag_mask():
    sub = lax.broadcasted_iota(jnp.int32, (RHS, BS), 0)
    lane = lax.broadcasted_iota(jnp.int32, (RHS, BS), 1)
    return sub == lane


def row_of(column):
    return jnp.sum(jnp.where(diag_mask(), column, 0.0), axis=0, keepdims=True)


def column_of(row):
    spread = jnp.broadcast_to(row, (RHS, BS))
    total = jnp.sum(jnp.where(diag_mask(), spread, 0.0), axis=1, keepdims=True)
    return jnp.broadcast_to(total, (RHS, BS))


def squares(values):
    cube = values.reshape(values.shape[0] // RHS, RHS, BS)
    total = jnp.sum(jnp.sum(cube * cube, axis=0), axis=1, keepdims=True)
    return jnp.broadcast_to(total, (RHS, BS))


def part_squares(values):
    cube = values.reshape(values.shape[0] // RHS, RHS, BS)
    total = jnp.sum(cube * cube, axis=0)
    total = total[:PART] + total[PART:]
    total = jnp.sum(jnp.concatenate([total, total], axis=0), axis=1, keepdims=True)
    return jnp.broadcast_to(total, (RHS, BS))


def part_mask(shift):
    sub = lax.broadcasted_iota(jnp.int32, (RHS, BS), 0)
    lane = lax.broadcasted_iota(jnp.int32, (RHS, BS), 1)
    return sub, lane, lane == jnp.where(sub < PART, sub, sub - PART) + shift


def part_row(column, shift=0):
    sub, _, mask = part_mask(shift)
    return jnp.sum(jnp.where(mask & (sub < PART), column, 0.0), axis=0, keepdims=True)


def part_column(row, shift=0):
    _, _, mask = part_mask(shift)
    spread = jnp.broadcast_to(row, (RHS, BS))
    total = jnp.sum(jnp.where(mask, spread, 0.0), axis=1, keepdims=True)
    return jnp.broadcast_to(total, (RHS, BS))


def tiled(column, count):
    return jnp.concatenate([column] * count, axis=0)


def sum_rows(ref, column_of):
    rows = [ref[pl.ds(MSG * o + MSG - 1, 1), :] for o in range(OWNERS)]
    while len(rows) > 1:
        rows = [rows[i] + rows[i + 1] for i in range(0, len(rows), 2)]
    return column_of(rows[0])


def put_rows(ref, row):
    for o in range(OWNERS):
        ref[pl.ds(MSG * o + MSG - 1, 1), :] = row


def split(x):
    high = x.astype(bf16)
    low = (x - high.astype(f32)).astype(bf16)
    return high, low


def stacked(x):
    high = x.astype(bf16).astype(f32)
    both = jnp.concatenate([high, x - high], axis=0).astype(bf16)
    return jnp.concatenate([both, both], axis=1)


def fold(out):
    half = out.shape[0] // 2
    return out[:half] + out[half:]


def chunk_copy(blocks, bbuf, sem, c):
    span = pl.ds(c * CHUNK, CHUNK)
    return pltpu.make_async_copy(blocks.at[span], bbuf.at[span], sem.at[c])


def split_left(us, left, height):
    for r in range(left.shape[0] // height):
        us[r] = stacked(left[r * height : (r + 1) * height])


def adjoint_block(pos, row, us, high, low, msg):
    rhs = jnp.concatenate([high, low], axis=0)
    out = lax.dot_general(us[row], rhs, (((1,), (0,)), ((), ())), preferred_element_type=f32)
    sent = fold(out)
    msg[pl.ds(pos, sent.shape[0]), :] = sent


def forward_block(piece, high, low):
    rhs = jnp.concatenate([high, low], axis=1)
    out = lax.dot_general(
        stacked(piece), rhs, (((1,), (1,)), ((), ())), preferred_element_type=f32
    )
    return fold(out)


def first_kernel(
    owner_in, row_in, col_in, right_in, blocks,
    msg, tab, line_row, high, low,
    bbuf, right, us, owner, row, col, taken, sem, little,
):
    loads = [
        pltpu.make_async_copy(owner_in, owner, little.at[0]),
        pltpu.make_async_copy(row_in, row, little.at[1]),
        pltpu.make_async_copy(col_in, col, little.at[2]),
        pltpu.make_async_copy(right_in, right, little.at[3]),
    ]
    for load in loads:
        load.start()

    def begin(c, carry):
        chunk_copy(blocks, bbuf, sem, c).start()
        return carry

    lax.fori_loop(0, CHUNKS, begin, 0)
    msg[...] = jnp.zeros((TALL, BS), f32)

    def clear(g, carry):
        for j in range(8):
            taken[g * 8 + j] = 0
        return carry

    lax.fori_loop(0, OWNERS // 8, clear, 0)
    for load in loads:
        load.wait()
    right_all = right[...]
    put_rows(msg, row_of(squares(right_all)))
    split_left(us, right_all, RHS)
    grp = lax.axis_index("grp")
    listed = jnp.zeros((1, BS), f32)
    lane = lax.broadcasted_iota(jnp.int32, (1, BS), 1)

    for c in range(CHUNKS):
        chunk_copy(blocks, bbuf, sem, c).wait()
        for k in range(c * CHUNK, (c + 1) * CHUNK):
            o = owner[k]
            rank = taken[o]
            taken[o] = rank + 1
            pos = o * MSG + rank * RHS
            line = lax.rem(row[k], ROWS)
            place = o * MSG + grp * (CAP * PART) + rank * PART
            here = line + grp * ROWS
            tab[k] = place
            tab[COUNT + k] = here
            listed = jnp.where(lane == k, place.astype(f32), listed)
            listed = jnp.where(lane == COUNT + k, here.astype(f32), listed)
            span = pl.ds(o * MSG + MSG - 1, 1)
            msg[span, :] = jnp.where(lane == RHS + rank, col[k].astype(f32), msg[span, :])
            h, l = split(bbuf[k])
            high[k] = h
            low[k] = l
            adjoint_block(pos, line, us, h, l, msg)
    line_row[...] = jnp.broadcast_to(listed, (RHS, BS))


def first_owner_kernel(inc, right, line_row, keep, send, p0, p1, p2, p3, vcols, cols, sem):
    grp = lax.axis_index("grp")
    parts = (p0, p1, p2, p3)
    lane = lax.broadcasted_iota(jnp.int32, (1, BS), 1)
    pairs = [
        jnp.where(
            lane == o * CAP,
            inc[pl.ds(MSG * o + MSG - 1, 1), RHS : RHS + 1],
            jnp.where(lane == o * CAP + 1, inc[pl.ds(MSG * o + MSG - 1, 1), RHS + 1 : RHS + 2], 0.0),
        )
        for o in range(OWNERS)
    ]
    while len(pairs) > 1:
        pairs = [pairs[i] + pairs[i + 1] for i in range(0, len(pairs), 2)]
    vcols[...] = pairs[0][0].astype(jnp.int32)
    copy = pltpu.make_async_copy(vcols, cols, sem)
    copy.start()
    norm = sum_rows(inc, column_of)
    for ref in (keep, send):
        ref[pl.ds(VEC, RHS), :] = norm
        ref[pl.ds(VEC + RHS, 1), :] = pairs[0]
        ref[pl.ds(VEC + RHS + 1, 1), :] = line_row[pl.ds(0, 1), :]
        ref[pl.ds(VEC + RHS + 2, RHS - 2), :] = jnp.zeros((RHS - 2, BS), f32)
    for part in parts:
        part[...] = jnp.zeros((COLS_OWN * RHS, BS), f32)

    def halves(at, tile):
        first, second = tile[:PART], tile[PART:]
        keep[pl.ds(at, PART), :] = jnp.where(grp == 0, first, second)
        send[pl.ds(at, PART), :] = jnp.where(grp == 0, second, first)

    for r in range(ROWS):
        halves(VEC + 2 * RHS + r * PART, right[pl.ds(r * RHS, RHS), :])
    copy.wait()

    def step(g, carry):
        for j in range(8):
            o = g * 8 + j
            for s in range(CAP):
                span = pl.ds(pl.multiple_of(cols[o * CAP + s] * RHS, RHS), RHS)
                part = parts[(2 * j + s) % len(parts)]
                part[span, :] = part[span, :] + inc[pl.ds(o * MSG + s * RHS, RHS), :]
        return carry

    lax.fori_loop(0, OWNERS // 8, step, 0)
    for c in range(COLS_OWN):
        span = pl.ds(c * RHS, RHS)
        halves(c * PART, (p0[span, :] + p1[span, :]) + (p2[span, :] + p3[span, :]))


def send_slots(cols, raw, msg):
    put_rows(msg, part_row(part_squares(raw[...])))

    def step(g, carry):
        for j in range(8):
            o = g * 8 + j
            for s in range(2 * CAP):
                c = cols[s // CAP][o * CAP + s % CAP]
                msg[pl.ds(o * MSG + s * PART, PART), :] = raw[pl.ds(c * PART, PART), :]
        return carry

    lax.fori_loop(0, OWNERS // 8, step, 0)


def first_send_kernel(
    keep, theirs,
    msg, raw, nleft, left, tab, cols0, cols1,
    vtab, vcols0, vcols1, sem,
):
    grp = lax.axis_index("grp")
    mine_cols = keep[pl.ds(VEC + RHS, 1), :]
    other_cols = theirs[pl.ds(VEC + RHS, 1), :]
    vtab[...] = theirs[pl.ds(VEC + RHS + 1, 1), :][0].astype(jnp.int32)
    vcols0[...] = jnp.where(grp == 0, mine_cols, other_cols)[0].astype(jnp.int32)
    vcols1[...] = jnp.where(grp == 0, other_cols, mine_cols)[0].astype(jnp.int32)
    copies = [
        pltpu.make_async_copy(vtab, tab, sem.at[0]),
        pltpu.make_async_copy(vcols0, cols0, sem.at[1]),
        pltpu.make_async_copy(vcols1, cols1, sem.at[2]),
    ]
    for copy in copies:
        copy.start()
    norm = jnp.sqrt(keep[pl.ds(VEC, RHS), :] + theirs[pl.ds(VEC, RHS), :])
    own = jnp.where(grp == 0, norm[:PART], norm[PART:])
    norm = jnp.concatenate([own, own], axis=0)
    nleft[...] = norm
    body = pl.ds(0, VEC)
    raw[...] = (keep[body, :] + theirs[body, :]) / tiled(norm, VEC // RHS)
    size = ROWS * PART
    tail = pl.ds(VEC + 2 * RHS, size)
    left[pl.ds(pl.multiple_of(grp * size, RHS), size), :] = keep[tail, :]
    left[pl.ds(pl.multiple_of((1 - grp) * size, RHS), size), :] = theirs[tail, :]
    for copy in copies:
        copy.wait()
    send_slots((cols0, cols1), raw, msg)


def send_kernel(first, cols0, cols1, inc, qprev, nright, *refs):
    parts = refs[-4:]
    if first:
        start, msg, raw, nleft, sol, search, scal = refs[:-4]
    else:
        sol_in, search_in, scal_in, msg, raw, nleft, sol, search, scal = refs[:-4]
    cols = (cols0, cols1)
    for part in parts:
        part[...] = jnp.zeros((VEC, BS), f32)

    def step(g, carry):
        for j in range(8):
            o = g * 8 + j
            for s in range(2 * CAP):
                span = pl.ds(cols[s // CAP][o * CAP + s % CAP] * PART, PART)
                part = parts[s]
                part[span, :] = part[span, :] + inc[pl.ds(o * MSG + s * PART, PART), :]
        return carry

    lax.fori_loop(0, OWNERS // 8, step, 0)
    total = (parts[0][...] + parts[1][...]) + (parts[2][...] + parts[3][...])
    n = VEC // RHS
    norm_left = jnp.sqrt(sum_rows(inc, part_column))
    norm_right = nright[...]
    nleft[...] = norm_left
    vec = qprev[...] / tiled(norm_right, n)
    raw[...] = total / tiled(norm_left, n) - tiled(norm_left, n) * vec
    send_slots(cols, raw, msg)
    if first:
        old_search = vec
        diag_bar = norm_right
        residual = start[...]
        old_sol = jnp.zeros((VEC, BS), f32)
    else:
        radius = scal_in[pl.ds(0, RHS), :]
        cosine = scal_in[pl.ds(RHS, RHS), :]
        sine_term = scal_in[pl.ds(2 * RHS, RHS), :]
        residual = scal_in[pl.ds(3 * RHS, RHS), :]
        coupling = sine_term * norm_right
        old_search = vec - tiled(coupling / radius, n) * search_in[...]
        diag_bar = -cosine * norm_right
        old_sol = sol_in[...]
    radius = jnp.sqrt(diag_bar * diag_bar + norm_left * norm_left)
    cosine = diag_bar / radius
    sine_term = norm_left / radius
    sol[...] = old_sol + tiled(cosine * residual / radius, n) * old_search
    search[...] = old_search
    scal[pl.ds(0, RHS), :] = radius
    scal[pl.ds(RHS, RHS), :] = cosine
    scal[pl.ds(2 * RHS, RHS), :] = sine_term
    scal[pl.ds(3 * RHS, RHS), :] = sine_term * residual


def forward_all(tab, inc, high, low, into):
    for k in range(COUNT):
        part = forward_block(inc[pl.ds(tab[k], PART), :], high[k], low[k])
        span = pl.ds(tab[COUNT + k] * PART, PART)
        ref = into[k % 2]
        ref[span, :] = ref[span, :] + part


def adjoint_all(tab, us, high, low, msg):
    for k in range(COUNT):
        adjoint_block(tab[k], tab[COUNT + k], us, high[k], low[k], msg)


def left_of(lraw, other, uraw, nleft, norm_right):
    n = LINES * PART // RHS
    left = (lraw[...] + other[...]) / tiled(norm_right, n) - tiled(norm_right, n) * (
        uraw[...] / tiled(nleft[...], n)
    )
    lraw[...] = left
    return left


def first_user_kernel(
    tab, tab2, inc, uraw, nleft, high, low, blocks,
    msg, lraw, nright, high2, low2,
    other, us, bbuf, sem,
):
    for c in range(CHUNKS):
        chunk_copy(blocks, bbuf, sem, c).start()
    norm_right = jnp.sqrt(sum_rows(inc, part_column))
    nright[...] = norm_right
    lraw[...] = jnp.zeros(lraw.shape, f32)
    other[...] = jnp.zeros(lraw.shape, f32)
    forward_all(tab, inc, high, low, (lraw, other))
    for c in range(CHUNKS):
        chunk_copy(blocks, bbuf, sem, c).wait()
        for k in range(c * CHUNK, (c + 1) * CHUNK):
            h, l = split(bbuf[k])
            high2[k] = h
            low2[k] = l
            part = forward_block(inc[pl.ds(tab2[k], PART), :], h, l)
            span = pl.ds(tab2[COUNT + k] * PART, PART)
            ref = other if k % 2 else lraw
            ref[span, :] = ref[span, :] + part
    left = left_of(lraw, other, uraw, nleft, norm_right)
    msg[...] = jnp.zeros((TALL, BS), f32)
    put_rows(msg, part_row(part_squares(left)))
    split_left(us, left, PART)
    adjoint_all(tab, us, high, low, msg)
    adjoint_all(tab2, us, high2, low2, msg)


def user_kernel(
    tab, tab2, inc, uraw, nleft, high, low, high2, low2, msg, lraw, nright, other, us
):
    norm_right = jnp.sqrt(sum_rows(inc, part_column))
    nright[...] = norm_right
    lraw[...] = jnp.zeros(lraw.shape, f32)
    other[...] = jnp.zeros(lraw.shape, f32)
    forward_all(tab, inc, high, low, (lraw, other))
    forward_all(tab2, inc, high2, low2, (lraw, other))
    left = left_of(lraw, other, uraw, nleft, norm_right)
    msg[...] = jnp.zeros((TALL, BS), f32)
    put_rows(msg, part_row(part_squares(left)))
    split_left(us, left, PART)
    adjoint_all(tab, us, high, low, msg)
    adjoint_all(tab2, us, high2, low2, msg)


def last_user_kernel(
    tab, tab2, inc, uraw, nleft, high, low, high2, low2, msg, lraw, nright, other
):
    norm_right = jnp.sqrt(sum_rows(inc, part_column))
    nright[...] = norm_right
    lraw[...] = jnp.zeros(lraw.shape, f32)
    other[...] = jnp.zeros(lraw.shape, f32)
    forward_all(tab, inc, high, low, (lraw, other))
    forward_all(tab2, inc, high2, low2, (lraw, other))
    left = left_of(lraw, other, uraw, nleft, norm_right)
    row = part_row(part_squares(left), lax.axis_index("grp") * PART)
    msg[...] = jnp.broadcast_to(row, msg.shape)


def final_kernel(rows, lraw, qprev, nright, sol_in, search_in, scal_in, start, keep, send):
    grp = lax.axis_index("grp")
    total = jnp.sum(rows[...], axis=0, keepdims=True)
    norm_left = jnp.sqrt(part_column(total, grp * PART))
    norm_right = nright[...]
    size = ROWS * PART
    n = size // RHS
    for ref, at in ((keep, grp), (send, 1 - grp)):
        left = lraw[pl.ds(pl.multiple_of(at * size, RHS), size), :] / tiled(norm_left, n)
        ref[pl.ds(VEC + RHS, size), :] = left
    n = VEC // RHS
    radius = scal_in[pl.ds(0, RHS), :]
    cosine = scal_in[pl.ds(RHS, RHS), :]
    sine_term = scal_in[pl.ds(2 * RHS, RHS), :]
    residual = scal_in[pl.ds(3 * RHS, RHS), :]
    vec = qprev[...] / tiled(norm_right, n)
    search = vec - tiled(sine_term * norm_right / radius, n) * search_in[...]
    diag_bar = -cosine * norm_right
    radius = jnp.sqrt(diag_bar * diag_bar + norm_left * norm_left)
    cosine = diag_bar / radius
    sine_term = norm_left / radius
    sol = sol_in[...] + tiled(cosine * residual / radius, n) * search
    rel = sine_term * residual / start[...]
    for ref in (keep, send):
        ref[pl.ds(0, VEC), :] = sol
        ref[pl.ds(VEC, RHS), :] = rel


def join_kernel(keep, theirs, sol, left, rel):
    grp = lax.axis_index("grp")

    def joined(at):
        mine = keep[pl.ds(at, PART), :]
        other = theirs[pl.ds(at, PART), :]
        first = jnp.where(grp == 0, mine, other)
        second = jnp.where(grp == 0, other, mine)
        return jnp.concatenate([first, second], axis=0)

    for c in range(COLS_OWN):
        sol[pl.ds(c * RHS, RHS), :] = joined(c * PART)
    for r in range(ROWS):
        left[pl.ds(r * RHS, RHS), :] = joined(VEC + RHS + r * PART)
    rel[...] = row_of(joined(VEC))[0, :RHS]


def shape(*dims, dtype=f32):
    return jax.ShapeDtypeStruct(dims, dtype)


VMEM = pl.BlockSpec(memory_space=pltpu.VMEM)
SMEM = pl.BlockSpec(memory_space=pltpu.SMEM)
HBM = pl.BlockSpec(memory_space=pltpu.HBM)
PARTS = [pltpu.VMEM((COLS_OWN * RHS, BS), f32)] * 4
LEFTS = pltpu.VMEM((ROWS, 2 * RHS, 2 * BS), bf16)
LEFTS2 = pltpu.VMEM((LINES, RHS, 2 * BS), bf16)
LEFT = pltpu.VMEM((ROWS * RHS, BS), f32)
BUFFER = pltpu.VMEM((COUNT, BS, BS), f32)
SEMS = pltpu.SemaphoreType.DMA((CHUNKS,))
ONE = pltpu.SemaphoreType.DMA(())
LINE = pltpu.VMEM((SLOTS,), jnp.int32)


def call(body, ins, outs, specs_out=None, scratch=()):
    return pl.pallas_call(
        body,
        out_shape=outs,
        in_specs=ins,
        out_specs=specs_out or jax.tree.map(lambda _: VMEM, outs),
        scratch_shapes=scratch,
        compiler_params=pltpu.CompilerParams(vmem_limit_bytes=24 * 1024 * 1024),
    )


def exchange(msg):
    sent = msg.reshape(OWNERS, MSG * BS)
    return lax.all_to_all(sent, SHARD, 0, 0, tiled=True).reshape(TALL, BS)


def swap(half):
    return lax.ppermute(half, "grp", [(0, 1), (1, 0)])


def small(*xs):
    return [pltpu.with_memory_space_constraint(x, pltpu.SMEM) for x in xs]


def near(*xs):
    return [pltpu.with_memory_space_constraint(x, pltpu.VMEM) for x in xs]


def far(*xs):
    return [pltpu.with_memory_space_constraint(x, pltpu.HBM) for x in xs]


def on_device(blocks, block_row, block_owner, block_col, right_side):
    owner = block_owner[:, 0]
    right = right_side.reshape(ROWS, BS, RHS).transpose(0, 2, 1).reshape(ROWS * RHS, BS)
    left_shape = shape(LINES * PART, BS)
    vec = shape(VEC, BS)
    col8 = shape(RHS, BS)
    msg_shape = shape(TALL, BS)
    table = pltpu.MemorySpace.SMEM((SLOTS,), jnp.int32)
    terms = pltpu.MemorySpace.VMEM((COUNT, BS, BS), bf16)
    swapped = shape(VEC + 2 * RHS + ROWS * PART, BS)

    blocks2 = swap(blocks)
    msg, tab, line_row, high, low = call(
        first_kernel,
        [HBM] * 5,
        (msg_shape, table, col8, terms, terms),
        (VMEM, SMEM, VMEM, VMEM, VMEM),
        [BUFFER, LEFT, LEFTS]
        + [pltpu.SMEM((COUNT,), jnp.int32)] * 4
        + [SEMS, pltpu.SemaphoreType.DMA((4,))],
    )(*far(owner, block_row, block_col, right, blocks))
    inc = exchange(msg)
    keep, send = call(
        first_owner_kernel,
        [VMEM] * 3,
        (swapped, swapped),
        None,
        PARTS + [LINE, pltpu.SMEM((SLOTS,), jnp.int32), ONE],
    )(inc, right, line_row)
    msg, raw, norm_left, left, tab2, cols0, cols1 = call(
        first_send_kernel,
        [VMEM] * 2,
        (msg_shape, vec, col8, left_shape, table, table, table),
        (VMEM,) * 4 + (SMEM,) * 3,
        [LINE] * 3 + [pltpu.SemaphoreType.DMA((3,))],
    )(keep, swap(send))
    start = norm_left
    state = None
    for repeat in range(ITERS):
        inc = exchange(msg)
        if repeat == ITERS - 1:
            break
        if repeat == 0:
            msg, left, norm_right, high2, low2 = call(
                first_user_kernel,
                [SMEM] * 2 + [VMEM] * 5 + [HBM],
                (msg_shape, left_shape, col8, terms, terms),
                (VMEM,) * 5,
                [LEFT, LEFTS2, BUFFER, SEMS],
            )(*small(tab, tab2), inc, left, norm_left, *near(high, low), *far(blocks2))
        else:
            msg, left, norm_right = call(
                user_kernel,
                [SMEM] * 2 + [VMEM] * 7,
                (msg_shape, left_shape, col8),
                None,
                [LEFT, LEFTS2],
            )(*small(tab, tab2), inc, left, norm_left, *near(high, low, high2, low2))
        inc = exchange(msg)
        first = repeat == 0
        tail = (start,) if first else state
        outs = call(
            lambda *refs, first=first: send_kernel(first, *refs),
            [SMEM] * 2 + [VMEM] * (3 + len(tail)),
            (msg_shape, vec, col8, vec, vec, shape(4 * RHS, BS)),
            None,
            [pltpu.VMEM((VEC, BS), f32)] * 4,
        )(*small(cols0, cols1), inc, raw, norm_right, *tail)
        msg, raw, norm_left = outs[:3]
        state = outs[3:]
    rows, left, norm_right = call(
        last_user_kernel,
        [SMEM] * 2 + [VMEM] * 7,
        (shape(2 * OWNERS, BS), left_shape, col8),
        None,
        [LEFT],
    )(*small(tab, tab2), inc, left, norm_left, *near(high, low, high2, low2))
    rows = lax.all_to_all(rows, GRP_SHARD, 0, 0, tiled=True)
    ends = shape(VEC + RHS + ROWS * PART, BS)
    keep, send = call(final_kernel, [VMEM] * 8, (ends, ends))(
        rows, left, raw, norm_right, *state, start
    )
    full = shape(COLS_OWN * RHS, BS)
    sol, left, rel = call(join_kernel, [VMEM] * 2, (full, full, shape(RHS)))(keep, swap(send))

    def tall(x):
        return x.reshape(COLS_OWN, RHS, BS).transpose(0, 2, 1).reshape(COLS_OWN * BS, RHS)

    return tall(sol), tall(left), rel


def solution(mesh):
    torus = Mesh(
        mesh.devices.reshape(mesh.shape["grp"], 4, 4, 4), ("grp", "shard_0", "shard_1", "shard_2")
    )
    return jax.shard_map(
        on_device,
        mesh=torus,
        in_specs=(
            P(GRP_SHARD, None, None),
            P(GRP_SHARD),
            P(GRP_SHARD, None),
            P(GRP_SHARD),
            P(GRP_SHARD, None),
        ),
        out_specs=(P(SHARD, None), P(GRP_SHARD, None), P()),
        check_vma=False,
    )
```

time: 186 us -> 189 us (1.016)
  Pallas kernels: 14.1 us -> 23.5 us
  blocking collectives: 164 us -> 158 us
  waiting for transfers between devices: 4.99 us -> 2.5 us
  local copies, waits for them, and re-layouts: 0.01 us -> 1.97 us
    pallas_call x14 -> x12, Pallas kernels: 14.1 us -> 23.5 us  [the longest x2 7.1 us: on_device(): call(user_kernel, [SMEM] * 2 + [VMEM] * 7, (msg_shape, left_shape, col8),...]
    all_to_all x8, blocking collectives: 151 us -> 145 us  [exchange(): return lax.all_to_all(sent, SHARD, 0, 0, tiled=True).reshape(TALL, BS)]
    ppermute x4 -> x3, waiting for transfers between devices: 4.99 us -> 2.5 us  [swap(): return lax.ppermute(half, 'grp', [(0, 1), (1, 0)])]
    unnamed x2 -> x4, local copies, waits for them, and re-layouts: 0.01 us -> 1.97 us
  transfers between devices with their start and end apart: 4 -> 3, of which waited for: 4 -> 2; matrix products, arithmetic and copies ran while one was open for 0% -> 0% of each run, Pallas kernels for 0% -> 3%
where the time goes in v5:
time: 189 us; the launch traced here: 187 us
  blocking collectives  158 us (84%)
  Pallas kernels  23.5 us (12%)
  waiting for transfers between devices  2.5 us (1%)
  local copies, waits for them, and re-layouts  1.97 us (1%)
    all_to_all x8, blocking collectives, exchange(): return lax.all_to_all(sent, SHARD, 0, 0, tiled=True).reshape(TALL, BS)  145 us
    all_to_all x1, blocking collectives, on_device(): rows = lax.all_to_all(rows, GRP_SHARD, 0, 0, tiled=True)  13.3 us
    pallas_call x2, Pallas kernels, on_device(): call(user_kernel, [SMEM] * 2 + [VMEM] * 7, (msg_shape, left_shape, col8),...  7.1 us
    pallas_call x1, Pallas kernels, on_device(): call(first_user_kernel, [SMEM] * 2 + [VMEM] * 5 + [HBM], (msg_shape, left...  5.52 us
  transfers between devices with their start and end apart: 3, of which 2 were waited for; matrix products, arithmetic and copies ran while one was open for 0% of the time, Pallas kernels for 3%

profile of v5, /device:TPU:0, one launch (start us, length us, event | category | flops | bytes accessed | tf_op | source)
XLA Modules:
  0.0 187.1 jit_solution(14821643940843245718)
XLA Ops:
  0.6 0.1 collective-permute-start.1
  0.7 0.0 copy-start
  0.7 2.8 %shard_map.76 = (f32[1088,128]{1,0:T(8,128)S(1)}, s32[128]{0:T(128)S(4)}, f32[8,128]{1,0:T(8,128)S(1)}, bf16[64,128,128]{2,1,0:T(8,128)(2,1)S(1)}, bf16[64,128,128]{2,1,0:T(8,128)(2,1)S(1)}) custom-call(s32[64]{0:T(128)} %bitcast.56, s32[64]{0:T(128)} %row_in.1, s32[64]{0:T(128)} %col_in.1, f32[128,128]{1,0:T(8,128)} %bitcast.52, f32[64,128,128]{2,1,0:T(8,128)} %blocks.1), custom_call_target="tpu_custom_call" | custom-call | tf_op jit(solution)/shard_map/pallas_call | solution.py:537
  3.5 25.8 %all_to_all.83 = f32[64,1,2176]{2,1,0:T(1,128)S(1)} all-to-all(f32[64,1,2176]{2,1,0:T(1,128)S(1)} %bitcast.51), channel_id=1, replica_groups=mesh['grp'=2,'shard_0'=4,'shard_1'=4,'shard_2'=4] {'shard_0','shard_1','..., dimensions={0} | all-to-all | bytes 1114112 | tf_op jit(solution)/shard_map/all_to_all | solution.py:506
  29.3 0.0 copy-done
  29.3 1.0 shard_map.77
  30.3 0.1 collective-permute-start
  30.4 1.3 collective-permute-done.theirs
  31.7 1.0 shard_map.78
  32.7 18.5 %all_to_all.84 = f32[64,1,2176]{2,1,0:T(1,128)S(1)} all-to-all(f32[64,1,2176]{2,1,0:T(1,128)S(1)} %bitcast.46), channel_id=1, replica_groups=mesh['grp'=2,'shard_0'=4,'shard_1'=4,'shard_2'=4] {'shard_0','shard_1','..., dimensions={0} | all-to-all | bytes 1114112 | tf_op jit(solution)/shard_map/all_to_all | solution.py:506
  51.2 0.0 collective-permute-done.1.blocks
  51.2 0.0 copy-start.1
  51.2 2.0 %copy-done.1 = f32[64,128,128]{2,1,0:T(8,128)} copy-done((f32[64,128,128]{2,1,0:T(8,128)}, f32[64,128,128]{2,1,0:T(8,128)S(1)}, u32[]{:S(2)}) %copy-start.1) | copy-done | bytes 4194328
  53.2 5.5 %shard_map.79 = (f32[1088,128]{1,0:T(8,128)S(1)}, f32[128,128]{1,0:T(8,128)S(1)}, f32[8,128]{1,0:T(8,128)S(1)}, bf16[64,128,128]{2,1,0:T(8,128)(2,1)S(1)}, bf16[64,128,128]{2,1,0:T(8,128)(2,1)S(1)}) custom-call(s32[128]{0:T(128)S(4)} %get-tuple-element.54.tab, s32[128]{0:T(128)S(4)} %get-tuple-element.59.tab2, f32[1088,128]{1,0:T(8,128)S(1)} %bitcast.37, ...), custom_call_target="tpu_custom_call" | custom-call | tf_op jit(solution)/shard_map/pallas_call | solution.py:568
  58.7 17.1 %all_to_all.85 = f32[64,1,2176]{2,1,0:T(1,128)S(1)} all-to-all(f32[64,1,2176]{2,1,0:T(1,128)S(1)} %bitcast.48), channel_id=1, replica_groups=mesh['grp'=2,'shard_0'=4,'shard_1'=4,'shard_2'=4] {'shard_0','shard_1','..., dimensions={0} | all-to-all | bytes 1114112 | tf_op jit(solution)/shard_map/all_to_all | solution.py:506
  75.8 0.9 shard_map.80
  76.8 16.7 %all_to_all.86 = f32[64,1,2176]{2,1,0:T(1,128)S(1)} all-to-all(f32[64,1,2176]{2,1,0:T(1,128)S(1)} %bitcast.47), channel_id=1, replica_groups=mesh['grp'=2,'shard_0'=4,'shard_1'=4,'shard_2'=4] {'shard_0','shard_1','..., dimensions={0} | all-to-all | bytes 1114112 | tf_op jit(solution)/shard_map/all_to_all | solution.py:506
  93.4 3.5 %shard_map.81 = (f32[1088,128]{1,0:T(8,128)S(1)}, f32[128,128]{1,0:T(8,128)S(1)}, f32[8,128]{1,0:T(8,128)S(1)}) custom-call(s32[128]{0:T(128)S(4)} %get-tuple-element.54.tab, s32[128]{0:T(128)S(4)} %get-tuple-element.59.tab2, f32[1088,128]{1,0:T(8,128)S(1)} %bitcast.38, f32[128,128]{1,0:T(8,128)S(1)} %get-tuple-element.71.uraw, ...), custom_call_target="tpu_custom_call" | custom-call | tf_op jit(solution)/shard_map/pallas_call | solution.py:576
  97.0 16.8 %all_to_all.87 = f32[64,1,2176]{2,1,0:T(1,128)S(1)} all-to-all(f32[64,1,2176]{2,1,0:T(1,128)S(1)} %bitcast.49), channel_id=1, replica_groups=mesh['grp'=2,'shard_0'=4,'shard_1'=4,'shard_2'=4] {'shard_0','shard_1','..., dimensions={0} | all-to-all | bytes 1114112 | tf_op jit(solution)/shard_map/all_to_all | solution.py:506
  113.8 1.0 shard_map.82
  114.8 16.7 %all_to_all.88 = f32[64,1,2176]{2,1,0:T(1,128)S(1)} all-to-all(f32[64,1,2176]{2,1,0:T(1,128)S(1)} %bitcast.45), channel_id=1, replica_groups=mesh['grp'=2,'shard_0'=4,'shard_1'=4,'shard_2'=4] {'shard_0','shard_1','..., dimensions={0} | all-to-all | bytes 1114112 | tf_op jit(solution)/shard_map/all_to_all | solution.py:506
  131.4 3.5 %shard_map.83 = (f32[1088,128]{1,0:T(8,128)S(1)}, f32[128,128]{1,0:T(8,128)S(1)}, f32[8,128]{1,0:T(8,128)S(1)}) custom-call(s32[128]{0:T(128)S(4)} %get-tuple-element.54.tab, s32[128]{0:T(128)S(4)} %get-tuple-element.59.tab2, f32[1088,128]{1,0:T(8,128)S(1)} %bitcast.39, f32[128,128]{1,0:T(8,128)S(1)} %get-tuple-element.82.uraw, ...), custom_call_target="tpu_custom_call" | custom-call | tf_op jit(solution)/shard_map/pallas_call | solution.py:576
  135.0 16.6 %all_to_all.89 = f32[64,1,2176]{2,1,0:T(1,128)S(1)} all-to-all(f32[64,1,2176]{2,1,0:T(1,128)S(1)} %bitcast.50), channel_id=1, replica_groups=mesh['grp'=2,'shard_0'=4,'shard_1'=4,'shard_2'=4] {'shard_0','shard_1','..., dimensions={0} | all-to-all | bytes 1114112 | tf_op jit(solution)/shard_map/all_to_all | solution.py:506
  151.6 1.0 shard_map.84
  152.6 16.7 %all_to_all.90 = f32[64,1,2176]{2,1,0:T(1,128)S(1)} all-to-all(f32[64,1,2176]{2,1,0:T(1,128)S(1)} %bitcast.44), channel_id=1, replica_groups=mesh['grp'=2,'shard_0'=4,'shard_1'=4,'shard_2'=4] {'shard_0','shard_1','..., dimensions={0} | all-to-all | bytes 1114112 | tf_op jit(solution)/shard_map/all_to_all | solution.py:506
  169.3 2.4 %shard_map.85 = (f32[128,128]{1,0:T(8,128)S(1)}, f32[128,128]{1,0:T(8,128)S(1)}, f32[8,128]{1,0:T(8,128)S(1)}) custom-call(s32[128]{0:T(128)S(4)} %get-tuple-element.54.tab, s32[128]{0:T(128)S(4)} %get-tuple-element.59.tab2, f32[1088,128]{1,0:T(8,128)S(1)} %bitcast.36, f32[128,128]{1,0:T(8,128)S(1)} %get-tuple-element.91.uraw, ...), custom_call_target="tpu_custom_call" | custom-call | tf_op jit(solution)/shard_map/pallas_call | solution.py:595
  171.7 13.3 %all_to_all.91 = f32[128,1,128]{2,1,0:T(1,128)S(1)} all-to-all(f32[128,1,128]{2,1,0:T(1,128)S(1)} %bitcast.55), channel_id=1, replica_groups=mesh['grp'=2,'shard_0'=4,'shard_1'=4,'shard_2'=4] {'grp','shard_0','shar..., dimensions={0} | all-to-all | bytes 131072 | tf_op jit(solution)/shard_map/all_to_all | solution.py:602
  185.0 0.1 shard_map.86
  185.1 0.1 collective-permute-start.2
  185.2 1.2 collective-permute-done.2.theirs
  186.4 0.7 shard_map.87
Async XLA Ops:
  0.6 50.6 %collective-permute-start.1 = (f32[64,128,128]{2,1,0:T(8,128)}, f32[64,128,128]{2,1,0:T(8,128)S(1)}, u32[]{:S(2)}, u32[]{:S(2)}) collective-permute-start(f32[64,128,128]{2,1,0:T(8,128)} %blocks.1), channel_id=1, source_target_pairs={{0,64},{64,0},{1,65},{65,1},{2,66},{66,2},{3,67},{67,3},{4,68},{68... | collective-permute-start | bytes 12582920 | tf_op jit(solution)/shard_map/ppermute | solution.py:510
  0.7 28.6 %copy-start = (f32[2048,8]{0,1:T(8,128)S(1)}, f32[2048,8]{0,1:T(8,128)}, u32[]{:S(2)}) copy-start(f32[2048,8]{0,1:T(8,128)} %param.9) | copy-start | bytes 196612
  30.3 1.3 collective-permute-start
  51.2 2.0 %copy-start.1 = (f32[64,128,128]{2,1,0:T(8,128)}, f32[64,128,128]{2,1,0:T(8,128)S(1)}, u32[]{:S(2)}) copy-start(f32[64,128,128]{2,1,0:T(8,128)S(1)} %collective-permute-done.1.blocks) | copy-start | bytes 12582916
  185.1 1.3 collective-permute-start.2

commit v6 on v5

--- a/solution.py
+++ b/solution.py
@@ -25,6 +25,7 @@
 PART = RHS // 2
 LINES = 2 * ROWS
 VEC = COLS_OWN * PART
+ENDS = 2 * VEC + 3 * RHS + ROWS * PART
 
 f32 = jnp.float32
 bf16 = jnp.bfloat16
@@ -247,16 +248,10 @@
 
 def send_slots(cols, raw, msg):
     put_rows(msg, part_row(part_squares(raw[...])))
-
-    def step(g, carry):
-        for j in range(8):
-            o = g * 8 + j
-            for s in range(2 * CAP):
-                c = cols[s // CAP][o * CAP + s % CAP]
-                msg[pl.ds(o * MSG + s * PART, PART), :] = raw[pl.ds(c * PART, PART), :]
-        return carry
-
-    lax.fori_loop(0, OWNERS // 8, step, 0)
+    for o in range(OWNERS):
+        for s in range(2 * CAP):
+            at = cols[s // CAP][o * CAP + s % CAP]
+            msg[pl.ds(o * MSG + s * PART, PART), :] = raw[pl.ds(at, PART), :]
 
 
 def first_send_kernel(
@@ -268,8 +263,8 @@
     mine_cols = keep[pl.ds(VEC + RHS, 1), :]
     other_cols = theirs[pl.ds(VEC + RHS, 1), :]
     vtab[...] = theirs[pl.ds(VEC + RHS + 1, 1), :][0].astype(jnp.int32)
-    vcols0[...] = jnp.where(grp == 0, mine_cols, other_cols)[0].astype(jnp.int32)
-    vcols1[...] = jnp.where(grp == 0, other_cols, mine_cols)[0].astype(jnp.int32)
+    vcols0[...] = jnp.where(grp == 0, mine_cols, other_cols)[0].astype(jnp.int32) * PART
+    vcols1[...] = jnp.where(grp == 0, other_cols, mine_cols)[0].astype(jnp.int32) * PART
     copies = [
         pltpu.make_async_copy(vtab, tab, sem.at[0]),
         pltpu.make_async_copy(vcols0, cols0, sem.at[1]),
@@ -302,16 +297,11 @@
     for part in parts:
         part[...] = jnp.zeros((VEC, BS), f32)
 
-    def step(g, carry):
-        for j in range(8):
-            o = g * 8 + j
-            for s in range(2 * CAP):
-                span = pl.ds(cols[s // CAP][o * CAP + s % CAP] * PART, PART)
-                part = parts[s]
-                part[span, :] = part[span, :] + inc[pl.ds(o * MSG + s * PART, PART), :]
-        return carry
-
-    lax.fori_loop(0, OWNERS // 8, step, 0)
+    for o in range(OWNERS):
+        for s in range(2 * CAP):
+            span = pl.ds(cols[s // CAP][o * CAP + s % CAP], PART)
+            part = parts[s]
+            part[span, :] = part[span, :] + inc[pl.ds(o * MSG + s * PART, PART), :]
     total = (parts[0][...] + parts[1][...]) + (parts[2][...] + parts[3][...])
     n = VEC // RHS
     norm_left = jnp.sqrt(sum_rows(inc, part_column))
@@ -370,25 +360,21 @@
 def first_user_kernel(
     tab, tab2, inc, uraw, nleft, high, low, blocks,
     msg, lraw, nright, high2, low2,
-    other, us, bbuf, sem,
+    other, us,
 ):
-    for c in range(CHUNKS):
-        chunk_copy(blocks, bbuf, sem, c).start()
     norm_right = jnp.sqrt(sum_rows(inc, part_column))
     nright[...] = norm_right
     lraw[...] = jnp.zeros(lraw.shape, f32)
     other[...] = jnp.zeros(lraw.shape, f32)
     forward_all(tab, inc, high, low, (lraw, other))
-    for c in range(CHUNKS):
-        chunk_copy(blocks, bbuf, sem, c).wait()
-        for k in range(c * CHUNK, (c + 1) * CHUNK):
-            h, l = split(bbuf[k])
-            high2[k] = h
-            low2[k] = l
-            part = forward_block(inc[pl.ds(tab2[k], PART), :], h, l)
-            span = pl.ds(tab2[COUNT + k] * PART, PART)
-            ref = other if k % 2 else lraw
-            ref[span, :] = ref[span, :] + part
+    for k in range(COUNT):
+        h, l = split(blocks[k])
+        high2[k] = h
+        low2[k] = l
+        part = forward_block(inc[pl.ds(tab2[k], PART), :], h, l)
+        span = pl.ds(tab2[COUNT + k] * PART, PART)
+        ref = other if k % 2 else lraw
+        ref[span, :] = ref[span, :] + part
     left = left_of(lraw, other, uraw, nleft, norm_right)
     msg[...] = jnp.zeros((TALL, BS), f32)
     put_rows(msg, part_row(part_squares(left)))
@@ -415,62 +401,69 @@
 
 
 def last_user_kernel(
-    tab, tab2, inc, uraw, nleft, high, low, high2, low2, msg, lraw, nright, other
+    tab, tab2, inc, uraw, nleft, high, low, high2, low2, qprev, start, sol_in, search_in, scal_in,
+    msg, keep, send, lraw, other,
 ):
+    grp = lax.axis_index("grp")
     norm_right = jnp.sqrt(sum_rows(inc, part_column))
-    nright[...] = norm_right
     lraw[...] = jnp.zeros(lraw.shape, f32)
     other[...] = jnp.zeros(lraw.shape, f32)
-    forward_all(tab, inc, high, low, (lraw, other))
-    forward_all(tab2, inc, high2, low2, (lraw, other))
-    left = left_of(lraw, other, uraw, nleft, norm_right)
-    row = part_row(part_squares(left), lax.axis_index("grp") * PART)
-    msg[...] = jnp.broadcast_to(row, msg.shape)
-
-
-def final_kernel(rows, lraw, qprev, nright, sol_in, search_in, scal_in, start, keep, send):
-    grp = lax.axis_index("grp")
-    total = jnp.sum(rows[...], axis=0, keepdims=True)
-    norm_left = jnp.sqrt(part_column(total, grp * PART))
-    norm_right = nright[...]
-    size = ROWS * PART
-    n = size // RHS
-    for ref, at in ((keep, grp), (send, 1 - grp)):
-        left = lraw[pl.ds(pl.multiple_of(at * size, RHS), size), :] / tiled(norm_left, n)
-        ref[pl.ds(VEC + RHS, size), :] = left
     n = VEC // RHS
     radius = scal_in[pl.ds(0, RHS), :]
     cosine = scal_in[pl.ds(RHS, RHS), :]
     sine_term = scal_in[pl.ds(2 * RHS, RHS), :]
-    residual = scal_in[pl.ds(3 * RHS, RHS), :]
     vec = qprev[...] / tiled(norm_right, n)
     search = vec - tiled(sine_term * norm_right / radius, n) * search_in[...]
-    diag_bar = -cosine * norm_right
+    for ref in (keep, send):
+        ref[pl.ds(0, VEC), :] = sol_in[...]
+        ref[pl.ds(VEC, VEC), :] = search
+        ref[pl.ds(2 * VEC, RHS), :] = -cosine * norm_right
+        ref[pl.ds(2 * VEC + RHS, RHS), :] = scal_in[pl.ds(3 * RHS, RHS), :]
+        ref[pl.ds(2 * VEC + 2 * RHS, RHS), :] = start[...]
+    forward_all(tab, inc, high, low, (lraw, other))
+    forward_all(tab2, inc, high2, low2, (lraw, other))
+    left = left_of(lraw, other, uraw, nleft, norm_right)
+    row = part_row(part_squares(left), grp * PART)
+    msg[...] = jnp.broadcast_to(row, msg.shape)
+    size = ROWS * PART
+    for ref, at in ((keep, grp), (send, 1 - grp)):
+        ref[pl.ds(ENDS - size, size), :] = lraw[pl.ds(pl.multiple_of(at * size, RHS), size), :]
+
+
+def finished(total, ref, grp):
+    norm_left = jnp.sqrt(part_column(total, grp * PART))
+    size = ROWS * PART
+    left = ref[pl.ds(ENDS - size, size), :] / tiled(norm_left, size // RHS)
+    diag_bar = ref[pl.ds(2 * VEC, RHS), :]
+    residual = ref[pl.ds(2 * VEC + RHS, RHS), :]
     radius = jnp.sqrt(diag_bar * diag_bar + norm_left * norm_left)
     cosine = diag_bar / radius
     sine_term = norm_left / radius
-    sol = sol_in[...] + tiled(cosine * residual / radius, n) * search
-    rel = sine_term * residual / start[...]
-    for ref in (keep, send):
-        ref[pl.ds(0, VEC), :] = sol
-        ref[pl.ds(VEC, RHS), :] = rel
-
-
-def join_kernel(keep, theirs, sol, left, rel):
+    step = tiled(cosine * residual / radius, VEC // RHS)
+    sol = ref[pl.ds(0, VEC), :] + step * ref[pl.ds(VEC, VEC), :]
+    rel = sine_term * residual / ref[pl.ds(2 * VEC + 2 * RHS, RHS), :]
+    return sol, left, rel
+
+
+def final_kernel(rows, keep, theirs, sol, left, rel):
     grp = lax.axis_index("grp")
-
-    def joined(at):
-        mine = keep[pl.ds(at, PART), :]
-        other = theirs[pl.ds(at, PART), :]
+    total = jnp.sum(rows[...], axis=0, keepdims=True)
+    mine = finished(total, keep, grp)
+    other = finished(total, theirs, 1 - grp)
+
+    def join(ref, mine, other):
         first = jnp.where(grp == 0, mine, other)
         second = jnp.where(grp == 0, other, mine)
-        return jnp.concatenate([first, second], axis=0)
-
-    for c in range(COLS_OWN):
-        sol[pl.ds(c * RHS, RHS), :] = joined(c * PART)
-    for r in range(ROWS):
-        left[pl.ds(r * RHS, RHS), :] = joined(VEC + RHS + r * PART)
-    rel[...] = row_of(joined(VEC))[0, :RHS]
+        for c in range(mine.shape[0] // PART):
+            ref[pl.ds(c * RHS, PART), :] = first[c * PART : (c + 1) * PART]
+            ref[pl.ds(c * RHS + PART, PART), :] = second[c * PART : (c + 1) * PART]
+
+    join(sol, mine[0], other[0])
+    join(left, mine[1], other[1])
+    first = jnp.where(grp == 0, mine[2], other[2])
+    second = jnp.where(grp == 0, other[2], mine[2])
+    both = jnp.concatenate([first[:PART], second[:PART]], axis=0)
+    rel[...] = row_of(both)[0, :RHS]
 
 
 def shape(*dims, dtype=f32):
@@ -567,11 +560,11 @@
         if repeat == 0:
             msg, left, norm_right, high2, low2 = call(
                 first_user_kernel,
-                [SMEM] * 2 + [VMEM] * 5 + [HBM],
+                [SMEM] * 2 + [VMEM] * 6,
                 (msg_shape, left_shape, col8, terms, terms),
                 (VMEM,) * 5,
-                [LEFT, LEFTS2, BUFFER, SEMS],
-            )(*small(tab, tab2), inc, left, norm_left, *near(high, low), *far(blocks2))
+                [LEFT, LEFTS2],
+            )(*small(tab, tab2), inc, left, norm_left, *near(high, low, blocks2))
         else:
             msg, left, norm_right = call(
                 user_kernel,
@@ -592,20 +585,21 @@
         )(*small(cols0, cols1), inc, raw, norm_right, *tail)
         msg, raw, norm_left = outs[:3]
         state = outs[3:]
-    rows, left, norm_right = call(
+    ends = shape(ENDS, BS)
+    rows, keep, send = call(
         last_user_kernel,
-        [SMEM] * 2 + [VMEM] * 7,
-        (shape(2 * OWNERS, BS), left_shape, col8),
+        [SMEM] * 2 + [VMEM] * 12,
+        (shape(2 * OWNERS, BS), ends, ends),
         None,
-        [LEFT],
-    )(*small(tab, tab2), inc, left, norm_left, *near(high, low, high2, low2))
+        [LEFT] * 2,
+    )(
+        *small(tab, tab2), inc, left, norm_left, *near(high, low, high2, low2),
+        raw, start, *state,
+    )
+    theirs = swap(send)
     rows = lax.all_to_all(rows, GRP_SHARD, 0, 0, tiled=True)
-    ends = shape(VEC + RHS + ROWS * PART, BS)
-    keep, send = call(final_kernel, [VMEM] * 8, (ends, ends))(
-        rows, left, raw, norm_right, *state, start
-    )
     full = shape(COLS_OWN * RHS, BS)
-    sol, left, rel = call(join_kernel, [VMEM] * 2, (full, full, shape(RHS)))(keep, swap(send))
+    sol, left, rel = call(final_kernel, [VMEM] * 3, (full, full, shape(RHS)))(rows, keep, theirs)
 
     def tall(x):
         return x.reshape(COLS_OWN, RHS, BS).transpose(0, 2, 1).reshape(COLS_OWN * BS, RHS)

time: 189 us -> 182 us (0.963)
  Pallas kernels: 23.5 us -> 20.6 us
  local copies, waits for them, and re-layouts: 1.97 us -> 0.01 us
    pallas_call x4 -> x3, Pallas kernels: 8.74 us -> 6.74 us  [the longest x1 3.54 us: on_device(): call(first_user_kernel, [SMEM] * 2 + [VMEM] * 6, (msg_shape, left_shape,...]
    unnamed x4 -> x2, local copies, waits for them, and re-layouts: 1.97 us -> 0.01 us
  transfers between devices with their start and end apart: 3 -> 3, of which waited for: 2 -> 1; matrix products, arithmetic and copies ran while one was open for 0% -> 0% of each run, Pallas kernels for 3% -> 3%
where the time goes in v6:
time: 182 us; the launch traced here: 181 us
  blocking collectives  158 us (87%)
  Pallas kernels  20.6 us (11%)
    all_to_all x8, blocking collectives, exchange(): return lax.all_to_all(sent, SHARD, 0, 0, tiled=True).reshape(TALL, BS)  145 us
    all_to_all x1, blocking collectives, on_device(): rows = lax.all_to_all(rows, GRP_SHARD, 0, 0, tiled=True)  13.4 us
    pallas_call x2, Pallas kernels, on_device(): call(user_kernel, [SMEM] * 2 + [VMEM] * 7, (msg_shape, left_shape, col8),...  7.08 us
  transfers between devices with their start and end apart: 3, of which 1 were waited for; matrix products, arithmetic and copies ran while one was open for 0% of the time, Pallas kernels for 3%

profile of v6, /device:TPU:0, one launch (start us, length us, event | category | flops | bytes accessed | tf_op | source)
XLA Modules:
  0.0 180.9 jit_solution(14708521014732463361)
XLA Ops:
  0.6 0.1 collective-permute-start.1
  0.7 0.0 copy-start
  0.7 2.8 %shard_map.76 = (f32[1088,128]{1,0:T(8,128)S(1)}, s32[128]{0:T(128)S(4)}, f32[8,128]{1,0:T(8,128)S(1)}, bf16[64,128,128]{2,1,0:T(8,128)(2,1)S(1)}, bf16[64,128,128]{2,1,0:T(8,128)(2,1)S(1)}) custom-call(s32[64]{0:T(128)} %bitcast.56, s32[64]{0:T(128)} %row_in.1, s32[64]{0:T(128)} %col_in.1, f32[128,128]{1,0:T(8,128)} %bitcast.52, f32[64,128,128]{2,1,0:T(8,128)} %blocks.1), custom_call_target="tpu_custom_call" | custom-call | tf_op jit(solution)/shard_map/pallas_call | solution.py:530
  3.5 25.8 %all_to_all.83 = f32[64,1,2176]{2,1,0:T(1,128)S(1)} all-to-all(f32[64,1,2176]{2,1,0:T(1,128)S(1)} %bitcast.51), channel_id=1, replica_groups=mesh['grp'=2,'shard_0'=4,'shard_1'=4,'shard_2'=4] {'shard_0','shard_1','..., dimensions={0} | all-to-all | bytes 1114112 | tf_op jit(solution)/shard_map/all_to_all | solution.py:499
  29.3 0.0 copy-done
  29.3 1.0 shard_map.77
  30.3 0.1 collective-permute-start
  30.4 1.3 collective-permute-done.theirs
  31.7 0.8 shard_map.78
  32.5 18.5 %all_to_all.84 = f32[64,1,2176]{2,1,0:T(1,128)S(1)} all-to-all(f32[64,1,2176]{2,1,0:T(1,128)S(1)} %bitcast.46), channel_id=1, replica_groups=mesh['grp'=2,'shard_0'=4,'shard_1'=4,'shard_2'=4] {'shard_0','shard_1','..., dimensions={0} | all-to-all | bytes 1114112 | tf_op jit(solution)/shard_map/all_to_all | solution.py:499
  51.0 0.0 collective-permute-done.1.blocks
  51.0 3.5 %shard_map.79 = (f32[1088,128]{1,0:T(8,128)S(1)}, f32[128,128]{1,0:T(8,128)S(1)}, f32[8,128]{1,0:T(8,128)S(1)}, bf16[64,128,128]{2,1,0:T(8,128)(2,1)S(1)}, bf16[64,128,128]{2,1,0:T(8,128)(2,1)S(1)}) custom-call(s32[128]{0:T(128)S(4)} %get-tuple-element.52.tab, s32[128]{0:T(128)S(4)} %get-tuple-element.57.tab2, f32[1088,128]{1,0:T(8,128)S(1)} %bitcast.37, ...), custom_call_target="tpu_custom_call" | custom-call | tf_op jit(solution)/shard_map/pallas_call | solution.py:561
  54.5 17.1 %all_to_all.85 = f32[64,1,2176]{2,1,0:T(1,128)S(1)} all-to-all(f32[64,1,2176]{2,1,0:T(1,128)S(1)} %bitcast.48), channel_id=1, replica_groups=mesh['grp'=2,'shard_0'=4,'shard_1'=4,'shard_2'=4] {'shard_0','shard_1','..., dimensions={0} | all-to-all | bytes 1114112 | tf_op jit(solution)/shard_map/all_to_all | solution.py:499
  71.7 0.7 shard_map.80
  72.4 16.7 %all_to_all.86 = f32[64,1,2176]{2,1,0:T(1,128)S(1)} all-to-all(f32[64,1,2176]{2,1,0:T(1,128)S(1)} %bitcast.47), channel_id=1, replica_groups=mesh['grp'=2,'shard_0'=4,'shard_1'=4,'shard_2'=4] {'shard_0','shard_1','..., dimensions={0} | all-to-all | bytes 1114112 | tf_op jit(solution)/shard_map/all_to_all | solution.py:499
  89.1 3.5 %shard_map.81 = (f32[1088,128]{1,0:T(8,128)S(1)}, f32[128,128]{1,0:T(8,128)S(1)}, f32[8,128]{1,0:T(8,128)S(1)}) custom-call(s32[128]{0:T(128)S(4)} %get-tuple-element.52.tab, s32[128]{0:T(128)S(4)} %get-tuple-element.57.tab2, f32[1088,128]{1,0:T(8,128)S(1)} %bitcast.38, f32[128,128]{1,0:T(8,128)S(1)} %get-tuple-element.69.uraw, ...), custom_call_target="tpu_custom_call" | custom-call | tf_op jit(solution)/shard_map/pallas_call | solution.py:569
  92.6 16.7 %all_to_all.87 = f32[64,1,2176]{2,1,0:T(1,128)S(1)} all-to-all(f32[64,1,2176]{2,1,0:T(1,128)S(1)} %bitcast.49), channel_id=1, replica_groups=mesh['grp'=2,'shard_0'=4,'shard_1'=4,'shard_2'=4] {'shard_0','shard_1','..., dimensions={0} | all-to-all | bytes 1114112 | tf_op jit(solution)/shard_map/all_to_all | solution.py:499
  109.3 0.7 shard_map.82
  110.0 16.7 %all_to_all.88 = f32[64,1,2176]{2,1,0:T(1,128)S(1)} all-to-all(f32[64,1,2176]{2,1,0:T(1,128)S(1)} %bitcast.45), channel_id=1, replica_groups=mesh['grp'=2,'shard_0'=4,'shard_1'=4,'shard_2'=4] {'shard_0','shard_1','..., dimensions={0} | all-to-all | bytes 1114112 | tf_op jit(solution)/shard_map/all_to_all | solution.py:499
  126.7 3.5 %shard_map.83 = (f32[1088,128]{1,0:T(8,128)S(1)}, f32[128,128]{1,0:T(8,128)S(1)}, f32[8,128]{1,0:T(8,128)S(1)}) custom-call(s32[128]{0:T(128)S(4)} %get-tuple-element.52.tab, s32[128]{0:T(128)S(4)} %get-tuple-element.57.tab2, f32[1088,128]{1,0:T(8,128)S(1)} %bitcast.39, f32[128,128]{1,0:T(8,128)S(1)} %get-tuple-element.80.uraw, ...), custom_call_target="tpu_custom_call" | custom-call | tf_op jit(solution)/shard_map/pallas_call | solution.py:569
  130.2 16.7 %all_to_all.89 = f32[64,1,2176]{2,1,0:T(1,128)S(1)} all-to-all(f32[64,1,2176]{2,1,0:T(1,128)S(1)} %bitcast.50), channel_id=1, replica_groups=mesh['grp'=2,'shard_0'=4,'shard_1'=4,'shard_2'=4] {'shard_0','shard_1','..., dimensions={0} | all-to-all | bytes 1114112 | tf_op jit(solution)/shard_map/all_to_all | solution.py:499
  146.9 0.7 shard_map.84
  147.6 16.7 %all_to_all.90 = f32[64,1,2176]{2,1,0:T(1,128)S(1)} all-to-all(f32[64,1,2176]{2,1,0:T(1,128)S(1)} %bitcast.44), channel_id=1, replica_groups=mesh['grp'=2,'shard_0'=4,'shard_1'=4,'shard_2'=4] {'shard_0','shard_1','..., dimensions={0} | all-to-all | bytes 1114112 | tf_op jit(solution)/shard_map/all_to_all | solution.py:499
  164.2 2.4 %shard_map.85 = (f32[128,128]{1,0:T(8,128)S(1)}, f32[216,128]{1,0:T(8,128)S(1)}, f32[216,128]{1,0:T(8,128)S(1)}) custom-call(s32[128]{0:T(128)S(4)} %get-tuple-element.52.tab, s32[128]{0:T(128)S(4)} %get-tuple-element.57.tab2, f32[1088,128]{1,0:T(8,128)S(1)} %bitcast.36, f32[128,128]{1,0:T(8,128)S(1)} %get-tuple-element.89.uraw, ...), custom_call_target="tpu_custom_call" | custom-call | tf_op jit(solution)/shard_map/pallas_call | solution.py:589
  166.7 0.1 collective-permute-start.2
  166.7 13.4 %all_to_all.91 = f32[128,1,128]{2,1,0:T(1,128)S(1)} all-to-all(f32[128,1,128]{2,1,0:T(1,128)S(1)} %bitcast.55), channel_id=1, replica_groups=mesh['grp'=2,'shard_0'=4,'shard_1'=4,'shard_2'=4] {'grp','shard_0','shar..., dimensions={0} | all-to-all | bytes 131072 | tf_op jit(solution)/shard_map/all_to_all | solution.py:600
  180.1 0.0 collective-permute-done.2.theirs
  180.1 0.8 shard_map.86
Async XLA Ops:
  0.6 50.4 %collective-permute-start.1 = (f32[64,128,128]{2,1,0:T(8,128)}, f32[64,128,128]{2,1,0:T(8,128)S(1)}, u32[]{:S(2)}, u32[]{:S(2)}) collective-permute-start(f32[64,128,128]{2,1,0:T(8,128)} %blocks.1), channel_id=1, source_target_pairs={{0,64},{64,0},{1,65},{65,1},{2,66},{66,2},{3,67},{67,3},{4,68},{68... | collective-permute-start | bytes 12582920 | tf_op jit(solution)/shard_map/ppermute | solution.py:503
  0.7 28.6 %copy-start = (f32[2048,8]{0,1:T(8,128)S(1)}, f32[2048,8]{0,1:T(8,128)}, u32[]{:S(2)}) copy-start(f32[2048,8]{0,1:T(8,128)} %param.9) | copy-start | bytes 196612
  30.3 1.3 collective-permute-start
  166.7 13.5 %collective-permute-start.2 = (f32[216,128]{1,0:T(8,128)S(1)}, f32[216,128]{1,0:T(8,128)S(1)}, u32[]{:S(2)}, u32[]{:S(2)}) collective-permute-start(f32[216,128]{1,0:T(8,128)S(1)} %get-tuple-element.97), channel_id=1, source_target_pairs={{0,64},{64,0},{1,65},{65,1},{2,66},{66,2},{3,67},{67,3},{4,68},{68... | collective-permute-start | bytes 331784 | tf_op jit(solution)/shard_map/ppermute | solution.py:503

commit v7 on v6

--- a/solution.py
+++ b/solution.py
@@ -130,16 +130,16 @@
 
 
 def forward_block(piece, high, low):
-    rhs = jnp.concatenate([high, low], axis=1)
+    rhs = jnp.concatenate([high, low], axis=0)
     out = lax.dot_general(
-        stacked(piece), rhs, (((1,), (1,)), ((), ())), preferred_element_type=f32
+        stacked(piece), rhs, (((1,), (0,)), ((), ())), preferred_element_type=f32
     )
     return fold(out)
 
 
 def first_kernel(
     owner_in, row_in, col_in, right_in, blocks,
-    msg, tab, line_row, high, low,
+    msg, tab, line_row, high, low, high_t, low_t,
     bbuf, right, us, owner, row, col, taken, sem, little,
 ):
     loads = [
@@ -193,6 +193,7 @@
             high[k] = h
             low[k] = l
             adjoint_block(pos, line, us, h, l, msg)
+            high_t[k], low_t[k] = split(bbuf[k].T)
     line_row[...] = jnp.broadcast_to(listed, (RHS, BS))
 
 
@@ -358,19 +359,20 @@
 
 
 def first_user_kernel(
-    tab, tab2, inc, uraw, nleft, high, low, blocks,
-    msg, lraw, nright, high2, low2,
+    tab, tab2, inc, uraw, nleft, high, low, high_t, low_t, blocks,
+    msg, lraw, nright, high2, low2, high2_t, low2_t,
     other, us,
 ):
     norm_right = jnp.sqrt(sum_rows(inc, part_column))
     nright[...] = norm_right
     lraw[...] = jnp.zeros(lraw.shape, f32)
     other[...] = jnp.zeros(lraw.shape, f32)
-    forward_all(tab, inc, high, low, (lraw, other))
+    forward_all(tab, inc, high_t, low_t, (lraw, other))
     for k in range(COUNT):
-        h, l = split(blocks[k])
-        high2[k] = h
-        low2[k] = l
+        high2[k], low2[k] = split(blocks[k])
+        h, l = split(blocks[k].T)
+        high2_t[k] = h
+        low2_t[k] = l
         part = forward_block(inc[pl.ds(tab2[k], PART), :], h, l)
         span = pl.ds(tab2[COUNT + k] * PART, PART)
         ref = other if k % 2 else lraw
@@ -384,14 +386,15 @@
 
 
 def user_kernel(
-    tab, tab2, inc, uraw, nleft, high, low, high2, low2, msg, lraw, nright, other, us
+    tab, tab2, inc, uraw, nleft, high, low, high2, low2, high_t, low_t, high2_t, low2_t,
+    msg, lraw, nright, other, us,
 ):
     norm_right = jnp.sqrt(sum_rows(inc, part_column))
     nright[...] = norm_right
     lraw[...] = jnp.zeros(lraw.shape, f32)
     other[...] = jnp.zeros(lraw.shape, f32)
-    forward_all(tab, inc, high, low, (lraw, other))
-    forward_all(tab2, inc, high2, low2, (lraw, other))
+    forward_all(tab, inc, high_t, low_t, (lraw, other))
+    forward_all(tab2, inc, high2_t, low2_t, (lraw, other))
     left = left_of(lraw, other, uraw, nleft, norm_right)
     msg[...] = jnp.zeros((TALL, BS), f32)
     put_rows(msg, part_row(part_squares(left)))
@@ -527,11 +530,11 @@
     swapped = shape(VEC + 2 * RHS + ROWS * PART, BS)
 
     blocks2 = swap(blocks)
-    msg, tab, line_row, high, low = call(
+    msg, tab, line_row, high, low, high_t, low_t = call(
         first_kernel,
         [HBM] * 5,
-        (msg_shape, table, col8, terms, terms),
-        (VMEM, SMEM, VMEM, VMEM, VMEM),
+        (msg_shape, table, col8, terms, terms, terms, terms),
+        (VMEM, SMEM) + (VMEM,) * 5,
         [BUFFER, LEFT, LEFTS]
         + [pltpu.SMEM((COUNT,), jnp.int32)] * 4
         + [SEMS, pltpu.SemaphoreType.DMA((4,))],
@@ -558,21 +561,24 @@
         if repeat == ITERS - 1:
             break
         if repeat == 0:
-            msg, left, norm_right, high2, low2 = call(
+            msg, left, norm_right, high2, low2, high2_t, low2_t = call(
                 first_user_kernel,
-                [SMEM] * 2 + [VMEM] * 6,
-                (msg_shape, left_shape, col8, terms, terms),
-                (VMEM,) * 5,
+                [SMEM] * 2 + [VMEM] * 8,
+                (msg_shape, left_shape, col8, terms, terms, terms, terms),
+                (VMEM,) * 7,
                 [LEFT, LEFTS2],
-            )(*small(tab, tab2), inc, left, norm_left, *near(high, low, blocks2))
+            )(*small(tab, tab2), inc, left, norm_left, *near(high, low, high_t, low_t, blocks2))
         else:
             msg, left, norm_right = call(
                 user_kernel,
-                [SMEM] * 2 + [VMEM] * 7,
+                [SMEM] * 2 + [VMEM] * 11,
                 (msg_shape, left_shape, col8),
                 None,
                 [LEFT, LEFTS2],
-            )(*small(tab, tab2), inc, left, norm_left, *near(high, low, high2, low2))
+            )(
+                *small(tab, tab2), inc, left, norm_left,
+                *near(high, low, high2, low2, high_t, low_t, high2_t, low2_t),
+            )
         inc = exchange(msg)
         first = repeat == 0
         tail = (start,) if first else state
@@ -593,7 +599,7 @@
         None,
         [LEFT] * 2,
     )(
-        *small(tab, tab2), inc, left, norm_left, *near(high, low, high2, low2),
+        *small(tab, tab2), inc, left, norm_left, *near(high_t, low_t, high2_t, low2_t),
         raw, start, *state,
     )
     theirs = swap(send)

time: 182 us -> 178 us (0.978)
  Pallas kernels: 20.6 us -> 16.9 us
    pallas_call x4, Pallas kernels: 13.4 us -> 10.8 us  [the longest x2 4.95 us: on_device(): call(user_kernel, [SMEM] * 2 + [VMEM] * 11, (msg_shape, left_shape, col8)...]
where the time goes in v7:
time: 178 us; the launch traced here: 177 us
  blocking collectives  158 us (89%)
  Pallas kernels  16.9 us (9%)
    all_to_all x8, blocking collectives, exchange(): return lax.all_to_all(sent, SHARD, 0, 0, tiled=True).reshape(TALL, BS)  145 us
    all_to_all x1, blocking collectives, on_device(): rows = lax.all_to_all(rows, GRP_SHARD, 0, 0, tiled=True)  13.4 us
    pallas_call x2, Pallas kernels, on_device(): call(user_kernel, [SMEM] * 2 + [VMEM] * 11, (msg_shape, left_shape, col8)...  4.95 us
  transfers between devices with their start and end apart: 3, of which 1 were waited for; matrix products, arithmetic and copies ran while one was open for 0% of the time, Pallas kernels for 3%

profile of v7, /device:TPU:0, one launch (start us, length us, event | category | flops | bytes accessed | tf_op | source)
XLA Modules:
  0.0 177.2 jit_solution(5594549503467234697)
XLA Ops:
  0.6 0.1 collective-permute-start.1
  0.7 0.0 copy-start
  0.7 2.9 %shard_map.76 = (f32[1088,128]{1,0:T(8,128)S(1)}, s32[128]{0:T(128)S(4)}, f32[8,128]{1,0:T(8,128)S(1)}, bf16[64,128,128]{2,1,0:T(8,128)(2,1)S(1)}, bf16[64,128,1...) custom-call(s32[64]{0:T(128)} %bitcast.56, s32[64]{0:T(128)} %row_in.1, ...), custom_call_target="tpu_custom_call" | custom-call | tf_op jit(solution)/shard_map/pallas_call | solution.py:533
  3.7 25.8 %all_to_all.83 = f32[64,1,2176]{2,1,0:T(1,128)S(1)} all-to-all(f32[64,1,2176]{2,1,0:T(1,128)S(1)} %bitcast.50), channel_id=1, replica_groups=mesh['grp'=2,'shard_0'=4,'shard_1'=4,'shard_2'=4] {'shard_0','shard_1','..., dimensions={0} | all-to-all | bytes 1114112 | tf_op jit(solution)/shard_map/all_to_all | solution.py:502
  29.4 0.0 copy-done
  29.4 1.0 shard_map.77
  30.5 0.1 collective-permute-start
  30.6 1.3 collective-permute-done.theirs
  31.8 0.8 shard_map.78
  32.6 18.5 %all_to_all.84 = f32[64,1,2176]{2,1,0:T(1,128)S(1)} all-to-all(f32[64,1,2176]{2,1,0:T(1,128)S(1)} %bitcast.48), channel_id=1, replica_groups=mesh['grp'=2,'shard_0'=4,'shard_1'=4,'shard_2'=4] {'shard_0','shard_1','..., dimensions={0} | all-to-all | bytes 1114112 | tf_op jit(solution)/shard_map/all_to_all | solution.py:502
  51.1 0.0 collective-permute-done.1.blocks
  51.1 2.9 %shard_map.79 = (f32[1088,128]{1,0:T(8,128)S(1)}, f32[128,128]{1,0:T(8,128)S(1)}, f32[8,128]{1,0:T(8,128)S(1)}, bf16[64,128,128]{2,1,0:T(8,128)(2,1)S(1)}, bf16[...) custom-call(s32[128]{0:T(128)S(4)} %get-tuple-element.56.tab, ...), custom_call_target="tpu_custom_call" | custom-call | tf_op jit(solution)/shard_map/pallas_call | solution.py:564
  54.1 17.1 %all_to_all.85 = f32[64,1,2176]{2,1,0:T(1,128)S(1)} all-to-all(f32[64,1,2176]{2,1,0:T(1,128)S(1)} %bitcast.46), channel_id=1, replica_groups=mesh['grp'=2,'shard_0'=4,'shard_1'=4,'shard_2'=4] {'shard_0','shard_1','..., dimensions={0} | all-to-all | bytes 1114112 | tf_op jit(solution)/shard_map/all_to_all | solution.py:502
  71.2 0.7 shard_map.80
  72.0 16.6 %all_to_all.86 = f32[64,1,2176]{2,1,0:T(1,128)S(1)} all-to-all(f32[64,1,2176]{2,1,0:T(1,128)S(1)} %bitcast.49), channel_id=1, replica_groups=mesh['grp'=2,'shard_0'=4,'shard_1'=4,'shard_2'=4] {'shard_0','shard_1','..., dimensions={0} | all-to-all | bytes 1114112 | tf_op jit(solution)/shard_map/all_to_all | solution.py:502
  88.6 2.5 %shard_map.81 = (f32[1088,128]{1,0:T(8,128)S(1)}, f32[128,128]{1,0:T(8,128)S(1)}, f32[8,128]{1,0:T(8,128)S(1)}) custom-call(s32[128]{0:T(128)S(4)} %get-tuple-element.56.tab, s32[128]{0:T(128)S(4)} %get-tuple-element.61.tab2, f32[1088,128]{1,0:T(8,128)S(1)} %bitcast.39, f32[128,128]{1,0:T(8,128)S(1)} %get-tuple-element.75.uraw, ...), custom_call_target="tpu_custom_call" | custom-call | tf_op jit(solution)/shard_map/pallas_call | solution.py:572
  91.1 16.6 %all_to_all.87 = f32[64,1,2176]{2,1,0:T(1,128)S(1)} all-to-all(f32[64,1,2176]{2,1,0:T(1,128)S(1)} %bitcast.51), channel_id=1, replica_groups=mesh['grp'=2,'shard_0'=4,'shard_1'=4,'shard_2'=4] {'shard_0','shard_1','..., dimensions={0} | all-to-all | bytes 1114112 | tf_op jit(solution)/shard_map/all_to_all | solution.py:502
  107.7 0.7 shard_map.82
  108.5 16.6 %all_to_all.88 = f32[64,1,2176]{2,1,0:T(1,128)S(1)} all-to-all(f32[64,1,2176]{2,1,0:T(1,128)S(1)} %bitcast.45), channel_id=1, replica_groups=mesh['grp'=2,'shard_0'=4,'shard_1'=4,'shard_2'=4] {'shard_0','shard_1','..., dimensions={0} | all-to-all | bytes 1114112 | tf_op jit(solution)/shard_map/all_to_all | solution.py:502
  125.1 2.5 %shard_map.83 = (f32[1088,128]{1,0:T(8,128)S(1)}, f32[128,128]{1,0:T(8,128)S(1)}, f32[8,128]{1,0:T(8,128)S(1)}) custom-call(s32[128]{0:T(128)S(4)} %get-tuple-element.56.tab, s32[128]{0:T(128)S(4)} %get-tuple-element.61.tab2, f32[1088,128]{1,0:T(8,128)S(1)} %bitcast.38, f32[128,128]{1,0:T(8,128)S(1)} %get-tuple-element.88.uraw, ...), custom_call_target="tpu_custom_call" | custom-call | tf_op jit(solution)/shard_map/pallas_call | solution.py:572
  127.6 16.6 %all_to_all.89 = f32[64,1,2176]{2,1,0:T(1,128)S(1)} all-to-all(f32[64,1,2176]{2,1,0:T(1,128)S(1)} %bitcast.47), channel_id=1, replica_groups=mesh['grp'=2,'shard_0'=4,'shard_1'=4,'shard_2'=4] {'shard_0','shard_1','..., dimensions={0} | all-to-all | bytes 1114112 | tf_op jit(solution)/shard_map/all_to_all | solution.py:502
  144.2 0.7 shard_map.84
  145.0 16.6 %all_to_all.90 = f32[64,1,2176]{2,1,0:T(1,128)S(1)} all-to-all(f32[64,1,2176]{2,1,0:T(1,128)S(1)} %bitcast.44), channel_id=1, replica_groups=mesh['grp'=2,'shard_0'=4,'shard_1'=4,'shard_2'=4] {'shard_0','shard_1','..., dimensions={0} | all-to-all | bytes 1114112 | tf_op jit(solution)/shard_map/all_to_all | solution.py:502
  161.6 1.4 shard_map.85
  163.0 0.1 collective-permute-start.2
  163.1 13.4 %all_to_all.91 = f32[128,1,128]{2,1,0:T(1,128)S(1)} all-to-all(f32[128,1,128]{2,1,0:T(1,128)S(1)} %bitcast.55), channel_id=1, replica_groups=mesh['grp'=2,'shard_0'=4,'shard_1'=4,'shard_2'=4] {'grp','shard_0','shar..., dimensions={0} | all-to-all | bytes 131072 | tf_op jit(solution)/shard_map/all_to_all | solution.py:606
  176.4 0.0 collective-permute-done.2.theirs
  176.4 0.8 shard_map.86
Async XLA Ops:
  0.6 50.5 %collective-permute-start.1 = (f32[64,128,128]{2,1,0:T(8,128)}, f32[64,128,128]{2,1,0:T(8,128)S(1)}, u32[]{:S(2)}, u32[]{:S(2)}) collective-permute-start(f32[64,128,128]{2,1,0:T(8,128)} %blocks.1), channel_id=1, source_target_pairs={{0,64},{64,0},{1,65},{65,1},{2,66},{66,2},{3,67},{67,3},{4,68},{68... | collective-permute-start | bytes 12582920 | tf_op jit(solution)/shard_map/ppermute | solution.py:506
  0.7 28.7 %copy-start = (f32[2048,8]{0,1:T(8,128)S(1)}, f32[2048,8]{0,1:T(8,128)}, u32[]{:S(2)}) copy-start(f32[2048,8]{0,1:T(8,128)} %param.9) | copy-start | bytes 196612
  30.5 1.3 collective-permute-start
  163.0 13.4 %collective-permute-start.2 = (f32[216,128]{1,0:T(8,128)S(1)}, f32[216,128]{1,0:T(8,128)S(1)}, u32[]{:S(2)}, u32[]{:S(2)}) collective-permute-start(f32[216,128]{1,0:T(8,128)S(1)} %get-tuple-element.105), channel_id=1, source_target_pairs={{0,64},{64,0},{1,65},{65,1},{2,66},{66,2},{3,67},{67,3},{4,68},{68... | collective-permute-start | bytes 331784 | tf_op jit(solution)/shard_map/ppermute | solution.py:506

commit v8 on v7

--- a/solution.py
+++ b/solution.py
@@ -24,6 +24,7 @@
 CHUNKS = COUNT // CHUNK
 PART = RHS // 2
 LINES = 2 * ROWS
+STAGGER = 3000
 VEC = COLS_OWN * PART
 ENDS = 2 * VEC + 3 * RHS + ROWS * PART
 
@@ -232,16 +233,11 @@
         halves(VEC + 2 * RHS + r * PART, right[pl.ds(r * RHS, RHS), :])
     copy.wait()
 
-    def step(g, carry):
-        for j in range(8):
-            o = g * 8 + j
-            for s in range(CAP):
-                span = pl.ds(pl.multiple_of(cols[o * CAP + s] * RHS, RHS), RHS)
-                part = parts[(2 * j + s) % len(parts)]
-                part[span, :] = part[span, :] + inc[pl.ds(o * MSG + s * RHS, RHS), :]
-        return carry
-
-    lax.fori_loop(0, OWNERS // 8, step, 0)
+    for o in range(OWNERS):
+        for s in range(CAP):
+            span = pl.ds(pl.multiple_of(cols[o * CAP + s] * RHS, RHS), RHS)
+            part = parts[(2 * o + s) % len(parts)]
+            part[span, :] = part[span, :] + inc[pl.ds(o * MSG + s * RHS, RHS), :]
     for c in range(COLS_OWN):
         span = pl.ds(c * RHS, RHS)
         halves(c * PART, (p0[span, :] + p1[span, :]) + (p2[span, :] + p3[span, :]))
@@ -286,6 +282,10 @@
     for copy in copies:
         copy.wait()
     send_slots((cols0, cols1), raw, msg)
+
+    @pl.when(grp == 1)
+    def _():
+        pl.delay(STAGGER)
 
 
 def send_kernel(first, cols0, cols1, inc, qprev, nright, *refs):

time: 178 us -> 182 us (1.022)
  blocking collectives: 158 us -> 162 us
    all_to_all x8, blocking collectives: 145 us -> 148 us  [exchange(): return lax.all_to_all(sent, SHARD, 0, 0, tiled=True).reshape(TALL, BS)]
where the time goes in v8:
time: 182 us; the launch traced here: 181 us
  blocking collectives  162 us (89%)
  Pallas kernels  16.9 us (9%)
    all_to_all x8, blocking collectives, exchange(): return lax.all_to_all(sent, SHARD, 0, 0, tiled=True).reshape(TALL, BS)  148 us
    all_to_all x1, blocking collectives, on_device(): rows = lax.all_to_all(rows, GRP_SHARD, 0, 0, tiled=True)  13.4 us
    pallas_call x2, Pallas kernels, on_device(): call(user_kernel, [SMEM] * 2 + [VMEM] * 11, (msg_shape, left_shape, col8)...  4.95 us
  transfers between devices with their start and end apart: 3, of which 1 were waited for; matrix products, arithmetic and copies ran while one was open for 0% of the time, Pallas kernels for 3%

profile of v8, /device:TPU:0, one launch (start us, length us, event | category | flops | bytes accessed | tf_op | source)
XLA Modules:
  0.0 180.8 jit_solution(8100554038516506636)
XLA Ops:
  0.6 0.1 collective-permute-start.1
  0.7 0.0 copy-start
  0.7 2.9 %shard_map.76 = (f32[1088,128]{1,0:T(8,128)S(1)}, s32[128]{0:T(128)S(4)}, f32[8,128]{1,0:T(8,128)S(1)}, bf16[64,128,128]{2,1,0:T(8,128)(2,1)S(1)}, bf16[64,128,1...) custom-call(s32[64]{0:T(128)} %bitcast.56, s32[64]{0:T(128)} %row_in.1, ...), custom_call_target="tpu_custom_call" | custom-call | tf_op jit(solution)/shard_map/pallas_call | solution.py:533
  3.7 25.8 %all_to_all.83 = f32[64,1,2176]{2,1,0:T(1,128)S(1)} all-to-all(f32[64,1,2176]{2,1,0:T(1,128)S(1)} %bitcast.50), channel_id=1, replica_groups=mesh['grp'=2,'shard_0'=4,'shard_1'=4,'shard_2'=4] {'shard_0','shard_1','..., dimensions={0} | all-to-all | bytes 1114112 | tf_op jit(solution)/shard_map/all_to_all | solution.py:502
  29.4 0.0 copy-done
  29.4 1.0 shard_map.77
  30.5 0.1 collective-permute-start
  30.6 1.3 collective-permute-done.theirs
  31.8 0.8 shard_map.78
  32.6 17.7 %all_to_all.84 = f32[64,1,2176]{2,1,0:T(1,128)S(1)} all-to-all(f32[64,1,2176]{2,1,0:T(1,128)S(1)} %bitcast.48), channel_id=1, replica_groups=mesh['grp'=2,'shard_0'=4,'shard_1'=4,'shard_2'=4] {'shard_0','shard_1','..., dimensions={0} | all-to-all | bytes 1114112 | tf_op jit(solution)/shard_map/all_to_all | solution.py:502
  50.2 0.0 collective-permute-done.1.blocks
  50.2 2.9 %shard_map.79 = (f32[1088,128]{1,0:T(8,128)S(1)}, f32[128,128]{1,0:T(8,128)S(1)}, f32[8,128]{1,0:T(8,128)S(1)}, bf16[64,128,128]{2,1,0:T(8,128)(2,1)S(1)}, bf16[...) custom-call(s32[128]{0:T(128)S(4)} %get-tuple-element.56.tab, ...), custom_call_target="tpu_custom_call" | custom-call | tf_op jit(solution)/shard_map/pallas_call | solution.py:564
  53.2 18.9 %all_to_all.85 = f32[64,1,2176]{2,1,0:T(1,128)S(1)} all-to-all(f32[64,1,2176]{2,1,0:T(1,128)S(1)} %bitcast.46), channel_id=1, replica_groups=mesh['grp'=2,'shard_0'=4,'shard_1'=4,'shard_2'=4] {'shard_0','shard_1','..., dimensions={0} | all-to-all | bytes 1114112 | tf_op jit(solution)/shard_map/all_to_all | solution.py:502
  72.1 0.7 shard_map.80
  72.8 18.8 %all_to_all.86 = f32[64,1,2176]{2,1,0:T(1,128)S(1)} all-to-all(f32[64,1,2176]{2,1,0:T(1,128)S(1)} %bitcast.49), channel_id=1, replica_groups=mesh['grp'=2,'shard_0'=4,'shard_1'=4,'shard_2'=4] {'shard_0','shard_1','..., dimensions={0} | all-to-all | bytes 1114112 | tf_op jit(solution)/shard_map/all_to_all | solution.py:502
  91.6 2.5 %shard_map.81 = (f32[1088,128]{1,0:T(8,128)S(1)}, f32[128,128]{1,0:T(8,128)S(1)}, f32[8,128]{1,0:T(8,128)S(1)}) custom-call(s32[128]{0:T(128)S(4)} %get-tuple-element.56.tab, s32[128]{0:T(128)S(4)} %get-tuple-element.61.tab2, f32[1088,128]{1,0:T(8,128)S(1)} %bitcast.39, f32[128,128]{1,0:T(8,128)S(1)} %get-tuple-element.75.uraw, ...), custom_call_target="tpu_custom_call" | custom-call | tf_op jit(solution)/shard_map/pallas_call | solution.py:572
  94.1 17.4 %all_to_all.87 = f32[64,1,2176]{2,1,0:T(1,128)S(1)} all-to-all(f32[64,1,2176]{2,1,0:T(1,128)S(1)} %bitcast.51), channel_id=1, replica_groups=mesh['grp'=2,'shard_0'=4,'shard_1'=4,'shard_2'=4] {'shard_0','shard_1','..., dimensions={0} | all-to-all | bytes 1114112 | tf_op jit(solution)/shard_map/all_to_all | solution.py:502
  111.5 0.7 shard_map.82
  112.3 16.6 %all_to_all.88 = f32[64,1,2176]{2,1,0:T(1,128)S(1)} all-to-all(f32[64,1,2176]{2,1,0:T(1,128)S(1)} %bitcast.45), channel_id=1, replica_groups=mesh['grp'=2,'shard_0'=4,'shard_1'=4,'shard_2'=4] {'shard_0','shard_1','..., dimensions={0} | all-to-all | bytes 1114112 | tf_op jit(solution)/shard_map/all_to_all | solution.py:502
  128.8 2.5 %shard_map.83 = (f32[1088,128]{1,0:T(8,128)S(1)}, f32[128,128]{1,0:T(8,128)S(1)}, f32[8,128]{1,0:T(8,128)S(1)}) custom-call(s32[128]{0:T(128)S(4)} %get-tuple-element.56.tab, s32[128]{0:T(128)S(4)} %get-tuple-element.61.tab2, f32[1088,128]{1,0:T(8,128)S(1)} %bitcast.38, f32[128,128]{1,0:T(8,128)S(1)} %get-tuple-element.88.uraw, ...), custom_call_target="tpu_custom_call" | custom-call | tf_op jit(solution)/shard_map/pallas_call | solution.py:572
  131.3 16.6 %all_to_all.89 = f32[64,1,2176]{2,1,0:T(1,128)S(1)} all-to-all(f32[64,1,2176]{2,1,0:T(1,128)S(1)} %bitcast.47), channel_id=1, replica_groups=mesh['grp'=2,'shard_0'=4,'shard_1'=4,'shard_2'=4] {'shard_0','shard_1','..., dimensions={0} | all-to-all | bytes 1114112 | tf_op jit(solution)/shard_map/all_to_all | solution.py:502
  148.0 0.7 shard_map.84
  148.7 16.6 %all_to_all.90 = f32[64,1,2176]{2,1,0:T(1,128)S(1)} all-to-all(f32[64,1,2176]{2,1,0:T(1,128)S(1)} %bitcast.44), channel_id=1, replica_groups=mesh['grp'=2,'shard_0'=4,'shard_1'=4,'shard_2'=4] {'shard_0','shard_1','..., dimensions={0} | all-to-all | bytes 1114112 | tf_op jit(solution)/shard_map/all_to_all | solution.py:502
  165.3 1.4 shard_map.85
  166.6 0.1 collective-permute-start.2
  166.7 13.4 %all_to_all.91 = f32[128,1,128]{2,1,0:T(1,128)S(1)} all-to-all(f32[128,1,128]{2,1,0:T(1,128)S(1)} %bitcast.55), channel_id=1, replica_groups=mesh['grp'=2,'shard_0'=4,'shard_1'=4,'shard_2'=4] {'grp','shard_0','shar..., dimensions={0} | all-to-all | bytes 131072 | tf_op jit(solution)/shard_map/all_to_all | solution.py:606
  180.1 0.0 collective-permute-done.2.theirs
  180.1 0.8 shard_map.86
Async XLA Ops:
  0.6 49.6 %collective-permute-start.1 = (f32[64,128,128]{2,1,0:T(8,128)}, f32[64,128,128]{2,1,0:T(8,128)S(1)}, u32[]{:S(2)}, u32[]{:S(2)}) collective-permute-start(f32[64,128,128]{2,1,0:T(8,128)} %blocks.1), channel_id=1, source_target_pairs={{0,64},{64,0},{1,65},{65,1},{2,66},{66,2},{3,67},{67,3},{4,68},{68... | collective-permute-start | bytes 12582920 | tf_op jit(solution)/shard_map/ppermute | solution.py:506
  0.7 28.7 %copy-start = (f32[2048,8]{0,1:T(8,128)S(1)}, f32[2048,8]{0,1:T(8,128)}, u32[]{:S(2)}) copy-start(f32[2048,8]{0,1:T(8,128)} %param.9) | copy-start | bytes 196612
  30.5 1.3 collective-permute-start
  166.6 13.4 %collective-permute-start.2 = (f32[216,128]{1,0:T(8,128)S(1)}, f32[216,128]{1,0:T(8,128)S(1)}, u32[]{:S(2)}, u32[]{:S(2)}) collective-permute-start(f32[216,128]{1,0:T(8,128)S(1)} %get-tuple-element.105), channel_id=1, source_target_pairs={{0,64},{64,0},{1,65},{65,1},{2,66},{66,2},{3,67},{67,3},{4,68},{68... | collective-permute-start | bytes 331784 | tf_op jit(solution)/shard_map/ppermute | solution.py:506

commit v9 on v8

--- a/solution.py
+++ b/solution.py
@@ -24,7 +24,6 @@
 CHUNKS = COUNT // CHUNK
 PART = RHS // 2
 LINES = 2 * ROWS
-STAGGER = 3000
 VEC = COLS_OWN * PART
 ENDS = 2 * VEC + 3 * RHS + ROWS * PART
 
@@ -181,7 +180,7 @@
             rank = taken[o]
             taken[o] = rank + 1
             pos = o * MSG + rank * RHS
-            line = lax.rem(row[k], ROWS)
+            line = row[k] & (ROWS - 1)
             place = o * MSG + grp * (CAP * PART) + rank * PART
             here = line + grp * ROWS
             tab[k] = place
@@ -194,7 +193,8 @@
             high[k] = h
             low[k] = l
             adjoint_block(pos, line, us, h, l, msg)
-            high_t[k], low_t[k] = split(bbuf[k].T)
+            high_t[k] = h.T
+            low_t[k] = l.T
     line_row[...] = jnp.broadcast_to(listed, (RHS, BS))
 
 
@@ -282,10 +282,6 @@
     for copy in copies:
         copy.wait()
     send_slots((cols0, cols1), raw, msg)
-
-    @pl.when(grp == 1)
-    def _():
-        pl.delay(STAGGER)
 
 
 def send_kernel(first, cols0, cols1, inc, qprev, nright, *refs):
@@ -369,8 +365,10 @@
     other[...] = jnp.zeros(lraw.shape, f32)
     forward_all(tab, inc, high_t, low_t, (lraw, other))
     for k in range(COUNT):
-        high2[k], low2[k] = split(blocks[k])
-        h, l = split(blocks[k].T)
+        h, l = split(blocks[k])
+        high2[k] = h
+        low2[k] = l
+        h, l = h.T, l.T
         high2_t[k] = h
         low2_t[k] = l
         part = forward_block(inc[pl.ds(tab2[k], PART), :], h, l)

time: 182 us -> 178 us (0.978)
  blocking collectives: 162 us -> 158 us
    all_to_all x8, blocking collectives: 148 us -> 145 us  [exchange(): return lax.all_to_all(sent, SHARD, 0, 0, tiled=True).reshape(TALL, BS)]
where the time goes in v9:
time: 178 us; the launch traced here: 177 us
  blocking collectives  158 us (89%)
  Pallas kernels  16.7 us (9%)
    all_to_all x8, blocking collectives, exchange(): return lax.all_to_all(sent, SHARD, 0, 0, tiled=True).reshape(TALL, BS)  145 us
    all_to_all x1, blocking collectives, on_device(): rows = lax.all_to_all(rows, GRP_SHARD, 0, 0, tiled=True)  13.4 us
    pallas_call x2, Pallas kernels, on_device(): call(user_kernel, [SMEM] * 2 + [VMEM] * 11, (msg_shape, left_shape, col8)...  4.96 us
  transfers between devices with their start and end apart: 3, of which 1 were waited for; matrix products, arithmetic and copies ran while one was open for 0% of the time, Pallas kernels for 3%

profile of v9, /device:TPU:0, one launch (start us, length us, event | category | flops | bytes accessed | tf_op | source)
XLA Modules:
  0.0 177.0 jit_solution(1717586698790625563)
XLA Ops:
  0.6 0.1 collective-permute-start.1
  0.7 0.0 copy-start
  0.7 2.8 %shard_map.76 = (f32[1088,128]{1,0:T(8,128)S(1)}, s32[128]{0:T(128)S(4)}, f32[8,128]{1,0:T(8,128)S(1)}, bf16[64,128,128]{2,1,0:T(8,128)(2,1)S(1)}, bf16[64,128,1...) custom-call(s32[64]{0:T(128)} %bitcast.56, s32[64]{0:T(128)} %row_in.1, ...), custom_call_target="tpu_custom_call" | custom-call | tf_op jit(solution)/shard_map/pallas_call | solution.py:531
  3.6 25.8 %all_to_all.83 = f32[64,1,2176]{2,1,0:T(1,128)S(1)} all-to-all(f32[64,1,2176]{2,1,0:T(1,128)S(1)} %bitcast.50), channel_id=1, replica_groups=mesh['grp'=2,'shard_0'=4,'shard_1'=4,'shard_2'=4] {'shard_0','shard_1','..., dimensions={0} | all-to-all | bytes 1114112 | tf_op jit(solution)/shard_map/all_to_all | solution.py:500
  29.4 0.0 copy-done
  29.4 1.0 shard_map.77
  30.4 0.1 collective-permute-start
  30.5 1.3 collective-permute-done.theirs
  31.7 0.8 shard_map.78
  32.5 18.5 %all_to_all.84 = f32[64,1,2176]{2,1,0:T(1,128)S(1)} all-to-all(f32[64,1,2176]{2,1,0:T(1,128)S(1)} %bitcast.48), channel_id=1, replica_groups=mesh['grp'=2,'shard_0'=4,'shard_1'=4,'shard_2'=4] {'shard_0','shard_1','..., dimensions={0} | all-to-all | bytes 1114112 | tf_op jit(solution)/shard_map/all_to_all | solution.py:500
  51.1 0.0 collective-permute-done.1.blocks
  51.1 2.8 %shard_map.79 = (f32[1088,128]{1,0:T(8,128)S(1)}, f32[128,128]{1,0:T(8,128)S(1)}, f32[8,128]{1,0:T(8,128)S(1)}, bf16[64,128,128]{2,1,0:T(8,128)(2,1)S(1)}, bf16[...) custom-call(s32[128]{0:T(128)S(4)} %get-tuple-element.56.tab, ...), custom_call_target="tpu_custom_call" | custom-call | tf_op jit(solution)/shard_map/pallas_call | solution.py:562
  53.9 17.1 %all_to_all.85 = f32[64,1,2176]{2,1,0:T(1,128)S(1)} all-to-all(f32[64,1,2176]{2,1,0:T(1,128)S(1)} %bitcast.46), channel_id=1, replica_groups=mesh['grp'=2,'shard_0'=4,'shard_1'=4,'shard_2'=4] {'shard_0','shard_1','..., dimensions={0} | all-to-all | bytes 1114112 | tf_op jit(solution)/shard_map/all_to_all | solution.py:500
  71.0 0.7 shard_map.80
  71.8 16.7 %all_to_all.86 = f32[64,1,2176]{2,1,0:T(1,128)S(1)} all-to-all(f32[64,1,2176]{2,1,0:T(1,128)S(1)} %bitcast.49), channel_id=1, replica_groups=mesh['grp'=2,'shard_0'=4,'shard_1'=4,'shard_2'=4] {'shard_0','shard_1','..., dimensions={0} | all-to-all | bytes 1114112 | tf_op jit(solution)/shard_map/all_to_all | solution.py:500
  88.4 2.5 %shard_map.81 = (f32[1088,128]{1,0:T(8,128)S(1)}, f32[128,128]{1,0:T(8,128)S(1)}, f32[8,128]{1,0:T(8,128)S(1)}) custom-call(s32[128]{0:T(128)S(4)} %get-tuple-element.56.tab, s32[128]{0:T(128)S(4)} %get-tuple-element.61.tab2, f32[1088,128]{1,0:T(8,128)S(1)} %bitcast.39, f32[128,128]{1,0:T(8,128)S(1)} %get-tuple-element.75.uraw, ...), custom_call_target="tpu_custom_call" | custom-call | tf_op jit(solution)/shard_map/pallas_call | solution.py:570
  90.9 16.6 %all_to_all.87 = f32[64,1,2176]{2,1,0:T(1,128)S(1)} all-to-all(f32[64,1,2176]{2,1,0:T(1,128)S(1)} %bitcast.51), channel_id=1, replica_groups=mesh['grp'=2,'shard_0'=4,'shard_1'=4,'shard_2'=4] {'shard_0','shard_1','..., dimensions={0} | all-to-all | bytes 1114112 | tf_op jit(solution)/shard_map/all_to_all | solution.py:500
  107.5 0.7 shard_map.82
  108.3 16.7 %all_to_all.88 = f32[64,1,2176]{2,1,0:T(1,128)S(1)} all-to-all(f32[64,1,2176]{2,1,0:T(1,128)S(1)} %bitcast.45), channel_id=1, replica_groups=mesh['grp'=2,'shard_0'=4,'shard_1'=4,'shard_2'=4] {'shard_0','shard_1','..., dimensions={0} | all-to-all | bytes 1114112 | tf_op jit(solution)/shard_map/all_to_all | solution.py:500
  124.9 2.5 %shard_map.83 = (f32[1088,128]{1,0:T(8,128)S(1)}, f32[128,128]{1,0:T(8,128)S(1)}, f32[8,128]{1,0:T(8,128)S(1)}) custom-call(s32[128]{0:T(128)S(4)} %get-tuple-element.56.tab, s32[128]{0:T(128)S(4)} %get-tuple-element.61.tab2, f32[1088,128]{1,0:T(8,128)S(1)} %bitcast.38, f32[128,128]{1,0:T(8,128)S(1)} %get-tuple-element.88.uraw, ...), custom_call_target="tpu_custom_call" | custom-call | tf_op jit(solution)/shard_map/pallas_call | solution.py:570
  127.4 16.6 %all_to_all.89 = f32[64,1,2176]{2,1,0:T(1,128)S(1)} all-to-all(f32[64,1,2176]{2,1,0:T(1,128)S(1)} %bitcast.47), channel_id=1, replica_groups=mesh['grp'=2,'shard_0'=4,'shard_1'=4,'shard_2'=4] {'shard_0','shard_1','..., dimensions={0} | all-to-all | bytes 1114112 | tf_op jit(solution)/shard_map/all_to_all | solution.py:500
  144.0 0.7 shard_map.84
  144.8 16.7 %all_to_all.90 = f32[64,1,2176]{2,1,0:T(1,128)S(1)} all-to-all(f32[64,1,2176]{2,1,0:T(1,128)S(1)} %bitcast.44), channel_id=1, replica_groups=mesh['grp'=2,'shard_0'=4,'shard_1'=4,'shard_2'=4] {'shard_0','shard_1','..., dimensions={0} | all-to-all | bytes 1114112 | tf_op jit(solution)/shard_map/all_to_all | solution.py:500
  161.4 1.4 shard_map.85
  162.8 0.1 collective-permute-start.2
  162.9 13.4 %all_to_all.91 = f32[128,1,128]{2,1,0:T(1,128)S(1)} all-to-all(f32[128,1,128]{2,1,0:T(1,128)S(1)} %bitcast.55), channel_id=1, replica_groups=mesh['grp'=2,'shard_0'=4,'shard_1'=4,'shard_2'=4] {'grp','shard_0','shar..., dimensions={0} | all-to-all | bytes 131072 | tf_op jit(solution)/shard_map/all_to_all | solution.py:604
  176.2 0.0 collective-permute-done.2.theirs
  176.2 0.8 shard_map.86
Async XLA Ops:
  0.6 50.4 %collective-permute-start.1 = (f32[64,128,128]{2,1,0:T(8,128)}, f32[64,128,128]{2,1,0:T(8,128)S(1)}, u32[]{:S(2)}, u32[]{:S(2)}) collective-permute-start(f32[64,128,128]{2,1,0:T(8,128)} %blocks.1), channel_id=1, source_target_pairs={{0,64},{64,0},{1,65},{65,1},{2,66},{66,2},{3,67},{67,3},{4,68},{68... | collective-permute-start | bytes 12582920 | tf_op jit(solution)/shard_map/ppermute | solution.py:504
  0.7 28.6 %copy-start = (f32[2048,8]{0,1:T(8,128)S(1)}, f32[2048,8]{0,1:T(8,128)}, u32[]{:S(2)}) copy-start(f32[2048,8]{0,1:T(8,128)} %param.9) | copy-start | bytes 196612
  30.4 1.3 collective-permute-start
  162.8 13.4 %collective-permute-start.2 = (f32[216,128]{1,0:T(8,128)S(1)}, f32[216,128]{1,0:T(8,128)S(1)}, u32[]{:S(2)}, u32[]{:S(2)}) collective-permute-start(f32[216,128]{1,0:T(8,128)S(1)} %get-tuple-element.105), channel_id=1, source_target_pairs={{0,64},{64,0},{1,65},{65,1},{2,66},{66,2},{3,67},{67,3},{4,68},{68... | collective-permute-start | bytes 331784 | tf_op jit(solution)/shard_map/ppermute | solution.py:504

commit v10 on v9

--- a/solution.py
+++ b/solution.py
@@ -20,7 +20,7 @@
 SLOTS = OWNERS * CAP
 MSG = RHS * CAP + 1
 TALL = OWNERS * MSG
-CHUNK = 8
+CHUNK = 16
 CHUNKS = COUNT // CHUNK
 PART = RHS // 2
 LINES = 2 * ROWS

time: 178 us -> 178 us (level)
  no operation moved by 1% of the time
where the time goes in v10:
time: 178 us; the launch traced here: 177 us
  blocking collectives  158 us (89%)
  Pallas kernels  16.6 us (9%)
    all_to_all x8, blocking collectives, exchange(): return lax.all_to_all(sent, SHARD, 0, 0, tiled=True).reshape(TALL, BS)  145 us
    all_to_all x1, blocking collectives, on_device(): rows = lax.all_to_all(rows, GRP_SHARD, 0, 0, tiled=True)  13.4 us
    pallas_call x2, Pallas kernels, on_device(): call(user_kernel, [SMEM] * 2 + [VMEM] * 11, (msg_shape, left_shape, col8)...  4.95 us
  transfers between devices with their start and end apart: 3, of which 1 were waited for; matrix products, arithmetic and copies ran while one was open for 0% of the time, Pallas kernels for 3%

profile of v10, /device:TPU:0, one launch (start us, length us, event | category | flops | bytes accessed | tf_op | source)
XLA Modules:
  0.0 176.9 jit_solution(5138209418521271691)
XLA Ops:
  0.6 0.1 collective-permute-start.1
  0.7 0.0 copy-start
  0.7 2.8 %shard_map.76 = (f32[1088,128]{1,0:T(8,128)S(1)}, s32[128]{0:T(128)S(4)}, f32[8,128]{1,0:T(8,128)S(1)}, bf16[64,128,128]{2,1,0:T(8,128)(2,1)S(1)}, bf16[64,128,1...) custom-call(s32[64]{0:T(128)} %bitcast.56, s32[64]{0:T(128)} %row_in.1, ...), custom_call_target="tpu_custom_call" | custom-call | tf_op jit(solution)/shard_map/pallas_call | solution.py:531
  3.5 25.8 %all_to_all.83 = f32[64,1,2176]{2,1,0:T(1,128)S(1)} all-to-all(f32[64,1,2176]{2,1,0:T(1,128)S(1)} %bitcast.50), channel_id=1, replica_groups=mesh['grp'=2,'shard_0'=4,'shard_1'=4,'shard_2'=4] {'shard_0','shard_1','..., dimensions={0} | all-to-all | bytes 1114112 | tf_op jit(solution)/shard_map/all_to_all | solution.py:500
  29.3 0.0 copy-done
  29.3 1.0 shard_map.77
  30.3 0.1 collective-permute-start
  30.4 1.3 collective-permute-done.theirs
  31.7 0.8 shard_map.78
  32.5 18.5 %all_to_all.84 = f32[64,1,2176]{2,1,0:T(1,128)S(1)} all-to-all(f32[64,1,2176]{2,1,0:T(1,128)S(1)} %bitcast.48), channel_id=1, replica_groups=mesh['grp'=2,'shard_0'=4,'shard_1'=4,'shard_2'=4] {'shard_0','shard_1','..., dimensions={0} | all-to-all | bytes 1114112 | tf_op jit(solution)/shard_map/all_to_all | solution.py:500
  51.0 0.0 collective-permute-done.1.blocks
  51.0 2.8 %shard_map.79 = (f32[1088,128]{1,0:T(8,128)S(1)}, f32[128,128]{1,0:T(8,128)S(1)}, f32[8,128]{1,0:T(8,128)S(1)}, bf16[64,128,128]{2,1,0:T(8,128)(2,1)S(1)}, bf16[...) custom-call(s32[128]{0:T(128)S(4)} %get-tuple-element.56.tab, ...), custom_call_target="tpu_custom_call" | custom-call | tf_op jit(solution)/shard_map/pallas_call | solution.py:562
  53.8 17.1 %all_to_all.85 = f32[64,1,2176]{2,1,0:T(1,128)S(1)} all-to-all(f32[64,1,2176]{2,1,0:T(1,128)S(1)} %bitcast.46), channel_id=1, replica_groups=mesh['grp'=2,'shard_0'=4,'shard_1'=4,'shard_2'=4] {'shard_0','shard_1','..., dimensions={0} | all-to-all | bytes 1114112 | tf_op jit(solution)/shard_map/all_to_all | solution.py:500
  70.9 0.7 shard_map.80
  71.7 16.7 %all_to_all.86 = f32[64,1,2176]{2,1,0:T(1,128)S(1)} all-to-all(f32[64,1,2176]{2,1,0:T(1,128)S(1)} %bitcast.49), channel_id=1, replica_groups=mesh['grp'=2,'shard_0'=4,'shard_1'=4,'shard_2'=4] {'shard_0','shard_1','..., dimensions={0} | all-to-all | bytes 1114112 | tf_op jit(solution)/shard_map/all_to_all | solution.py:500
  88.3 2.5 %shard_map.81 = (f32[1088,128]{1,0:T(8,128)S(1)}, f32[128,128]{1,0:T(8,128)S(1)}, f32[8,128]{1,0:T(8,128)S(1)}) custom-call(s32[128]{0:T(128)S(4)} %get-tuple-element.56.tab, s32[128]{0:T(128)S(4)} %get-tuple-element.61.tab2, f32[1088,128]{1,0:T(8,128)S(1)} %bitcast.39, f32[128,128]{1,0:T(8,128)S(1)} %get-tuple-element.75.uraw, ...), custom_call_target="tpu_custom_call" | custom-call | tf_op jit(solution)/shard_map/pallas_call | solution.py:570
  90.8 16.7 %all_to_all.87 = f32[64,1,2176]{2,1,0:T(1,128)S(1)} all-to-all(f32[64,1,2176]{2,1,0:T(1,128)S(1)} %bitcast.51), channel_id=1, replica_groups=mesh['grp'=2,'shard_0'=4,'shard_1'=4,'shard_2'=4] {'shard_0','shard_1','..., dimensions={0} | all-to-all | bytes 1114112 | tf_op jit(solution)/shard_map/all_to_all | solution.py:500
  107.5 0.7 shard_map.82
  108.2 16.7 %all_to_all.88 = f32[64,1,2176]{2,1,0:T(1,128)S(1)} all-to-all(f32[64,1,2176]{2,1,0:T(1,128)S(1)} %bitcast.45), channel_id=1, replica_groups=mesh['grp'=2,'shard_0'=4,'shard_1'=4,'shard_2'=4] {'shard_0','shard_1','..., dimensions={0} | all-to-all | bytes 1114112 | tf_op jit(solution)/shard_map/all_to_all | solution.py:500
  124.9 2.5 %shard_map.83 = (f32[1088,128]{1,0:T(8,128)S(1)}, f32[128,128]{1,0:T(8,128)S(1)}, f32[8,128]{1,0:T(8,128)S(1)}) custom-call(s32[128]{0:T(128)S(4)} %get-tuple-element.56.tab, s32[128]{0:T(128)S(4)} %get-tuple-element.61.tab2, f32[1088,128]{1,0:T(8,128)S(1)} %bitcast.38, f32[128,128]{1,0:T(8,128)S(1)} %get-tuple-element.88.uraw, ...), custom_call_target="tpu_custom_call" | custom-call | tf_op jit(solution)/shard_map/pallas_call | solution.py:570
  127.3 16.6 %all_to_all.89 = f32[64,1,2176]{2,1,0:T(1,128)S(1)} all-to-all(f32[64,1,2176]{2,1,0:T(1,128)S(1)} %bitcast.47), channel_id=1, replica_groups=mesh['grp'=2,'shard_0'=4,'shard_1'=4,'shard_2'=4] {'shard_0','shard_1','..., dimensions={0} | all-to-all | bytes 1114112 | tf_op jit(solution)/shard_map/all_to_all | solution.py:500
  144.0 0.7 shard_map.84
  144.7 16.7 %all_to_all.90 = f32[64,1,2176]{2,1,0:T(1,128)S(1)} all-to-all(f32[64,1,2176]{2,1,0:T(1,128)S(1)} %bitcast.44), channel_id=1, replica_groups=mesh['grp'=2,'shard_0'=4,'shard_1'=4,'shard_2'=4] {'shard_0','shard_1','..., dimensions={0} | all-to-all | bytes 1114112 | tf_op jit(solution)/shard_map/all_to_all | solution.py:500
  161.4 1.3 shard_map.85
  162.7 0.1 collective-permute-start.2
  162.8 13.4 %all_to_all.91 = f32[128,1,128]{2,1,0:T(1,128)S(1)} all-to-all(f32[128,1,128]{2,1,0:T(1,128)S(1)} %bitcast.55), channel_id=1, replica_groups=mesh['grp'=2,'shard_0'=4,'shard_1'=4,'shard_2'=4] {'grp','shard_0','shar..., dimensions={0} | all-to-all | bytes 131072 | tf_op jit(solution)/shard_map/all_to_all | solution.py:604
  176.2 0.0 collective-permute-done.2.theirs
  176.2 0.8 shard_map.86
Async XLA Ops:
  0.6 50.4 %collective-permute-start.1 = (f32[64,128,128]{2,1,0:T(8,128)}, f32[64,128,128]{2,1,0:T(8,128)S(1)}, u32[]{:S(2)}, u32[]{:S(2)}) collective-permute-start(f32[64,128,128]{2,1,0:T(8,128)} %blocks.1), channel_id=1, source_target_pairs={{0,64},{64,0},{1,65},{65,1},{2,66},{66,2},{3,67},{67,3},{4,68},{68... | collective-permute-start | bytes 12582920 | tf_op jit(solution)/shard_map/ppermute | solution.py:504
  0.7 28.6 %copy-start = (f32[2048,8]{0,1:T(8,128)S(1)}, f32[2048,8]{0,1:T(8,128)}, u32[]{:S(2)}) copy-start(f32[2048,8]{0,1:T(8,128)} %param.9) | copy-start | bytes 196612
  30.3 1.3 collective-permute-start
  162.7 13.4 %collective-permute-start.2 = (f32[216,128]{1,0:T(8,128)S(1)}, f32[216,128]{1,0:T(8,128)S(1)}, u32[]{:S(2)}, u32[]{:S(2)}) collective-permute-start(f32[216,128]{1,0:T(8,128)S(1)} %get-tuple-element.105), channel_id=1, source_target_pairs={{0,64},{64,0},{1,65},{65,1},{2,66},{66,2},{3,67},{67,3},{4,68},{68... | collective-permute-start | bytes 331784 | tf_op jit(solution)/shard_map/ppermute | solution.py:504

commit v11 on v9

--- a/solution.py
+++ b/solution.py
@@ -361,6 +361,7 @@
 ):
     norm_right = jnp.sqrt(sum_rows(inc, part_column))
     nright[...] = norm_right
+    msg[...] = jnp.zeros((TALL, BS), f32)
     lraw[...] = jnp.zeros(lraw.shape, f32)
     other[...] = jnp.zeros(lraw.shape, f32)
     forward_all(tab, inc, high_t, low_t, (lraw, other))
@@ -376,7 +377,6 @@
         ref = other if k % 2 else lraw
         ref[span, :] = ref[span, :] + part
     left = left_of(lraw, other, uraw, nleft, norm_right)
-    msg[...] = jnp.zeros((TALL, BS), f32)
     put_rows(msg, part_row(part_squares(left)))
     split_left(us, left, PART)
     adjoint_all(tab, us, high, low, msg)
@@ -389,12 +389,12 @@
 ):
     norm_right = jnp.sqrt(sum_rows(inc, part_column))
     nright[...] = norm_right
+    msg[...] = jnp.zeros((TALL, BS), f32)
     lraw[...] = jnp.zeros(lraw.shape, f32)
     other[...] = jnp.zeros(lraw.shape, f32)
     forward_all(tab, inc, high_t, low_t, (lraw, other))
     forward_all(tab2, inc, high2_t, low2_t, (lraw, other))
     left = left_of(lraw, other, uraw, nleft, norm_right)
-    msg[...] = jnp.zeros((TALL, BS), f32)
     put_rows(msg, part_row(part_squares(left)))
     split_left(us, left, PART)
     adjoint_all(tab, us, high, low, msg)

time: 178 us -> 178 us (level)
  no operation moved by 1% of the time
where the time goes in v11:
time: 178 us; the launch traced here: 177 us
  blocking collectives  158 us (89%)
  Pallas kernels  16.7 us (9%)
    all_to_all x8, blocking collectives, exchange(): return lax.all_to_all(sent, SHARD, 0, 0, tiled=True).reshape(TALL, BS)  144 us
    all_to_all x1, blocking collectives, on_device(): rows = lax.all_to_all(rows, GRP_SHARD, 0, 0, tiled=True)  13.4 us
    pallas_call x2, Pallas kernels, on_device(): call(user_kernel, [SMEM] * 2 + [VMEM] * 11, (msg_shape, left_shape, col8)...  4.96 us
  transfers between devices with their start and end apart: 3, of which 1 were waited for; matrix products, arithmetic and copies ran while one was open for 0% of the time, Pallas kernels for 3%

profile of v11, /device:TPU:0, one launch (start us, length us, event | category | flops | bytes accessed | tf_op | source)
XLA Modules:
  0.0 176.7 jit_solution(8043997196759213758)
XLA Ops:
  0.6 0.1 collective-permute-start.1
  0.7 0.0 copy-start
  0.7 2.8 %shard_map.76 = (f32[1088,128]{1,0:T(8,128)S(1)}, s32[128]{0:T(128)S(4)}, f32[8,128]{1,0:T(8,128)S(1)}, bf16[64,128,128]{2,1,0:T(8,128)(2,1)S(1)}, bf16[64,128,1...) custom-call(s32[64]{0:T(128)} %bitcast.56, s32[64]{0:T(128)} %row_in.1, ...), custom_call_target="tpu_custom_call" | custom-call | tf_op jit(solution)/shard_map/pallas_call | solution.py:531
  3.6 25.8 %all_to_all.83 = f32[64,1,2176]{2,1,0:T(1,128)S(1)} all-to-all(f32[64,1,2176]{2,1,0:T(1,128)S(1)} %bitcast.50), channel_id=1, replica_groups=mesh['grp'=2,'shard_0'=4,'shard_1'=4,'shard_2'=4] {'shard_0','shard_1','..., dimensions={0} | all-to-all | bytes 1114112 | tf_op jit(solution)/shard_map/all_to_all | solution.py:500
  29.4 0.0 copy-done
  29.4 1.0 shard_map.77
  30.4 0.1 collective-permute-start
  30.5 1.3 collective-permute-done.theirs
  31.7 0.8 shard_map.78
  32.5 18.5 %all_to_all.84 = f32[64,1,2176]{2,1,0:T(1,128)S(1)} all-to-all(f32[64,1,2176]{2,1,0:T(1,128)S(1)} %bitcast.48), channel_id=1, replica_groups=mesh['grp'=2,'shard_0'=4,'shard_1'=4,'shard_2'=4] {'shard_0','shard_1','..., dimensions={0} | all-to-all | bytes 1114112 | tf_op jit(solution)/shard_map/all_to_all | solution.py:500
  51.0 0.0 collective-permute-done.1.blocks
  51.0 2.8 %shard_map.79 = (f32[1088,128]{1,0:T(8,128)S(1)}, f32[128,128]{1,0:T(8,128)S(1)}, f32[8,128]{1,0:T(8,128)S(1)}, bf16[64,128,128]{2,1,0:T(8,128)(2,1)S(1)}, bf16[...) custom-call(s32[128]{0:T(128)S(4)} %get-tuple-element.56.tab, ...), custom_call_target="tpu_custom_call" | custom-call | tf_op jit(solution)/shard_map/pallas_call | solution.py:562
  53.8 17.1 %all_to_all.85 = f32[64,1,2176]{2,1,0:T(1,128)S(1)} all-to-all(f32[64,1,2176]{2,1,0:T(1,128)S(1)} %bitcast.46), channel_id=1, replica_groups=mesh['grp'=2,'shard_0'=4,'shard_1'=4,'shard_2'=4] {'shard_0','shard_1','..., dimensions={0} | all-to-all | bytes 1114112 | tf_op jit(solution)/shard_map/all_to_all | solution.py:500
  70.9 0.7 shard_map.80
  71.7 16.6 %all_to_all.86 = f32[64,1,2176]{2,1,0:T(1,128)S(1)} all-to-all(f32[64,1,2176]{2,1,0:T(1,128)S(1)} %bitcast.49), channel_id=1, replica_groups=mesh['grp'=2,'shard_0'=4,'shard_1'=4,'shard_2'=4] {'shard_0','shard_1','..., dimensions={0} | all-to-all | bytes 1114112 | tf_op jit(solution)/shard_map/all_to_all | solution.py:500
  88.3 2.5 %shard_map.81 = (f32[1088,128]{1,0:T(8,128)S(1)}, f32[128,128]{1,0:T(8,128)S(1)}, f32[8,128]{1,0:T(8,128)S(1)}) custom-call(s32[128]{0:T(128)S(4)} %get-tuple-element.56.tab, s32[128]{0:T(128)S(4)} %get-tuple-element.61.tab2, f32[1088,128]{1,0:T(8,128)S(1)} %bitcast.39, f32[128,128]{1,0:T(8,128)S(1)} %get-tuple-element.75.uraw, ...), custom_call_target="tpu_custom_call" | custom-call | tf_op jit(solution)/shard_map/pallas_call | solution.py:570
  90.7 16.6 %all_to_all.87 = f32[64,1,2176]{2,1,0:T(1,128)S(1)} all-to-all(f32[64,1,2176]{2,1,0:T(1,128)S(1)} %bitcast.51), channel_id=1, replica_groups=mesh['grp'=2,'shard_0'=4,'shard_1'=4,'shard_2'=4] {'shard_0','shard_1','..., dimensions={0} | all-to-all | bytes 1114112 | tf_op jit(solution)/shard_map/all_to_all | solution.py:500
  107.4 0.7 shard_map.82
  108.1 16.6 %all_to_all.88 = f32[64,1,2176]{2,1,0:T(1,128)S(1)} all-to-all(f32[64,1,2176]{2,1,0:T(1,128)S(1)} %bitcast.45), channel_id=1, replica_groups=mesh['grp'=2,'shard_0'=4,'shard_1'=4,'shard_2'=4] {'shard_0','shard_1','..., dimensions={0} | all-to-all | bytes 1114112 | tf_op jit(solution)/shard_map/all_to_all | solution.py:500
  124.7 2.5 %shard_map.83 = (f32[1088,128]{1,0:T(8,128)S(1)}, f32[128,128]{1,0:T(8,128)S(1)}, f32[8,128]{1,0:T(8,128)S(1)}) custom-call(s32[128]{0:T(128)S(4)} %get-tuple-element.56.tab, s32[128]{0:T(128)S(4)} %get-tuple-element.61.tab2, f32[1088,128]{1,0:T(8,128)S(1)} %bitcast.38, f32[128,128]{1,0:T(8,128)S(1)} %get-tuple-element.88.uraw, ...), custom_call_target="tpu_custom_call" | custom-call | tf_op jit(solution)/shard_map/pallas_call | solution.py:570
  127.2 16.6 %all_to_all.89 = f32[64,1,2176]{2,1,0:T(1,128)S(1)} all-to-all(f32[64,1,2176]{2,1,0:T(1,128)S(1)} %bitcast.47), channel_id=1, replica_groups=mesh['grp'=2,'shard_0'=4,'shard_1'=4,'shard_2'=4] {'shard_0','shard_1','..., dimensions={0} | all-to-all | bytes 1114112 | tf_op jit(solution)/shard_map/all_to_all | solution.py:500
  143.8 0.7 shard_map.84
  144.6 16.6 %all_to_all.90 = f32[64,1,2176]{2,1,0:T(1,128)S(1)} all-to-all(f32[64,1,2176]{2,1,0:T(1,128)S(1)} %bitcast.44), channel_id=1, replica_groups=mesh['grp'=2,'shard_0'=4,'shard_1'=4,'shard_2'=4] {'shard_0','shard_1','..., dimensions={0} | all-to-all | bytes 1114112 | tf_op jit(solution)/shard_map/all_to_all | solution.py:500
  161.1 1.4 shard_map.85
  162.5 0.1 collective-permute-start.2
  162.6 13.4 %all_to_all.91 = f32[128,1,128]{2,1,0:T(1,128)S(1)} all-to-all(f32[128,1,128]{2,1,0:T(1,128)S(1)} %bitcast.55), channel_id=1, replica_groups=mesh['grp'=2,'shard_0'=4,'shard_1'=4,'shard_2'=4] {'grp','shard_0','shar..., dimensions={0} | all-to-all | bytes 131072 | tf_op jit(solution)/shard_map/all_to_all | solution.py:604
  175.9 0.0 collective-permute-done.2.theirs
  175.9 0.8 shard_map.86
Async XLA Ops:
  0.6 50.4 %collective-permute-start.1 = (f32[64,128,128]{2,1,0:T(8,128)}, f32[64,128,128]{2,1,0:T(8,128)S(1)}, u32[]{:S(2)}, u32[]{:S(2)}) collective-permute-start(f32[64,128,128]{2,1,0:T(8,128)} %blocks.1), channel_id=1, source_target_pairs={{0,64},{64,0},{1,65},{65,1},{2,66},{66,2},{3,67},{67,3},{4,68},{68... | collective-permute-start | bytes 12582920 | tf_op jit(solution)/shard_map/ppermute | solution.py:504
  0.7 28.6 %copy-start = (f32[2048,8]{0,1:T(8,128)S(1)}, f32[2048,8]{0,1:T(8,128)}, u32[]{:S(2)}) copy-start(f32[2048,8]{0,1:T(8,128)} %param.9) | copy-start | bytes 196612
  30.4 1.3 collective-permute-start
  162.5 13.4 %collective-permute-start.2 = (f32[216,128]{1,0:T(8,128)S(1)}, f32[216,128]{1,0:T(8,128)S(1)}, u32[]{:S(2)}, u32[]{:S(2)}) collective-permute-start(f32[216,128]{1,0:T(8,128)S(1)} %get-tuple-element.105), channel_id=1, source_target_pairs={{0,64},{64,0},{1,65},{65,1},{2,66},{66,2},{3,67},{67,3},{4,68},{68... | collective-permute-start | bytes 331784 | tf_op jit(solution)/shard_map/ppermute | solution.py:504
